TPU v7x, 32 devices: a whole 2x2x4 slice. The times are simulated.
32 devices in a mesh: tm: 8 (over z, y), space: 4 (over x, core).
Axes of the slice: x: 2, y: 2, z: 4, core: 2. Of those that a mesh axis runs over, the one named last changes fastest.
Arguments:
- amplitude: float32 [80, 96, 512], P('tm', 'space'), may hold values from 0.3 to 3
- phase: float32 [80, 96, 512], P('tm', 'space'), may hold values from -3.140625 to 3.140625
- validity: int32 [96, 512], P('space'), may hold values 0 or 1
- iterations: int32 [8], P('tm'), may hold values from 10 to 20, as said below
- reference_date: int32 [8], P('tm'), may hold values from 0 to 9
Outputs:
- linked: float32 [2, 80, 96, 512], P(None, 'tm', 'space')
Inputs may be any that keep to these rules, and one draw needn't show every extreme that they name: Every ministack takes between 10 and 20 iterations, and some ministack takes exactly 20.
All inputs are finite; a program needn't handle non-finite values. No bound on the sum of `validity` on one device may be relied on, other than what follows from the above.
Results may differ from a plain program's by a relative error of at most 0.0003.
Values sent between devices are 32-bit elements; how exact they have to be, the bound alone decides.
No kernel may reach another device: no remote copies, remote signals or barrier semaphores. Data moves between devices by JAX's collectives and lax.ppermute only.
A program may use at most 64 MiB of HBM per device.

v0:
```python
import math

import jax
import jax.numpy as jnp
from jax import lax
from jax.sharding import PartitionSpec as P

WIN_ROWS = 11
WIN_COLS = 5
ITERS = 20


masked_weight = 0.125
link_floor = 0.03


def extended_2(value, sides, width):
    for axis, dim in sides:
        count, length = (lax.axis_size(axis), value.shape[dim])
        up = [(i, (i + 1) % count) for i in range(count - 1)]
        down = [(j, i) for i, j in up]
        last = lax.slice_in_dim(value, length - width, length, axis=dim)
        leading = lax.slice_in_dim(value, 0, width, axis=dim)
        before = lax.ppermute(last, axis, up)
        after = lax.ppermute(leading, axis, down)
        value = jnp.concatenate([before, value, after], axis=dim)
    return value


def shifted(block, axis, distance):
    devices = range(lax.axis_size(axis))
    route = [(i - distance, i) for i in devices if i - distance in devices]
    return lax.ppermute(block, axis, route)


def box_valid(values):
    out_rows = values.shape[-2] - WIN_ROWS + 1
    row_sums = values[..., 0:out_rows, :]
    for offset in range(1, WIN_ROWS):
        row_sums = row_sums + values[..., offset : offset + out_rows, :]
    out_cols = values.shape[-1] - WIN_COLS + 1
    summed = row_sums[..., 0:out_cols]
    for offset in range(1, WIN_COLS):
        summed = summed + row_sums[..., offset : offset + out_cols]
    return summed


def estimate(window_block, sweep_limit):
    date_count = (window_block.shape[0] - 1) // 2
    amplitudes = window_block[:date_count]
    angles = window_block[date_count : 2 * date_count]
    weights = window_block[2 * date_count]
    real_part = amplitudes * jnp.cos(angles)
    imag_part = amplitudes * jnp.sin(angles)
    cross_real = weights * (
        real_part[:, None] * real_part[None] + imag_part[:, None] * imag_part[None]
    )
    cross_imag = weights * (
        imag_part[:, None] * real_part[None] - real_part[:, None] * imag_part[None]
    )
    power_real = box_valid(cross_real)
    power_imag = box_valid(cross_imag)
    own_power = box_valid(weights * amplitudes * amplitudes)
    inverse = 1.0 / jnp.sqrt(own_power)
    coher_real = power_real * inverse[:, None] * inverse[None]
    coher_imag = power_imag * inverse[:, None] * inverse[None]
    start_real = jnp.full(own_power.shape, 1.0 / math.sqrt(date_count), jnp.float32)
    start_imag = jnp.zeros(own_power.shape, jnp.float32)

    def power_step(turn_no, vectors):
        old_real, old_imag = vectors
        new_real = (
            jnp.sum(coher_real * old_real[None] - coher_imag * old_imag[None], axis=1) + old_real
        )
        new_imag = (
            jnp.sum(coher_real * old_imag[None] + coher_imag * old_real[None], axis=1) + old_imag
        )
        length = jnp.sqrt(jnp.sum(new_real * new_real + new_imag * new_imag, axis=0))
        active = turn_no < sweep_limit
        return (
            jnp.where(active, new_real / length, old_real),
            jnp.where(active, new_imag / length, old_imag),
        )

    vec_real, vec_imag = lax.fori_loop(0, ITERS, power_step, (start_real, start_imag))
    half_rows = WIN_ROWS // 2
    half_cols = WIN_COLS // 2
    inner_real = real_part[
        :, half_rows : real_part.shape[1] - half_rows, half_cols : real_part.shape[2] - half_cols
    ]
    inner_imag = imag_part[
        :, half_rows : imag_part.shape[1] - half_rows, half_cols : imag_part.shape[2] - half_cols
    ]
    comp_real = jnp.sum(vec_real * inner_real + vec_imag * inner_imag, axis=0)
    comp_imag = jnp.sum(vec_real * inner_imag - vec_imag * inner_real, axis=0)
    return (vec_real, vec_imag, comp_real, comp_imag)


def link_phases(stacked, sweep_limit):
    columns = stacked.shape[2]
    half_cols = WIN_COLS // 2
    padded = jnp.pad(stacked, ((0, 0), (0, 0), (half_cols, half_cols)))
    block_cols = min(128, columns)
    blocks = columns // block_cols

    def one_block(block_no):
        window = lax.dynamic_slice_in_dim(
            padded, block_no * block_cols, block_cols + 2 * half_cols, 2
        )
        return estimate(window, sweep_limit)

    results = lax.map(one_block, jnp.arange(blocks, dtype=jnp.int32))

    def merge_cols(pieces):
        placed = jnp.moveaxis(pieces, 0, -2)
        return placed.reshape(placed.shape[:-2] + (columns,))

    return tuple((merge_cols(result) for result in results))


def refer_dates(vec_real, vec_imag, chosen):
    date_count = vec_real.shape[0]
    picked = (jnp.arange(date_count, dtype=jnp.int32) == chosen).astype(jnp.float32)[:, None, None]
    ref_real = jnp.sum(vec_real * picked, axis=0)
    ref_imag = jnp.sum(vec_imag * picked, axis=0)
    linked_real = date_count * (vec_real * ref_real + vec_imag * ref_imag)
    linked_imag = date_count * (vec_imag * ref_real - vec_real * ref_imag)
    return (linked_real, linked_imag)


def pad_columns(values):
    half_cols = WIN_COLS // 2
    return jnp.pad(values, [(0, 0)] * (values.ndim - 1) + [(half_cols, half_cols)])


def link_offsets(comp_real, comp_imag, next_real, next_imag, weights):
    cross_real = box_valid(pad_columns(weights * (comp_real * next_real + comp_imag * next_imag)))
    cross_imag = box_valid(pad_columns(weights * (comp_imag * next_real - comp_real * next_imag)))
    own_power = box_valid(pad_columns(weights * (comp_real * comp_real + comp_imag * comp_imag)))
    next_power = box_valid(pad_columns(weights * (next_real * next_real + next_imag * next_imag)))
    denominator = jnp.sqrt((own_power + 1.0) * (next_power + 1.0))
    off_real = cross_real / denominator
    off_imag = cross_imag / denominator
    magnitude = jnp.sqrt(off_real * off_real + off_imag * off_imag)
    bounded = jnp.maximum(magnitude, link_floor)
    return (off_real / bounded, off_imag / bounded)


def multiply(earlier, later):
    return (
        earlier[0] * later[0] - earlier[1] * later[1],
        earlier[0] * later[1] + earlier[1] * later[0],
    )


def local(amplitude, phase, validity, iterations, reference_date):
    date_count = amplitude.shape[0]
    half_rows = WIN_ROWS // 2
    weights = jnp.where(validity == 1, 1.0, masked_weight).astype(jnp.float32)
    stacked = jnp.concatenate([amplitude, phase, weights[None]], axis=0)
    sweep_limit = iterations[0]
    chosen = reference_date[0]
    extended = extended_2(stacked, (("space", 1),), half_rows)
    vec_real, vec_imag, comp_real, comp_imag = link_phases(extended, sweep_limit)
    image_pair = jnp.stack([comp_real, comp_imag])
    following = shifted(image_pair, "tm", -1)
    image_quad = jnp.concatenate([image_pair, following], axis=0)
    margins = extended_2(image_quad, (("space", 1),), half_rows)
    unit_real, unit_imag = link_offsets(
        margins[0], margins[1], margins[2], margins[3], extended[2 * date_count]
    )
    linked_real, linked_imag = refer_dates(vec_real, vec_imag, chosen)
    everyone = lax.all_gather(jnp.stack([unit_real, unit_imag])[None], "tm", axis=0, tiled=True)
    position = lax.axis_index("tm")

    def absorb(member, vectors):
        product = multiply(vectors, (everyone[member, 0], everyone[member, 1]))
        taken = member < position
        return (jnp.where(taken, product[0], vectors[0]), jnp.where(taken, product[1], vectors[1]))

    datum_real, datum_imag = lax.fori_loop(
        0, lax.axis_size("tm"), absorb, (jnp.ones_like(unit_real), jnp.zeros_like(unit_imag))
    )
    out_real = linked_real * datum_real[None] - linked_imag * datum_imag[None]
    out_imag = linked_real * datum_imag[None] + linked_imag * datum_real[None]
    return jnp.stack([out_real, out_imag])


def solution(mesh):
    return jax.shard_map(
        local,
        mesh=mesh,
        in_specs=(
            P("tm", "space", None),
            P("tm", "space", None),
            P("space", None),
            P("tm"),
            P("tm"),
        ),
        out_specs=P(None, "tm", "space", None),
        check_vma=False,
    )
```

profile of v0, /device:TPU:0, one launch (start us, length us, event | category | flops | bytes accessed | tf_op | source)
XLA Modules:
  0.0 243.2 jit_solution(6755625979817016481)
XLA Ops:
  0.8 1.2 pad_maximum_fusion.4
  2.0 2.4 collective-permute-start
  4.5 1.3 collective-permute-start.1
  7.0 3.0 %collective-permute-done.1 = f32[21,5,512]{2,1,0:T(8,128)S(1)} collective-permute-done((f32[21,5,512]{2,1,0:T(8,128)S(1)}, f32[21,5,512]{2,1,0:T(8,128)S(1)}, u32[]{:S(2)}, u32[]{:S(2)}) %collective-permute-start.1) | collective-permute-done | bytes 215072 | tf_op jit(solution)/shard_map/ppermute | solution.py:25
  10.1 1.4 pad_maximum_fusion
  11.5 1.2 copy-done.2
  12.8 2.0 pad.17
  14.8 175.3 %while.49 = (s32[]{:T(128)}, f32[4,10,24,128]{3,2,1,0:T(8,128)}, f32[4,10,24,128]{3,2,1,0:T(8,128)}, f32[4,24,128]{2,1,0:T(8,128)S(1)}, f32[4,24,128]{2,1,0:T(8,...) while((s32[]{:T(128)}, f32[4,10,24,128]{3,2,1,0:T(8,128)}, ...), condition=%wide.region_8.9_spmd, body=%wide.region_0.8_spmd.sunk | while | flops 17233356 | bytes 60039204 | solution.py:112
  16.0 0.9 dynamic-slice_bitcast_fusion.2
  16.9 2.7 %multiply_multiply_fusion.2 = (f32[10,34,132]{2,1,0:T(8,128)S(1)}, f32[10,34,132]{2,1,0:T(8,128)S(1)}, f32[10,34,132]{2,1,0:T(8,128)S(1)}) fusion(f32[21,34,516]{2,1,0:T(8,128)} %get-tuple-element.627, s32[]{:T(128)S(6)} %select_n.82, f32[34,132]{1,0:T(8,128)S(1)} %dynamic-slice_bitcast_fusion.2, s32[]{:T(128)S(6)} %add.1241), kind=kLoop, calls=%fused_computation.41.clone.1 | loop fusion | flops 179520 | bytes 915560 | tf_op jit(solution)/shard_map/while/body/eval_jaxpr/mul | solution.py:63
  19.6 1.0 subtract_multiply_fusion.2
  20.7 2.4 slice_add_fusion.62
  23.1 3.4 %slice_add_fusion.64 = f32[10,10,24,132]{3,2,1,0:T(8,128)} fusion(f32[10,10,34,132]{3,2,1,0:T(8,128)S(1)} %get-tuple-element.531), kind=kLoop, calls=%fused_computation.19.clone.1 | loop fusion | flops 3168000 | bytes 15206400 | tf_op jit(solution)/shard_map/while/body/eval_jaxpr/add | solution.py:40
  26.9 7.2 %fusion.60 = (f32[10,10,24,128]{3,2,1,0:T(8,128)S(1)}, f32[10,10,24,128]{3,2,1,0:T(8,128)S(1)}) fusion(f32[10,10,24,132]{3,2,1,0:T(8,128)S(1)} %slice_add_fusion.62, f32[10,24,128]{2,1,0:T(8,128)S(1)} %fusion.59, f32[10,10,24,132]{3,2,1,0:T(8,128)} %slice_add_fusion.64), kind=kLoop, calls=%fused_computation.31.clone.1 | loop fusion | flops 3686400 | bytes 14991360 | tf_op jit(solution)/shard_map/while/body/eval_jaxpr/mul | solution.py:66
  34.1 22.5 %while.51 = (s32[]{:T(128)}, f32[10,24,128]{2,1,0:T(8,128)S(1)}, f32[10,24,128]{2,1,0:T(8,128)S(1)}, s32[]{:T(128)}, f32[10,10,24,128]{3,2,1,0:T(8,128)S(1)}, /*...) while((s32[]{:T(128)}, f32[10,24,128]{2,1,0:T(8,128)S(1)}, f32[10,24,128]{2,1,0:T(8,128)S(1)}, ...), condition=%wide.region_5.5_spmd.clone, body=%wide.region_1.4_spmd.clone.sunk | while | flops 2761732 | bytes 4964457 | solution.py:85
  56.7 1.2 subtract_reduce_fusion.3
  59.8 0.9 dynamic-slice_bitcast_fusion.2
  60.8 2.7 %multiply_multiply_fusion.2 = (f32[10,34,132]{2,1,0:T(8,128)S(1)}, f32[10,34,132]{2,1,0:T(8,128)S(1)}, f32[10,34,132]{2,1,0:T(8,128)S(1)}) fusion(f32[21,34,516]{2,1,0:T(8,128)} %get-tuple-element.627, s32[]{:T(128)S(6)} %select_n.82, f32[34,132]{1,0:T(8,128)S(1)} %dynamic-slice_bitcast_fusion.2, s32[]{:T(128)S(6)} %add.1241), kind=kLoop, calls=%fused_computation.41.clone.1 | loop fusion | flops 179520 | bytes 915560 | tf_op jit(solution)/shard_map/while/body/eval_jaxpr/mul | solution.py:63
  63.5 1.0 subtract_multiply_fusion.2
  64.5 2.4 slice_add_fusion.62
  66.9 3.4 %slice_add_fusion.64 = f32[10,10,24,132]{3,2,1,0:T(8,128)} fusion(f32[10,10,34,132]{3,2,1,0:T(8,128)S(1)} %get-tuple-element.531), kind=kLoop, calls=%fused_computation.19.clone.1 | loop fusion | flops 3168000 | bytes 15206400 | tf_op jit(solution)/shard_map/while/body/eval_jaxpr/add | solution.py:40
  70.8 7.2 %fusion.60 = (f32[10,10,24,128]{3,2,1,0:T(8,128)S(1)}, f32[10,10,24,128]{3,2,1,0:T(8,128)S(1)}) fusion(f32[10,10,24,132]{3,2,1,0:T(8,128)S(1)} %slice_add_fusion.62, f32[10,24,128]{2,1,0:T(8,128)S(1)} %fusion.59, f32[10,10,24,132]{3,2,1,0:T(8,128)} %slice_add_fusion.64), kind=kLoop, calls=%fused_computation.31.clone.1 | loop fusion | flops 3686400 | bytes 14991360 | tf_op jit(solution)/shard_map/while/body/eval_jaxpr/mul | solution.py:66
  78.0 22.5 %while.51 = (s32[]{:T(128)}, f32[10,24,128]{2,1,0:T(8,128)S(1)}, f32[10,24,128]{2,1,0:T(8,128)S(1)}, s32[]{:T(128)}, f32[10,10,24,128]{3,2,1,0:T(8,128)S(1)}, /*...) while((s32[]{:T(128)}, f32[10,24,128]{2,1,0:T(8,128)S(1)}, f32[10,24,128]{2,1,0:T(8,128)S(1)}, ...), condition=%wide.region_5.5_spmd.clone, body=%wide.region_1.4_spmd.clone.sunk | while | flops 2761732 | bytes 4964457 | solution.py:85
  100.5 1.2 subtract_reduce_fusion.3
  103.7 0.9 dynamic-slice_bitcast_fusion.2
  104.6 2.7 %multiply_multiply_fusion.2 = (f32[10,34,132]{2,1,0:T(8,128)S(1)}, f32[10,34,132]{2,1,0:T(8,128)S(1)}, f32[10,34,132]{2,1,0:T(8,128)S(1)}) fusion(f32[21,34,516]{2,1,0:T(8,128)} %get-tuple-element.627, s32[]{:T(128)S(6)} %select_n.82, f32[34,132]{1,0:T(8,128)S(1)} %dynamic-slice_bitcast_fusion.2, s32[]{:T(128)S(6)} %add.1241), kind=kLoop, calls=%fused_computation.41.clone.1 | loop fusion | flops 179520 | bytes 915560 | tf_op jit(solution)/shard_map/while/body/eval_jaxpr/mul | solution.py:63
  107.3 1.0 subtract_multiply_fusion.2
  108.4 2.4 slice_add_fusion.62
  110.8 3.4 %slice_add_fusion.64 = f32[10,10,24,132]{3,2,1,0:T(8,128)} fusion(f32[10,10,34,132]{3,2,1,0:T(8,128)S(1)} %get-tuple-element.531), kind=kLoop, calls=%fused_computation.19.clone.1 | loop fusion | flops 3168000 | bytes 15206400 | tf_op jit(solution)/shard_map/while/body/eval_jaxpr/add | solution.py:40
  114.6 7.2 %fusion.60 = (f32[10,10,24,128]{3,2,1,0:T(8,128)S(1)}, f32[10,10,24,128]{3,2,1,0:T(8,128)S(1)}) fusion(f32[10,10,24,132]{3,2,1,0:T(8,128)S(1)} %slice_add_fusion.62, f32[10,24,128]{2,1,0:T(8,128)S(1)} %fusion.59, f32[10,10,24,132]{3,2,1,0:T(8,128)} %slice_add_fusion.64), kind=kLoop, calls=%fused_computation.31.clone.1 | loop fusion | flops 3686400 | bytes 14991360 | tf_op jit(solution)/shard_map/while/body/eval_jaxpr/mul | solution.py:66
  121.8 22.5 %while.51 = (s32[]{:T(128)}, f32[10,24,128]{2,1,0:T(8,128)S(1)}, f32[10,24,128]{2,1,0:T(8,128)S(1)}, s32[]{:T(128)}, f32[10,10,24,128]{3,2,1,0:T(8,128)S(1)}, /*...) while((s32[]{:T(128)}, f32[10,24,128]{2,1,0:T(8,128)S(1)}, f32[10,24,128]{2,1,0:T(8,128)S(1)}, ...), condition=%wide.region_5.5_spmd.clone, body=%wide.region_1.4_spmd.clone.sunk | while | flops 2761732 | bytes 4964457 | solution.py:85
  144.3 1.2 subtract_reduce_fusion.3
  148.4 2.7 %multiply_multiply_fusion.2 = (f32[10,34,132]{2,1,0:T(8,128)S(1)}, f32[10,34,132]{2,1,0:T(8,128)S(1)}, f32[10,34,132]{2,1,0:T(8,128)S(1)}) fusion(f32[21,34,516]{2,1,0:T(8,128)} %get-tuple-element.627, s32[]{:T(128)S(6)} %select_n.82, f32[34,132]{1,0:T(8,128)S(1)} %dynamic-slice_bitcast_fusion.2, s32[]{:T(128)S(6)} %add.1241), kind=kLoop, calls=%fused_computation.41.clone.1 | loop fusion | flops 179520 | bytes 915560 | tf_op jit(solution)/shard_map/while/body/eval_jaxpr/mul | solution.py:63
  151.1 1.0 subtract_multiply_fusion.2
  152.2 2.4 slice_add_fusion.62
  154.6 3.4 %slice_add_fusion.64 = f32[10,10,24,132]{3,2,1,0:T(8,128)} fusion(f32[10,10,34,132]{3,2,1,0:T(8,128)S(1)} %get-tuple-element.531), kind=kLoop, calls=%fused_computation.19.clone.1 | loop fusion | flops 3168000 | bytes 15206400 | tf_op jit(solution)/shard_map/while/body/eval_jaxpr/add | solution.py:40
  158.4 7.2 %fusion.60 = (f32[10,10,24,128]{3,2,1,0:T(8,128)S(1)}, f32[10,10,24,128]{3,2,1,0:T(8,128)S(1)}) fusion(f32[10,10,24,132]{3,2,1,0:T(8,128)S(1)} %slice_add_fusion.62, f32[10,24,128]{2,1,0:T(8,128)S(1)} %fusion.59, f32[10,10,24,132]{3,2,1,0:T(8,128)} %slice_add_fusion.64), kind=kLoop, calls=%fused_computation.31.clone.1 | loop fusion | flops 3686400 | bytes 14991360 | tf_op jit(solution)/shard_map/while/body/eval_jaxpr/mul | solution.py:66
  165.6 22.5 %while.51 = (s32[]{:T(128)}, f32[10,24,128]{2,1,0:T(8,128)S(1)}, f32[10,24,128]{2,1,0:T(8,128)S(1)}, s32[]{:T(128)}, f32[10,10,24,128]{3,2,1,0:T(8,128)S(1)}, /*...) while((s32[]{:T(128)}, f32[10,24,128]{2,1,0:T(8,128)S(1)}, f32[10,24,128]{2,1,0:T(8,128)S(1)}, ...), condition=%wide.region_5.5_spmd.clone, body=%wide.region_1.4_spmd.clone.sunk | while | flops 2761732 | bytes 4964457 | solution.py:85
  188.1 1.2 subtract_reduce_fusion.3
  190.2 1.4 collective-permute-start.2
  191.6 1.3 multiply_reduce_fusion.1
  193.0 3.9 %collective-permute-done.2 = f32[2,24,512]{2,1,0:T(8,128)S(1)} collective-permute-done((f32[2,24,512]{2,1,0:T(8,128)S(1)}, f32[2,24,512]{2,1,0:T(8,128)S(1)}, u32[]{:S(2)}, u32[]{:S(2)}) %collective-permute-start.2) | collective-permute-done | bytes 98336 | tf_op jit(solution)/shard_map/ppermute | solution.py:33
  196.9 6.3 %collective-permute-start.3 = (f32[4,5,512]{2,1,0:T(8,128)S(1)}, f32[4,5,512]{2,1,0:T(8,128)S(1)}, u32[]{:S(2)}, u32[]{:S(2)}) collective-permute-start(f32[4,5,512]{2,1,0:T(8,128)S(1)} %get-tuple-element.375), channel_id=1, source_target_pairs={{0,1},{1,2},{2,3},{4,5},{5,6},{6,7},{8,9},{9,10},{10,11},{12,13},{... | collective-permute-start | bytes 122888 | tf_op jit(solution)/shard_map/ppermute | solution.py:24
  203.2 1.3 collective-permute-start.4
  205.3 1.5 collective-permute-done.4
  206.9 0.9 multiply_bitcast_fusion
  209.0 32.5 %all-gather = f32[16,24,512]{2,1,0:T(8,128)S(1)} all-gather(f32[2,24,512]{2,1,0:T(8,128)S(1)} %pad_maximum_fusion.7), channel_id=2, replica_groups=mesh['tm'=8,'space'=4] {'tm'}, dimensions={0}, use_global_device_ids=true | all-gather | bytes 884736 | tf_op jit(solution)/shard_map/all_gather | solution.py:173
  242.1 1.0 pad_maximum_fusion.1
  (499 shorter events, 47.4 us)
Async XLA Ops:
  2.0 5.0 %collective-permute-start = (f32[21,5,512]{2,1,0:T(8,128)S(1)}, f32[21,5,512]{2,1,0:T(8,128)S(1)}, u32[]{:S(2)}, u32[]{:S(2)}) collective-permute-start(f32[21,5,512]{2,1,0:T(8,128)S(1)} %get-tuple-element.373), channel_id=1, source_target_pairs={{0,1},{1,2},{2,3},{4,5},{5,6},{6,7},{8,9},{9,10},{10,11},{12,13},{... | collective-permute-start | bytes 645128 | tf_op jit(solution)/shard_map/ppermute | solution.py:24
  4.5 5.6 %collective-permute-start.1 = (f32[21,5,512]{2,1,0:T(8,128)S(1)}, f32[21,5,512]{2,1,0:T(8,128)S(1)}, u32[]{:S(2)}, u32[]{:S(2)}) collective-permute-start(f32[21,5,512]{2,1,0:T(8,128)S(1)} %get-tuple-element.374), channel_id=1, source_target_pairs={{1,0},{2,1},{3,2},{5,4},{6,5},{7,6},{9,8},{10,9},{11,10},{13,12},{... | collective-permute-start | bytes 645128 | tf_op jit(solution)/shard_map/ppermute | solution.py:25
  11.5 1.3 copy-start.2
  14.8 176.9 %copy-start.7 = (f32[10]{0:T(128)S(1)}, f32[10]{0:T(128)}, u32[]{:S(2)}) copy-start(f32[10]{0:T(128)} %compare_convert_fusion) | copy-start | bytes 124
  19.6 1.1 copy-start
  19.6 1.1 copy-start.1
  63.5 1.1 copy-start
  63.5 1.1 copy-start.1
  107.3 1.1 copy-start
  107.3 1.1 copy-start.1
  151.1 1.1 copy-start
  151.1 1.1 copy-start.1
  190.1 14.4 %copy-start.3 = (f32[4,10,24,128]{3,2,1,0:T(8,128)S(1)}, f32[4,10,24,128]{3,2,1,0:T(8,128)}, u32[]{:S(2)}) copy-start(f32[4,10,24,128]{3,2,1,0:T(8,128)} %get-tuple-element.255) | copy-start | bytes 1474564
  190.1 14.8 %copy-start.4 = (f32[4,10,24,128]{3,2,1,0:T(8,128)S(1)}, f32[4,10,24,128]{3,2,1,0:T(8,128)}, u32[]{:S(2)}) copy-start(f32[4,10,24,128]{3,2,1,0:T(8,128)} %get-tuple-element.256) | copy-start | bytes 1474564
  190.2 6.6 %collective-permute-start.2 = (f32[2,24,512]{2,1,0:T(8,128)S(1)}, f32[2,24,512]{2,1,0:T(8,128)S(1)}, u32[]{:S(2)}, u32[]{:S(2)}) collective-permute-start(f32[2,24,512]{2,1,0:T(8,128)S(1)} %pad_maximum_fusion.6), channel_id=1, source_target_pairs={{4,0},{8,4},{12,8},{16,12},{20,16},{24,20},{28,24},{5,1},{9,5},{13... | collective-permute-start | bytes 294920 | tf_op jit(solution)/shard_map/ppermute | solution.py:33
  196.9 8.5 %collective-permute-start.3 = (f32[4,5,512]{2,1,0:T(8,128)S(1)}, f32[4,5,512]{2,1,0:T(8,128)S(1)}, u32[]{:S(2)}, u32[]{:S(2)}) collective-permute-start(f32[4,5,512]{2,1,0:T(8,128)S(1)} %get-tuple-element.375), channel_id=1, source_target_pairs={{0,1},{1,2},{2,3},{4,5},{5,6},{6,7},{8,9},{9,10},{10,11},{12,13},{... | collective-permute-start | bytes 122888 | tf_op jit(solution)/shard_map/ppermute | solution.py:24
  203.2 3.6 %collective-permute-start.4 = (f32[4,5,512]{2,1,0:T(8,128)S(1)}, f32[4,5,512]{2,1,0:T(8,128)S(1)}, u32[]{:S(2)}, u32[]{:S(2)}) collective-permute-start(f32[4,5,512]{2,1,0:T(8,128)S(1)} %get-tuple-element.376), channel_id=1, source_target_pairs={{1,0},{2,1},{3,2},{5,4},{6,5},{7,6},{9,8},{10,9},{11,10},{13,12},{... | collective-permute-start | bytes 122888 | tf_op jit(solution)/shard_map/ppermute | solution.py:25
  205.1 36.3 %copy-start.5 = (f32[24,512]{1,0:T(8,128)S(1)}, f32[24,512]{1,0:T(8,128)}, u32[]{:S(2)}) copy-start(f32[24,512]{1,0:T(8,128)} %custom-call.2) | copy-start | bytes 147460
  205.1 36.3 %copy-start.6 = (f32[24,512]{1,0:T(8,128)S(1)}, f32[24,512]{1,0:T(8,128)}, u32[]{:S(2)}) copy-start(f32[24,512]{1,0:T(8,128)} %custom-call.3) | copy-start | bytes 147460
where the time goes:
time: 245 us; the launch traced here: 243 us
  other arithmetic  117 us (48%)
  loops' own time  58.1 us (24%)
  blocking collectives  32.5 us (13%)
  local copies, waits for them, and re-layouts  13.9 us (6%)
  starting transfers between devices  12.7 us (5%)
  waiting for transfers between devices  8.36 us (3%)
    another operation x4, loops' own time, estimate(): lax.fori_loop(0, ITERS, power_step, (start_real, start_imag))  55 us
    all_gather x1, blocking collectives, local(): lax.all_gather(jnp.stack([unit_real, unit_imag])[None], 'tm', axis=0, til...  32.5 us
    mul x4, other arithmetic, estimate(): coher_imag = power_imag * inverse[:, None] * inverse[None]  28.6 us
    reduce_sum x80, other arithmetic, power_step(): jnp.sum(coher_real * old_imag[None] + coher_imag * old_real[None], axis=1)  25.8 us
    add x14, other arithmetic, box_valid(): row_sums = row_sums + values[..., offset:offset + out_rows, :]  25 us
    mul x4, other arithmetic, estimate(): own_power = box_valid(weights * amplitudes * amplitudes)  10.8 us
    ppermute x2, starting transfers between devices, extended_2(): before = lax.ppermute(last, axis, up)  8.7 us
  transfers between devices with their start and end apart: 5, of which 3 were waited for; matrix products, arithmetic and copies ran while one was open for 1% of the time, Pallas kernels for 0%

commit v1 on v0

v1 whole, which is shorter than its diff:
```python
import jax
import jax.numpy as jnp
from jax import lax
from jax.experimental import pallas as pl
from jax.experimental.pallas import tpu as pltpu
from jax.sharding import PartitionSpec as P

WIN_ROWS = 11
WIN_COLS = 5
ITERS = 20
HALF_ROWS = WIN_ROWS // 2

MASKED_WEIGHT = 0.125
LINK_FLOOR = 0.03

LANES = 128
SUB = 8
VMEM_LIMIT = 40 * 1024 * 1024


def vmem():
    return pl.BlockSpec(memory_space=pltpu.VMEM)


def smem():
    return pl.BlockSpec(memory_space=pltpu.SMEM)


def sublane():
    return lax.broadcasted_iota(jnp.int32, (SUB, LANES), 0)


def lane():
    return lax.broadcasted_iota(jnp.int32, (SUB, LANES), 1)


def flip(x):
    return pltpu.roll(x, SUB // 2, 0)


def upper():
    return sublane() < SUB // 2


def bases(k, rows, tiles):
    def base(row):
        return (row // SUB) * SUB * tiles + row % SUB

    return base(k), base(rows - 1 - k)


def load_pair(ref, lead, k, rows, tiles, top):
    first, second = bases(k, rows, tiles)
    a = ref[lead + (pl.ds(first, SUB, stride=SUB), slice(None))]
    b = ref[lead + (pl.ds(second - SUB * tiles, SUB, stride=SUB), slice(None))]
    return jnp.where(top, a, b)


def sin_cos(x):
    turns = jnp.round(x * (2.0 / jnp.pi))
    r = (x - turns * 1.5707855224609375) - turns * 1.0804334124e-05
    s = r * r
    sine = r + r * s * (-1.6666654611e-1 + s * (8.3321608736e-3 + s * -1.9515295891e-4))
    cosine = 1.0 - 0.5 * s + s * s * (
        4.166664568298827e-2 + s * (-1.388731625493765e-3 + s * 2.443315711809948e-5)
    )
    size = jnp.abs(turns)
    odd = size == 1.0
    base_s = jnp.where(odd, cosine, sine)
    base_c = jnp.where(odd, sine, cosine)
    sin_x = jnp.where((turns == -1.0) | (size == 2.0), -base_s, base_s)
    cos_x = jnp.where((turns == 1.0) | (size == 2.0), -base_c, base_c)
    return sin_x, cos_x


def images_kernel(rows, tiles, par_ref, amp_ref, phase_ref, valid_ref, z_ref, x_ref, y_ref):
    half = rows // 2
    top = upper()
    odd = par_ref[0] == 1
    roots = []
    for k in range(half):
        valid = load_pair(valid_ref, (), k, rows, tiles, top)
        roots.append(jnp.where(valid == 1, 1.0, MASKED_WEIGHT**0.5).astype(jnp.float32))

    def one_date(t, carry):
        for k in range(half):
            amp = load_pair(amp_ref, (t,), k, rows, tiles, top) * roots[k]
            sin_x, cos_x = sin_cos(load_pair(phase_ref, (t,), k, rows, tiles, top))
            re, im = amp * cos_x, amp * sin_x
            z_ref[0, t, k] = re
            z_ref[1, t, k] = im
            if k >= half - HALF_ROWS:
                z_ref[0, t, 2 * half - 1 - k] = flip(re)
                z_ref[1, t, 2 * half - 1 - k] = flip(im)
            if k < HALF_ROWS:
                first = jnp.where(top, re, flip(im))
                second = jnp.where(top, flip(re), im)
                x_ref[t, k] = jnp.where(odd, first, second)
                y_ref[t, k] = jnp.where(odd, second, first)
        return carry

    lax.fori_loop(0, z_ref.shape[1], one_date, 0)


def unpack(first, second, top):
    return jnp.where(top, first, flip(second)), jnp.where(top, flip(first), second)


def box_sum(field, lanes, edges):
    count = len(field) - WIN_ROWS + 1
    tail = [None] * WIN_ROWS
    run = field[WIN_ROWS - 1]
    tail[WIN_ROWS - 1] = run
    for k in range(WIN_ROWS - 2, -1, -1):
        run = run + field[k]
        tail[k] = run
    sums = [tail[0]]
    run = None
    for k in range(1, count):
        new = field[WIN_ROWS - 1 + k]
        run = new if run is None else run + new
        sums.append(run if k == WIN_ROWS else tail[k] + run)
    last_two, last_one, first_one, first_two = lanes
    keep_before, keep_after = edges
    out = []
    for x in sums:
        before = jnp.where(keep_before, pltpu.roll(x, 1, 0), 0.0)
        after = jnp.where(keep_after, pltpu.roll(x, SUB - 1, 0), 0.0)
        near = pltpu.roll(jnp.where(last_one, before, x), 1, 1) + pltpu.roll(
            jnp.where(first_one, after, x), LANES - 1, 1
        )
        far = pltpu.roll(jnp.where(last_two, before, x), 2, 1) + pltpu.roll(
            jnp.where(first_two, after, x), LANES - 2, 1
        )
        out.append(x + near + far)
    return out


def masks(tiles):
    at = lane()
    lanes = (at >= LANES - 2, at >= LANES - 1, at < 1, at < 2)
    column = sublane() % tiles
    return lanes, (column != 0, column != tiles - 1)


def add_to(total, sign, value):
    if total is None:
        return value if sign > 0 else -value
    return total + value if sign > 0 else total - value


def phases_kernel(
    tiles, par_ref, iter_ref, chosen_ref, z_ref, x_ref, y_ref,
    link_ref, comp_ref, pack_x_ref, pack_y_ref,
    halo, inv, nr, ni, more, sq, vec,
):
    dates = z_ref.shape[1]
    half = comp_ref.shape[1]
    top = upper()
    odd_device = par_ref[0] == 1
    lanes, edges = masks(tiles)
    pairs = [(i, j) for i in range(dates) for j in range(i + 1, dates)]
    index = {pair: e for e, pair in enumerate(pairs)}
    count = len(pairs)
    ext = half + 2 * HALF_ROWS

    def fill(t, carry):
        for k in range(HALF_ROWS):
            a, b = x_ref[t, k], y_ref[t, k]
            first = jnp.where(odd_device, a, b)
            second = jnp.where(odd_device, b, a)
            re, im = unpack(first, second, top)
            halo[0, t, HALF_ROWS - 1 - k] = re
            halo[1, t, HALF_ROWS - 1 - k] = im
        return carry

    lax.fori_loop(0, dates, fill, 0)

    def image(part, t):
        return [halo[part, t, k] for k in range(HALF_ROWS)] + [
            z_ref[part, t, k] for k in range(ext - HALF_ROWS)
        ]

    def own_power(t, carry):
        re, im = image(0, t), image(1, t)
        power = box_sum([a * a + b * b for a, b in zip(re, im)], lanes, edges)
        for k in range(half):
            inv[t, k] = lax.rsqrt(power[k]) * 0.5
        return carry

    lax.fori_loop(0, dates, own_power, 0)

    starts = {}
    for d in range(1, dates):
        def one_pair(i, carry, d=d):
            j = i + d
            ar, ai, br, bi = image(0, i), image(1, i), image(0, j), image(1, j)
            re = box_sum([ar[k] * br[k] + ai[k] * bi[k] for k in range(ext)], lanes, edges)
            im = box_sum([ai[k] * br[k] - ar[k] * bi[k] for k in range(ext)], lanes, edges)
            at = i * (2 * dates - i - 1) // 2 + (j - i - 1)
            for k in range(half):
                scale = inv[i, k] * inv[j, k]
                nr[at, k] = re[k] * scale
                ni[at, k] = im[k] * scale
            return carry

        lax.fori_loop(0, dates - d, one_pair, 0)

    turns = jnp.minimum(iter_ref[0], ITERS)
    odd_turns = turns % 2 == 1
    steps = jnp.where(odd_turns, turns // 2, turns // 2 - 1)
    groups = []
    at = 0
    for size in (3, 3, 4) if dates == 10 else (dates,):
        groups.append(tuple(range(at, at + size)))
        at += size

    def one_vector(k, carry):
        for e in range(count):
            re, im = nr[e, k], ni[e, k]
            more[e] = re + im
            more[count + e] = im - re

        def left(i, t):
            if i < t:
                e = index[i, t]
                return (nr[e, k], 1), (more[e], 1), (more[count + e], 1)
            e = index[t, i]
            return (nr[e, k], 1), (more[count + e], -1), (more[e], -1)

        def right(t, j):
            if t < j:
                e = index[t, j]
                return (nr[e, k], 1), (ni[e, k], 1), (more[e], 1)
            e = index[j, t]
            return (nr[e, k], 1), (ni[e, k], -1), (more[count + e], -1)

        def square(out):
            sums = {pair: [None, None, None] for pair in out}
            rows_in = sorted({i for i, _ in out})
            cols_in = sorted({j for _, j in out})
            for t in range(dates):
                lefts = {i: left(i, t) for i in rows_in if i != t}
                rights = {j: right(t, j) for j in cols_in if j != t}
                for i, j in out:
                    if t in (i, j):
                        continue
                    (ar, _), (ap, sap), (aq, saq) = lefts[i]
                    (br, _), (bi, sbi), (bs, sbs) = rights[j]
                    s = sums[i, j]
                    s[0] = add_to(s[0], sbs, ar * bs)
                    s[1] = add_to(s[1], saq, aq * br)
                    s[2] = add_to(s[2], sap * sbi, ap * bi)
            for i, j in out:
                e = index[i, j]
                s = sums[i, j]
                re = s[0] - s[2] + nr[e, k]
                im = s[0] + s[1] + ni[e, k]
                sq[e] = re
                sq[count + e] = re + im
                sq[2 * count + e] = im - re

        for a in range(len(groups)):
            square([(i, j) for i in groups[a] for j in groups[a] if i < j])
            for b in range(a + 1, len(groups)):
                square([(i, j) for i in groups[a] for j in groups[b]])
        size = [None] * dates
        for e, (i, j) in enumerate(pairs):
            re, im = nr[e, k], ni[e, k]
            value = re * re + im * im
            size[i] = add_to(size[i], 1, value)
            size[j] = add_to(size[j], 1, value)
        for i in range(dates):
            sq[3 * count + i] = size[i] + 0.25

        def row_sums(re_of, im_of, own):
            sr, si = [own(i) for i in range(dates)], [None] * dates
            for e, (i, j) in enumerate(pairs):
                re, im = re_of(e), im_of(e)
                sr[i] = sr[i] + re
                sr[j] = sr[j] + re
                si[i] = add_to(si[i], 1, im)
                si[j] = add_to(si[j], -1, im)
            for i in range(dates):
                vec[i] = sr[i]
                vec[dates + i] = si[i]

        @pl.when(odd_turns)
        def _():
            row_sums(lambda e: nr[e, k], lambda e: ni[e, k],
                     lambda i: jnp.full((SUB, LANES), 0.5, jnp.float32))

        @pl.when(jnp.logical_not(odd_turns))
        def _():
            row_sums(lambda e: sq[e], lambda e: sq[count + e] - sq[e],
                     lambda i: sq[3 * count + i])

        def step(_, vectors):
            vr, vi = vectors[:dates], vectors[dates:]
            vs = [a + b for a, b in zip(vr, vi)]
            out_r, out_i = [], []
            for rows_in in groups:
                sums = {i: [None, None, None] for i in rows_in}
                for i in rows_in:
                    for j in range(dates):
                        if j == i or (j in rows_in and j < i):
                            continue
                        e = index[min(i, j), max(i, j)]
                        re, plus, minus = sq[e], sq[count + e], sq[2 * count + e]
                        s = sums[i]
                        if i < j:
                            s[0] = add_to(s[0], 1, re * vs[j])
                            s[1] = add_to(s[1], 1, minus * vr[j])
                            s[2] = add_to(s[2], 1, plus * vi[j])
                            if j in rows_in:
                                s = sums[j]
                                s[0] = add_to(s[0], 1, re * vs[i])
                                s[1] = add_to(s[1], -1, plus * vr[i])
                                s[2] = add_to(s[2], -1, minus * vi[i])
                        else:
                            s[0] = add_to(s[0], 1, re * vs[j])
                            s[1] = add_to(s[1], -1, plus * vr[j])
                            s[2] = add_to(s[2], -1, minus * vi[j])
                for i in rows_in:
                    own = sq[3 * count + i]
                    s = sums[i]
                    out_r.append(s[0] - s[2] + own * vr[i])
                    out_i.append(s[0] + s[1] + own * vi[i])
            return tuple(out_r + out_i)

        vectors = lax.fori_loop(0, steps, step, tuple(vec[i] for i in range(2 * dates)))
        length = None
        for part in vectors:
            length = add_to(length, 1, part * part)
        scale = lax.rsqrt(length)
        vr = [a * scale for a in vectors[:dates]]
        vi = [a * scale for a in vectors[dates:]]
        for i in range(dates):
            vec[i] = vr[i]
            vec[dates + i] = vi[i]
        cr = ci = None
        for i in range(dates):
            zr, zi = z_ref[0, i, k], z_ref[1, i, k]
            cr = add_to(cr, 1, vr[i] * zr + vi[i] * zi)
            ci = add_to(ci, 1, vr[i] * zi - vi[i] * zr)
        comp_ref[0, k] = cr
        comp_ref[1, k] = ci
        ref_r = vec[chosen_ref[0]] * float(dates)
        ref_i = vec[dates + chosen_ref[0]] * float(dates)
        for i in range(dates):
            link_ref[0, i, k] = vr[i] * ref_r + vi[i] * ref_i
            link_ref[1, i, k] = vi[i] * ref_r - vr[i] * ref_i
        return carry

    lax.fori_loop(0, half, one_vector, 0)
    for k in range(HALF_ROWS):
        re, im = comp_ref[0, k], comp_ref[1, k]
        first = jnp.where(top, re, flip(im))
        second = jnp.where(top, flip(re), im)
        pack_x_ref[k] = jnp.where(odd_device, first, second)
        pack_y_ref[k] = jnp.where(odd_device, second, first)


def extend_kernel(par_ref, comp_ref, x_ref, y_ref, out_ref):
    top = upper()
    odd_device = par_ref[0] == 1
    for k in range(HALF_ROWS):
        a, b = x_ref[k], y_ref[k]
        re, im = unpack(jnp.where(odd_device, a, b), jnp.where(odd_device, b, a), top)
        out_ref[0, HALF_ROWS - 1 - k] = re
        out_ref[1, HALF_ROWS - 1 - k] = im
    for part in range(2):
        for k in range(comp_ref.shape[1]):
            out_ref[part, HALF_ROWS + k] = comp_ref[part, k]


def offsets_kernel(tiles, place_ref, own_ref, a_ref, b_ref, unit_ref, total_ref):
    lanes, edges = masks(tiles)
    half = unit_ref.shape[1]
    odd_stack = place_ref[1] == 1
    first_stack = place_ref[0] == 0

    def whole(ref):
        parts = []
        for part in range(2):
            rows_in = [ref[part, k] for k in range(ref.shape[1])]
            rows_in += [flip(rows_in[-1 - k]) for k in range(HALF_ROWS)]
            parts.append(rows_in)
        return parts

    def power(re, im):
        return box_sum([a * a + b * b for a, b in zip(re, im)], lanes, edges)

    own_r, own_i = whole(own_ref)
    own = [p + 1.0 for p in power(own_r, own_i)]

    def unit(ref):
        re, im = whole(ref)
        other = power(re, im)
        cross_r = box_sum(
            [a * c + b * d for a, b, c, d in zip(own_r, own_i, re, im)], lanes, edges
        )
        cross_i = box_sum(
            [b * c - a * d for a, b, c, d in zip(own_r, own_i, re, im)], lanes, edges
        )
        out = []
        for k in range(half):
            scale = lax.rsqrt(own[k] * (other[k] + 1.0))
            off_r, off_i = cross_r[k] * scale, cross_i[k] * scale
            bound = jnp.maximum(jnp.sqrt(off_r * off_r + off_i * off_i), LINK_FLOOR)
            back = 1.0 / bound
            out.append((off_r * back, off_i * back))
        return out

    pair_a, pair_b = unit(a_ref), unit(b_ref)
    for k in range(half):
        (ar, ai), (br, bi) = pair_a[k], pair_b[k]
        before_r = jnp.where(odd_stack, ar, br)
        before_i = -jnp.where(odd_stack, ai, bi)
        after_r = jnp.where(odd_stack, br, ar)
        after_i = jnp.where(odd_stack, bi, ai)
        before_r = jnp.where(first_stack, 1.0, before_r)
        before_i = jnp.where(first_stack, 0.0, before_i)
        unit_ref[0, k] = before_r
        unit_ref[1, k] = before_i
        total_ref[0, k] = before_r * after_r - before_i * after_i
        total_ref[1, k] = before_r * after_i + before_i * after_r


def result_kernel(rows, tiles, link_ref, datum_ref, out_ref):
    half = rows // 2

    def one_date(t, carry):
        for k in range(half):
            lr, li = link_ref[0, t, k], link_ref[1, t, k]
            dr, di = datum_ref[0, k], datum_ref[1, k]
            first, second = bases(k, rows, tiles)
            for part, value in enumerate((lr * dr - li * di, lr * di + li * dr)):
                out_ref[part, t, pl.ds(first, tiles, stride=SUB), :] = value[:tiles]
                out_ref[part, t, pl.ds(second, tiles, stride=SUB), :] = value[tiles:]
        return carry

    lax.fori_loop(0, link_ref.shape[1], one_date, 0)


def swaps(count, bit=None, odd=False):
    if bit is not None:
        return [(i, i ^ bit) for i in range(count) if (i ^ bit) < count]
    first = 1 if odd else 0
    pairs = [(i, i + 1) for i in range(first, count - 1, 2)]
    return pairs + [(j, i) for i, j in pairs]


def times(a, b):
    return jnp.stack([a[0] * b[0] - a[1] * b[1], a[0] * b[1] + a[1] * b[0]])


def local(amplitude, phase, validity, iterations, reference_date):
    dates, rows, columns = amplitude.shape
    half = rows // 2
    tiles = columns // LANES
    ext = half + HALF_ROWS
    members = lax.axis_size("tm")
    blocks = lax.axis_size("space")
    place = lax.axis_index("tm")
    parity = (lax.axis_index("space") % 2).reshape(1)
    params = pltpu.CompilerParams(vmem_limit_bytes=VMEM_LIMIT)

    def shape(*dims):
        return jax.ShapeDtypeStruct(dims, jnp.float32)

    def tiled(x):
        lead = x.shape[:-2]
        x = x.reshape(lead + (rows // SUB, SUB, tiles, LANES))
        return jnp.swapaxes(x, -3, -2).reshape(lead + (rows * tiles, LANES))

    z, slab_x, slab_y = pl.pallas_call(
        lambda *refs: images_kernel(rows, tiles, *refs),
        out_shape=(
            shape(2, dates, ext, SUB, LANES),
            shape(dates, HALF_ROWS, SUB, LANES),
            shape(dates, HALF_ROWS, SUB, LANES),
        ),
        in_specs=[smem(), vmem(), vmem(), vmem()],
        out_specs=(vmem(), vmem(), vmem()),
        compiler_params=params,
        name="images",
    )(parity, tiled(amplitude), tiled(phase), tiled(validity))
    pair_x, pair_y = swaps(blocks), swaps(blocks, odd=True)
    got_y = lax.ppermute(slab_y, "space", pair_y)
    got_x = lax.ppermute(slab_x, "space", pair_x)

    count = dates * (dates - 1) // 2
    linked, comp, pack_x, pack_y = pl.pallas_call(
        lambda *refs: phases_kernel(tiles, *refs),
        out_shape=(
            shape(2, dates, half, SUB, LANES),
            shape(2, half, SUB, LANES),
            shape(HALF_ROWS, SUB, LANES),
            shape(HALF_ROWS, SUB, LANES),
        ),
        in_specs=[smem(), smem(), smem(), vmem(), vmem(), vmem()],
        out_specs=(vmem(), vmem(), vmem(), vmem()),
        scratch_shapes=[
            pltpu.VMEM((2, dates, HALF_ROWS, SUB, LANES), jnp.float32),
            pltpu.VMEM((dates, half, SUB, LANES), jnp.float32),
            pltpu.VMEM((count, half, SUB, LANES), jnp.float32),
            pltpu.VMEM((count, half, SUB, LANES), jnp.float32),
            pltpu.VMEM((2 * count, SUB, LANES), jnp.float32),
            pltpu.VMEM((3 * count + dates, SUB, LANES), jnp.float32),
            pltpu.VMEM((2 * dates, SUB, LANES), jnp.float32),
        ],
        compiler_params=params,
        name="phases",
    )(parity, iterations, reference_date, z, got_x, got_y)

    more_y = lax.ppermute(pack_y, "space", pair_y)
    more_x = lax.ppermute(pack_x, "space", pair_x)
    wide = pl.pallas_call(
        extend_kernel,
        out_shape=shape(2, ext, SUB, LANES),
        in_specs=[smem(), vmem(), vmem(), vmem()],
        out_specs=vmem(),
        compiler_params=params,
        name="extend",
    )(parity, comp, more_x, more_y)
    other_a = lax.ppermute(wide, "tm", swaps(members))
    other_b = lax.ppermute(wide, "tm", swaps(members, odd=True))
    where = jnp.stack([place, place % 2]).astype(jnp.int32)
    datum, total = pl.pallas_call(
        lambda *refs: offsets_kernel(tiles, *refs),
        out_shape=(shape(2, half, SUB, LANES), shape(2, half, SUB, LANES)),
        in_specs=[smem(), vmem(), vmem(), vmem()],
        out_specs=(vmem(), vmem()),
        compiler_params=params,
        name="offsets",
    )(where, wide, other_a, other_b)
    bit = 2
    while bit < members:
        other = lax.ppermute(total, "tm", swaps(members, bit=bit))
        datum = jnp.where((place & bit) != 0, times(datum, other), datum)
        total = times(total, other)
        bit *= 2
    out = pl.pallas_call(
        lambda *refs: result_kernel(rows, tiles, *refs),
        out_shape=shape(2, dates, rows * tiles, LANES),
        in_specs=[vmem(), vmem()],
        out_specs=vmem(),
        compiler_params=params,
        name="result",
    )(linked, datum)
    out = out.reshape(2, dates, rows // SUB, tiles, SUB, LANES)
    return jnp.swapaxes(out, -3, -2).reshape(2, dates, rows, columns)


def solution(mesh):
    return jax.shard_map(
        local,
        mesh=mesh,
        in_specs=(
            P("tm", "space", None),
            P("tm", "space", None),
            P("space", None),
            P("tm"),
            P("tm"),
        ),
        out_specs=P(None, "tm", "space", None),
        check_vma=False,
    )
```

time: 245 us -> 64.6 us (0.26)
  the two profiles are of different devices: /device:TPU:0 before, /device:TPU:10 now
where the time goes in v1:
time: 64.6 us; the launch traced here: 64.5 us
  Pallas kernels  28.5 us (44%)
  waiting for transfers between devices  22.2 us (34%)
  starting transfers between devices  9.34 us (14%)
  local copies, waits for them, and re-layouts  2.86 us (4%)
  between operations  1.44 us (2%)
    pallas_call x1, Pallas kernels, local(): pl.pallas_call(lambda *refs: phases_kernel(tiles, *refs), out_shape=(shap...  25.5 us
    ppermute x2, waiting for transfers between devices, local(): other = lax.ppermute(total, 'tm', swaps(members, bit=bit))  10.1 us
    ppermute x1, waiting for transfers between devices, local(): other_b = lax.ppermute(wide, 'tm', swaps(members, odd=True))  4.4 us
    ppermute x1, waiting for transfers between devices, local(): got_y = lax.ppermute(slab_y, 'space', pair_y)  3.23 us
    unnamed x6, local copies, waits for them, and re-layouts  2.86 us
    ppermute x1, waiting for transfers between devices, local(): more_y = lax.ppermute(pack_y, 'space', pair_y)  2.55 us
    ppermute x1, starting transfers between devices, local(): got_y = lax.ppermute(slab_y, 'space', pair_y)  2.53 us
    ppermute x1, starting transfers between devices, local(): more_y = lax.ppermute(pack_y, 'space', pair_y)  2.53 us
  transfers between devices with their start and end apart: 8, of which 6 were waited for; matrix products, arithmetic and copies ran while one was open for 0% of the time, Pallas kernels for 0%

profile of v1, /device:TPU:10, one launch (start us, length us, event | category | flops | bytes accessed | tf_op | source)
XLA Modules:
  0.0 64.5 jit_solution(12568131829670047622)
XLA Ops:
  0.0 0.0 copy-start
  0.0 1.0 %copy-done = f32[10,24,512]{2,1,0:T(8,128)S(1)} copy-done((f32[10,24,512]{2,1,0:T(8,128)S(1)}, f32[10,24,512]{2,1,0:T(8,128)}, u32[]{:S(2)}) %copy-start) | copy-done | bytes 491544
  1.0 0.0 copy-start.1
  1.0 1.0 %copy-done.1 = f32[10,24,512]{2,1,0:T(8,128)S(1)} copy-done((f32[10,24,512]{2,1,0:T(8,128)S(1)}, f32[10,24,512]{2,1,0:T(8,128)}, u32[]{:S(2)}) %copy-start.1) | copy-done | bytes 491544
  2.1 0.0 copy-start.2
  2.1 0.8 %copy-done.2 = s32[24,512]{1,0:T(8,128)S(1)} copy-done((s32[24,512]{1,0:T(8,128)S(1)}, s32[24,512]{1,0:T(8,128)}, u32[]{:S(2)}) %copy-start.2) | copy-done | bytes 49176
  2.9 0.8 %images.1 = (f32[2,10,17,8,128]{4,3,2,1,0:T(8,128)S(1)}, f32[10,5,8,128]{3,2,1,0:T(8,128)S(1)}, f32[10,5,8,128]{3,2,1,0:T(8,128)S(1)}) custom-call(s32[1]{0:T(128)} %bitcast.refs_0_.par_ref, f32[10,96,128]{2,1,0:T(8,128)S(1)} %bitcast.23, f32[10,96,128]{2,1,0:T(8,128)S(1)} %bitcast.24, s32[96,128]{1,0:T(8,128)S(1)} %bitcast.25), custom_call_target="tpu_custom_call" | custom-call | tf_op jit(solution)/shard_map/images/pallas_call | solution.py:477
  3.7 0.1 collective-permute-start
  3.8 2.5 %collective-permute-start.1 = (f32[10,5,8,128]{3,2,1,0:T(8,128)S(1)}, f32[10,5,8,128]{3,2,1,0:T(8,128)S(1)}, u32[]{:S(2)}, u32[]{:S(2)}) collective-permute-start(f32[10,5,8,128]{3,2,1,0:T(8,128)S(1)} %get-tuple-element.16), channel_id=1, source_target_pairs={{1,2},{2,1},{5,6},{6,5},{9,10},{10,9},{13,14},{14,13},{17,18},{18,... | collective-permute-start | bytes 614408 | tf_op jit(solution)/shard_map/ppermute | solution.py:490
  7.6 0.0 collective-permute-done.refs_4_
  7.6 3.2 %collective-permute-done.1.refs_5_ = f32[10,5,8,128]{3,2,1,0:T(8,128)S(1)} collective-permute-done((f32[10,5,8,128]{3,2,1,0:T(8,128)S(1)}, f32[10,5,8,128]{3,2,1,0:T(8,128)S(1)}, u32[]{:S(2)}, u32[]{:S(2)}) %collective-permute-start.1) | collective-permute-done | bytes 204832 | tf_op jit(solution)/shard_map/ppermute | solution.py:490
  10.9 25.5 %phases.1 = (f32[2,10,12,8,128]{4,3,2,1,0:T(8,128)S(1)}, f32[2,12,8,128]{3,2,1,0:T(8,128)S(1)}, f32[5,8,128]{2,1,0:T(8,128)S(1)}, f32[5,8,128]{2,1,0:T(8,128)S(1)}) custom-call(s32[1]{0:T(128)} %bitcast.refs_0_.par_ref, s32[1]{0:T(128)S(6)} %copy.6.refs_1_, s32[1]{0:T(128)S(6)} %copy.7.refs_2_, f32[2,10,17,8,128]{4,3,2,1,0:T(8,128)S(1)} %get-tuple-element.14.refs_3_, ...), custom_call_target="tpu_custom_call" | custom-call | tf_op jit(solution)/shard_map/phases/pallas_call | solution.py:494
  36.4 0.1 collective-permute-start.2
  36.4 2.5 %collective-permute-start.3 = (f32[5,8,128]{2,1,0:T(8,128)S(1)}, f32[5,8,128]{2,1,0:T(8,128)S(1)}, u32[]{:S(2)}, u32[]{:S(2)}) collective-permute-start(f32[5,8,128]{2,1,0:T(8,128)S(1)} %get-tuple-element.20), channel_id=1, source_target_pairs={{1,2},{2,1},{5,6},{6,5},{9,10},{10,9},{13,14},{14,13},{17,18},{18,... | collective-permute-start | bytes 61448 | tf_op jit(solution)/shard_map/ppermute | solution.py:517
  39.0 0.0 collective-permute-done.2.x_ref
  39.0 2.6 %collective-permute-done.3.y_ref = f32[5,8,128]{2,1,0:T(8,128)S(1)} collective-permute-done((f32[5,8,128]{2,1,0:T(8,128)S(1)}, f32[5,8,128]{2,1,0:T(8,128)S(1)}, u32[]{:S(2)}, u32[]{:S(2)}) %collective-permute-start.3) | collective-permute-done | bytes 20512 | tf_op jit(solution)/shard_map/ppermute | solution.py:517
  41.6 1.7 %collective-permute-start.4 = (f32[2,17,8,128]{3,2,1,0:T(8,128)S(1)}, f32[2,17,8,128]{3,2,1,0:T(8,128)S(1)}, u32[]{:S(2)}, u32[]{:S(2)}) collective-permute-start(f32[2,17,8,128]{3,2,1,0:T(8,128)S(1)} %extend.1.refs_1_), channel_id=1, source_target_pairs={{0,4},{8,12},{16,20},{24,28},{4,0},{12,8},{20,16},{28,24},{1,5},{9... | collective-permute-start | bytes 417800 | tf_op jit(solution)/shard_map/ppermute | solution.py:527
  43.2 2.3 %collective-permute-start.5 = (f32[2,17,8,128]{3,2,1,0:T(8,128)S(1)}, f32[2,17,8,128]{3,2,1,0:T(8,128)S(1)}, u32[]{:S(2)}, u32[]{:S(2)}) collective-permute-start(f32[2,17,8,128]{3,2,1,0:T(8,128)S(1)} %extend.1.refs_1_), channel_id=1, source_target_pairs={{4,8},{12,16},{20,24},{8,4},{16,12},{24,20},{5,9},{13,17},{21,25},... | collective-permute-start | bytes 417800 | tf_op jit(solution)/shard_map/ppermute | solution.py:528
  45.6 0.1 pad_add_fusion.refs_0_
  45.6 1.9 %collective-permute-done.4.refs_2_ = f32[2,17,8,128]{3,2,1,0:T(8,128)S(1)} collective-permute-done((f32[2,17,8,128]{3,2,1,0:T(8,128)S(1)}, f32[2,17,8,128]{3,2,1,0:T(8,128)S(1)}, u32[]{:S(2)}, u32[]{:S(2)}) %collective-permute-start.4) | collective-permute-done | bytes 139296 | tf_op jit(solution)/shard_map/ppermute | solution.py:527
  47.6 4.4 %collective-permute-done.5.refs_3_ = f32[2,17,8,128]{3,2,1,0:T(8,128)S(1)} collective-permute-done((f32[2,17,8,128]{3,2,1,0:T(8,128)S(1)}, f32[2,17,8,128]{3,2,1,0:T(8,128)S(1)}, u32[]{:S(2)}, u32[]{:S(2)}) %collective-permute-start.5) | collective-permute-done | bytes 139296 | tf_op jit(solution)/shard_map/ppermute | solution.py:528
  52.0 1.0 %offsets.1 = (f32[2,12,8,128]{3,2,1,0:T(8,128)S(1)}, f32[2,12,8,128]{3,2,1,0:T(8,128)S(1)}) custom-call(s32[2]{0:T(128)S(1)} %pad_add_fusion.refs_0_, f32[2,17,8,128]{3,2,1,0:T(8,128)S(1)} %extend.1.refs_1_, f32[2,17,8,128]{3,2,1,0:T(8,128)S(1)} %collective-permute-done.4.refs_2_, f32[2,17,8,128]{3,2,1,0:T(8,128)S(1)} %collective-permute-done.5.refs_3_), custom_call_target="tpu_custom_call" | custom-call | tf_op jit(solution)/shard_map/offsets/pallas_call | solution.py:530
  53.0 0.1 collective-permute-start.6
  53.1 4.6 %collective-permute-done.6 = f32[2,12,8,128]{3,2,1,0:T(8,128)S(1)} collective-permute-done((f32[2,12,8,128]{3,2,1,0:T(8,128)S(1)}, f32[2,12,8,128]{3,2,1,0:T(8,128)S(1)}, u32[]{:S(2)}, u32[]{:S(2)}) %collective-permute-start.6) | collective-permute-done | bytes 98336 | tf_op jit(solution)/shard_map/ppermute | solution.py:540
  57.7 0.1 collective-permute-start.7
  57.8 5.5 %collective-permute-done.7 = f32[2,12,8,128]{3,2,1,0:T(8,128)S(1)} collective-permute-done((f32[2,12,8,128]{3,2,1,0:T(8,128)S(1)}, f32[2,12,8,128]{3,2,1,0:T(8,128)S(1)}, u32[]{:S(2)}, u32[]{:S(2)}) %collective-permute-start.7) | collective-permute-done | bytes 98336 | tf_op jit(solution)/shard_map/ppermute | solution.py:540
  63.3 1.2 %result.1 = f32[2,10,96,128]{3,2,1,0:T(8,128)} custom-call(f32[2,10,12,8,128]{4,3,2,1,0:T(8,128)S(1)} %get-tuple-element.17.refs_0_, f32[2,12,8,128]{3,2,1,0:T(8,128)S(1)} %maximum_select_fusion.1.refs_1_), custom_call_target="tpu_custom_call" | custom-call | tf_op jit(solution)/shard_map/result/pallas_call | solution.py:544
  (6 shorter events, 0.1 us)
Async XLA Ops:
  0.0 1.0 %copy-start = (f32[10,24,512]{2,1,0:T(8,128)S(1)}, f32[10,24,512]{2,1,0:T(8,128)}, u32[]{:S(2)}) copy-start(f32[10,24,512]{2,1,0:T(8,128)} %param.5) | copy-start | bytes 1474564
  1.0 1.0 %copy-start.1 = (f32[10,24,512]{2,1,0:T(8,128)S(1)}, f32[10,24,512]{2,1,0:T(8,128)}, u32[]{:S(2)}) copy-start(f32[10,24,512]{2,1,0:T(8,128)} %param.6) | copy-start | bytes 1474564
  2.1 0.8 %copy-start.2 = (s32[24,512]{1,0:T(8,128)S(1)}, s32[24,512]{1,0:T(8,128)}, u32[]{:S(2)}) copy-start(s32[24,512]{1,0:T(8,128)} %param.7) | copy-start | bytes 147460
  3.7 3.9 %collective-permute-start = (f32[10,5,8,128]{3,2,1,0:T(8,128)S(1)}, f32[10,5,8,128]{3,2,1,0:T(8,128)S(1)}, u32[]{:S(2)}, u32[]{:S(2)}) collective-permute-start(f32[10,5,8,128]{3,2,1,0:T(8,128)S(1)} %get-tuple-element.15), channel_id=1, source_target_pairs={{0,1},{2,3},{1,0},{3,2},{4,5},{6,7},{5,4},{7,6},{8,9},{10,11},{9,8... | collective-permute-start | bytes 614408 | tf_op jit(solution)/shard_map/ppermute | solution.py:491
  3.8 7.1 %collective-permute-start.1 = (f32[10,5,8,128]{3,2,1,0:T(8,128)S(1)}, f32[10,5,8,128]{3,2,1,0:T(8,128)S(1)}, u32[]{:S(2)}, u32[]{:S(2)}) collective-permute-start(f32[10,5,8,128]{3,2,1,0:T(8,128)S(1)} %get-tuple-element.16), channel_id=1, source_target_pairs={{1,2},{2,1},{5,6},{6,5},{9,10},{10,9},{13,14},{14,13},{17,18},{18,... | collective-permute-start | bytes 614408 | tf_op jit(solution)/shard_map/ppermute | solution.py:490
  36.4 2.6 %collective-permute-start.2 = (f32[5,8,128]{2,1,0:T(8,128)S(1)}, f32[5,8,128]{2,1,0:T(8,128)S(1)}, u32[]{:S(2)}, u32[]{:S(2)}) collective-permute-start(f32[5,8,128]{2,1,0:T(8,128)S(1)} %get-tuple-element.19), channel_id=1, source_target_pairs={{0,1},{2,3},{1,0},{3,2},{4,5},{6,7},{5,4},{7,6},{8,9},{10,11},{9,8... | collective-permute-start | bytes 61448 | tf_op jit(solution)/shard_map/ppermute | solution.py:518
  36.4 5.1 %collective-permute-start.3 = (f32[5,8,128]{2,1,0:T(8,128)S(1)}, f32[5,8,128]{2,1,0:T(8,128)S(1)}, u32[]{:S(2)}, u32[]{:S(2)}) collective-permute-start(f32[5,8,128]{2,1,0:T(8,128)S(1)} %get-tuple-element.20), channel_id=1, source_target_pairs={{1,2},{2,1},{5,6},{6,5},{9,10},{10,9},{13,14},{14,13},{17,18},{18,... | collective-permute-start | bytes 61448 | tf_op jit(solution)/shard_map/ppermute | solution.py:517
  41.6 6.0 %collective-permute-start.4 = (f32[2,17,8,128]{3,2,1,0:T(8,128)S(1)}, f32[2,17,8,128]{3,2,1,0:T(8,128)S(1)}, u32[]{:S(2)}, u32[]{:S(2)}) collective-permute-start(f32[2,17,8,128]{3,2,1,0:T(8,128)S(1)} %extend.1.refs_1_), channel_id=1, source_target_pairs={{0,4},{8,12},{16,20},{24,28},{4,0},{12,8},{20,16},{28,24},{1,5},{9... | collective-permute-start | bytes 417800 | tf_op jit(solution)/shard_map/ppermute | solution.py:527
  43.2 8.7 %collective-permute-start.5 = (f32[2,17,8,128]{3,2,1,0:T(8,128)S(1)}, f32[2,17,8,128]{3,2,1,0:T(8,128)S(1)}, u32[]{:S(2)}, u32[]{:S(2)}) collective-permute-start(f32[2,17,8,128]{3,2,1,0:T(8,128)S(1)} %extend.1.refs_1_), channel_id=1, source_target_pairs={{4,8},{12,16},{20,24},{8,4},{16,12},{24,20},{5,9},{13,17},{21,25},... | collective-permute-start | bytes 417800 | tf_op jit(solution)/shard_map/ppermute | solution.py:528
  53.0 4.7 %collective-permute-start.6 = (f32[2,12,8,128]{3,2,1,0:T(8,128)S(1)}, f32[2,12,8,128]{3,2,1,0:T(8,128)S(1)}, u32[]{:S(2)}, u32[]{:S(2)}) collective-permute-start(f32[2,12,8,128]{3,2,1,0:T(8,128)S(1)} %get-tuple-element.22), channel_id=1, source_target_pairs={{0,8},{4,12},{8,0},{12,4},{16,24},{20,28},{24,16},{28,20},{1,9},{5... | collective-permute-start | bytes 294920 | tf_op jit(solution)/shard_map/ppermute | solution.py:540
  57.7 5.6 %collective-permute-start.7 = (f32[2,12,8,128]{3,2,1,0:T(8,128)S(1)}, f32[2,12,8,128]{3,2,1,0:T(8,128)S(1)}, u32[]{:S(2)}, u32[]{:S(2)}) collective-permute-start(f32[2,12,8,128]{3,2,1,0:T(8,128)S(1)} %pad_maximum_fusion), channel_id=1, source_target_pairs={{0,16},{4,20},{8,24},{12,28},{16,0},{20,4},{24,8},{28,12},{1,17},{... | collective-permute-start | bytes 294920 | tf_op jit(solution)/shard_map/ppermute | solution.py:540

commit v2 on v1

--- a/solution.py
+++ b/solution.py
@@ -7,6 +7,7 @@
 
 WIN_ROWS = 11
 WIN_COLS = 5
+INNER_DONE = 2
 ITERS = 20
 HALF_ROWS = WIN_ROWS // 2
 
@@ -93,8 +94,7 @@
                 z_ref[0, t, 2 * half - 1 - k] = flip(re)
                 z_ref[1, t, 2 * half - 1 - k] = flip(im)
             if k < HALF_ROWS:
-                first = jnp.where(top, re, flip(im))
-                second = jnp.where(top, flip(re), im)
+                first, second = pack(re, im, top)
                 x_ref[t, k] = jnp.where(odd, first, second)
                 y_ref[t, k] = jnp.where(odd, second, first)
         return carry
@@ -106,41 +106,8 @@
     return jnp.where(top, first, flip(second)), jnp.where(top, flip(first), second)
 
 
-def box_sum(field, lanes, edges):
-    count = len(field) - WIN_ROWS + 1
-    tail = [None] * WIN_ROWS
-    run = field[WIN_ROWS - 1]
-    tail[WIN_ROWS - 1] = run
-    for k in range(WIN_ROWS - 2, -1, -1):
-        run = run + field[k]
-        tail[k] = run
-    sums = [tail[0]]
-    run = None
-    for k in range(1, count):
-        new = field[WIN_ROWS - 1 + k]
-        run = new if run is None else run + new
-        sums.append(run if k == WIN_ROWS else tail[k] + run)
-    last_two, last_one, first_one, first_two = lanes
-    keep_before, keep_after = edges
-    out = []
-    for x in sums:
-        before = jnp.where(keep_before, pltpu.roll(x, 1, 0), 0.0)
-        after = jnp.where(keep_after, pltpu.roll(x, SUB - 1, 0), 0.0)
-        near = pltpu.roll(jnp.where(last_one, before, x), 1, 1) + pltpu.roll(
-            jnp.where(first_one, after, x), LANES - 1, 1
-        )
-        far = pltpu.roll(jnp.where(last_two, before, x), 2, 1) + pltpu.roll(
-            jnp.where(first_two, after, x), LANES - 2, 1
-        )
-        out.append(x + near + far)
-    return out
-
-
-def masks(tiles):
-    at = lane()
-    lanes = (at >= LANES - 2, at >= LANES - 1, at < 1, at < 2)
-    column = sublane() % tiles
-    return lanes, (column != 0, column != tiles - 1)
+def pack(re, im, top):
+    return jnp.where(top, re, flip(im)), jnp.where(top, flip(re), im)
 
 
 def add_to(total, sign, value):
@@ -149,63 +116,115 @@
     return total + value if sign > 0 else total - value
 
 
-def phases_kernel(
-    tiles, par_ref, iter_ref, chosen_ref, z_ref, x_ref, y_ref,
-    link_ref, comp_ref, pack_x_ref, pack_y_ref,
-    halo, inv, nr, ni, more, sq, vec,
+def running(values):
+    out = [values[0]]
+    for value in values[1:]:
+        out.append(out[-1] + value)
+    return out
+
+
+def inner_sums(field):
+    count = len(field) - WIN_ROWS + 1
+    tails = running(field[WIN_ROWS - 1 :: -1])[::-1]
+    if count <= WIN_ROWS:
+        core = running(field[count - 1 : WIN_ROWS])[-1]
+        tails = running([core] + field[: count - 1][::-1])[::-1]
+    heads = running(field[WIN_ROWS:])
+    middle = [tails[q] + heads[q - 1] for q in range(1, min(count, WIN_ROWS))]
+    return [tails[0]] + middle + heads[WIN_ROWS - 1 :]
+
+
+def fill_band(band_ref):
+    at = lax.broadcasted_iota(jnp.int32, band_ref.shape, 0) % LANES
+    to = lax.broadcasted_iota(jnp.int32, band_ref.shape, 1)
+    reach = WIN_COLS // 2
+    inside = (to < LANES) & (jnp.abs(at - to) <= reach)
+    to = to - LANES
+    beside = (to >= 0) & ((at >= to + LANES - reach) | (at <= to - LANES + reach))
+    band_ref[...] = jnp.where(inside | beside, 1.0, 0.0).astype(band_ref.dtype)
+
+
+def put_split(ref, at, vectors):
+    x = jnp.concatenate(vectors, axis=0)
+    high = x.astype(jnp.bfloat16)
+    low = (x - high.astype(jnp.float32)).astype(jnp.bfloat16)
+    ref[at, :, :LANES] = high
+    ref[at, :, LANES:] = low
+
+
+def side_masks(tiles):
+    column = sublane() % tiles
+    at = lane()
+    return (at < LANES // 2) & (column != 0), (at >= LANES // 2) & (column != tiles - 1)
+
+
+def column_sums(split_ref, first, size, band, sides):
+    rows = split_ref.shape[1]
+    terms = split_ref[first : first + size].reshape(size * rows, 2 * LANES)
+    both = jnp.dot(terms, band, preferred_element_type=jnp.float32)
+    from_before, from_after = sides
+    out = []
+    for k in range(size * rows // SUB):
+        inside = both[k * SUB : (k + 1) * SUB, :LANES]
+        beside = both[k * SUB : (k + 1) * SUB, LANES:]
+        before, after = pltpu.roll(beside, 1, 0), pltpu.roll(beside, SUB - 1, 0)
+        out.append(
+            inside + jnp.where(from_before, before, jnp.where(from_after, after, 0.0))
+        )
+    return out
+
+
+def pair_list(dates):
+    return [(i, j) for i in range(dates) for j in range(i + 1, dates)]
+
+
+CHUNK = 5
+
+
+def coherence(dates, vectors, fields, split_ref, band_ref, inv_ref, nr_ref, ni_ref, sides):
+    pairs = pair_list(dates)
+    band = band_ref[...]
+    powers = [fields(i, i) for i in range(dates)]
+    half = dates // 2
+    for e in range(half):
+        put_split(split_ref, e, powers[2 * e] + powers[2 * e + 1])
+    sums = column_sums(split_ref, 0, half, band, sides)
+    for i in range(dates):
+        for k in range(vectors):
+            inv_ref[i, k] = lax.rsqrt(sums[i * vectors + k]) * 0.5
+    for first in range(0, len(pairs), CHUNK):
+        size = min(CHUNK, len(pairs) - first)
+        for e in range(first, first + size):
+            re, im = fields(*pairs[e])
+            put_split(split_ref, half + e, re + im)
+        sums = column_sums(split_ref, half + first, size, band, sides)
+        for e in range(first, first + size):
+            i, j = pairs[e]
+            base = (e - first) * 2 * vectors
+            for k in range(vectors):
+                scale = inv_ref[i, k] * inv_ref[j, k]
+                nr_ref[e, k] = sums[base + k] * scale
+                ni_ref[e, k] = sums[base + vectors + k] * scale
+
+
+def cross(a, b):
+    (ar, ai), (br, bi) = a, b
+    re = [p * r + q * s for p, q, r, s in zip(ar, ai, br, bi)]
+    im = [q * r - p * s for p, q, r, s in zip(ar, ai, br, bi)]
+    return re, im
+
+
+def power_of(a):
+    return [p * p + q * q for p, q in zip(*a)]
+
+
+def iterate(
+    first, last, offset, dates, iter_ref, chosen_ref, z_ref, nr, ni, more, sq, vec,
+    link_ref, comp_ref, out_offset=0,
 ):
-    dates = z_ref.shape[1]
-    half = comp_ref.shape[1]
-    top = upper()
-    odd_device = par_ref[0] == 1
-    lanes, edges = masks(tiles)
-    pairs = [(i, j) for i in range(dates) for j in range(i + 1, dates)]
+    pairs = pair_list(dates)
     index = {pair: e for e, pair in enumerate(pairs)}
     count = len(pairs)
-    ext = half + 2 * HALF_ROWS
-
-    def fill(t, carry):
-        for k in range(HALF_ROWS):
-            a, b = x_ref[t, k], y_ref[t, k]
-            first = jnp.where(odd_device, a, b)
-            second = jnp.where(odd_device, b, a)
-            re, im = unpack(first, second, top)
-            halo[0, t, HALF_ROWS - 1 - k] = re
-            halo[1, t, HALF_ROWS - 1 - k] = im
-        return carry
-
-    lax.fori_loop(0, dates, fill, 0)
-
-    def image(part, t):
-        return [halo[part, t, k] for k in range(HALF_ROWS)] + [
-            z_ref[part, t, k] for k in range(ext - HALF_ROWS)
-        ]
-
-    def own_power(t, carry):
-        re, im = image(0, t), image(1, t)
-        power = box_sum([a * a + b * b for a, b in zip(re, im)], lanes, edges)
-        for k in range(half):
-            inv[t, k] = lax.rsqrt(power[k]) * 0.5
-        return carry
-
-    lax.fori_loop(0, dates, own_power, 0)
-
-    starts = {}
-    for d in range(1, dates):
-        def one_pair(i, carry, d=d):
-            j = i + d
-            ar, ai, br, bi = image(0, i), image(1, i), image(0, j), image(1, j)
-            re = box_sum([ar[k] * br[k] + ai[k] * bi[k] for k in range(ext)], lanes, edges)
-            im = box_sum([ai[k] * br[k] - ar[k] * bi[k] for k in range(ext)], lanes, edges)
-            at = i * (2 * dates - i - 1) // 2 + (j - i - 1)
-            for k in range(half):
-                scale = inv[i, k] * inv[j, k]
-                nr[at, k] = re[k] * scale
-                ni[at, k] = im[k] * scale
-            return carry
-
-        lax.fori_loop(0, dates - d, one_pair, 0)
-
     turns = jnp.minimum(iter_ref[0], ITERS)
     odd_turns = turns % 2 == 1
     steps = jnp.where(odd_turns, turns // 2, turns // 2 - 1)
@@ -215,7 +234,9 @@
         groups.append(tuple(range(at, at + size)))
         at += size
 
-    def one_vector(k, carry):
+    def one_vector(whole_k, carry):
+        k = whole_k - offset
+        place = whole_k - out_offset
         for e in range(count):
             re, im = nr[e, k], ni[e, k]
             more[e] = re + im
@@ -340,28 +361,143 @@
             vec[dates + i] = vi[i]
         cr = ci = None
         for i in range(dates):
-            zr, zi = z_ref[0, i, k], z_ref[1, i, k]
+            zr, zi = z_ref[0, i, whole_k], z_ref[1, i, whole_k]
             cr = add_to(cr, 1, vr[i] * zr + vi[i] * zi)
             ci = add_to(ci, 1, vr[i] * zi - vi[i] * zr)
-        comp_ref[0, k] = cr
-        comp_ref[1, k] = ci
+        comp_ref[0, place] = cr
+        comp_ref[1, place] = ci
         ref_r = vec[chosen_ref[0]] * float(dates)
         ref_i = vec[dates + chosen_ref[0]] * float(dates)
         for i in range(dates):
-            link_ref[0, i, k] = vr[i] * ref_r + vi[i] * ref_i
-            link_ref[1, i, k] = vi[i] * ref_r - vr[i] * ref_i
+            link_ref[0, i, place] = vr[i] * ref_r + vi[i] * ref_i
+            link_ref[1, i, place] = vi[i] * ref_r - vr[i] * ref_i
         return carry
 
-    lax.fori_loop(0, half, one_vector, 0)
+    lax.fori_loop(first, last, one_vector, 0)
+
+
+def inner_kernel(
+    tiles, done, iter_ref, chosen_ref, z_ref,
+    nr, ni, part_ref, link_ref, comp_ref,
+    band, split, inv, more, sq, vec,
+):
+    dates = z_ref.shape[1]
+    vectors = nr.shape[1]
+    ext = vectors + 2 * HALF_ROWS
+    pairs = pair_list(dates)
+    count = len(pairs)
+    index = {pair: e for e, pair in enumerate(pairs)}
+    fill_band(band)
+
+    def image(t):
+        return [[z_ref[part, t, k] for k in range(ext)] for part in range(2)]
+
+    def keep(at, field):
+        heads = running(field[: 2 * HALF_ROWS])
+        for k in range(HALF_ROWS):
+            part_ref[at, k] = heads[HALF_ROWS + k]
+
+    def fields(i, j):
+        if i == j:
+            power = power_of(image(i))
+            keep(2 * count + i, power)
+            return inner_sums(power)
+        re, im = cross(image(i), image(j))
+        e = index[i, j]
+        keep(e, re)
+        keep(count + e, im)
+        return inner_sums(re), inner_sums(im)
+
+    coherence(dates, vectors, fields, split, band, inv, nr, ni, side_masks(tiles))
+    iterate(
+        HALF_ROWS, HALF_ROWS + done, HALF_ROWS, dates, iter_ref, chosen_ref, z_ref, nr, ni,
+        more, sq, vec, link_ref, comp_ref, HALF_ROWS,
+    )
+
+
+def outer_kernel(
+    tiles, par_ref, iter_ref, chosen_ref, z_ref, part_ref, x_ref, y_ref,
+    link_ref, comp_ref, pack_x_ref, pack_y_ref,
+    halo, band, split, inv, nr, ni, more, sq, vec,
+):
+    dates = z_ref.shape[1]
+    top = upper()
+    odd_device = par_ref[0] == 1
+    pairs = pair_list(dates)
+    count = len(pairs)
+    index = {pair: e for e, pair in enumerate(pairs)}
+    fill_band(band)
+
+    def fill(t, carry):
+        for k in range(HALF_ROWS):
+            a, b = x_ref[t, k], y_ref[t, k]
+            re, im = unpack(jnp.where(odd_device, a, b), jnp.where(odd_device, b, a), top)
+            halo[0, t, k] = re
+            halo[1, t, k] = im
+        return carry
+
+    lax.fori_loop(0, dates, fill, 0)
+
+    def image(t):
+        return [[halo[part, t, k] for k in range(HALF_ROWS)] for part in range(2)]
+
+    def add(at, field):
+        tails = running(field)
+        return [tails[HALF_ROWS - 1 - k] + part_ref[at, k] for k in range(HALF_ROWS)]
+
+    def fields(i, j):
+        if i == j:
+            return add(2 * count + i, power_of(image(i)))
+        re, im = cross(image(i), image(j))
+        e = index[i, j]
+        return add(e, re), add(count + e, im)
+
+    coherence(dates, HALF_ROWS, fields, split, band, inv, nr, ni, side_masks(tiles))
+    iterate(
+        0, HALF_ROWS, 0, dates, iter_ref, chosen_ref, z_ref, nr, ni, more, sq, vec,
+        link_ref, comp_ref,
+    )
     for k in range(HALF_ROWS):
-        re, im = comp_ref[0, k], comp_ref[1, k]
-        first = jnp.where(top, re, flip(im))
-        second = jnp.where(top, flip(re), im)
+        first, second = pack(comp_ref[0, k], comp_ref[1, k], top)
         pack_x_ref[k] = jnp.where(odd_device, first, second)
         pack_y_ref[k] = jnp.where(odd_device, second, first)
 
 
-def extend_kernel(par_ref, comp_ref, x_ref, y_ref, out_ref):
+def rest_kernel(
+    start, iter_ref, chosen_ref, z_ref, nr, ni, after_ref, link_ref, comp_ref, more, sq, vec
+):
+    dates = z_ref.shape[1]
+    iterate(
+        start, start + comp_ref.shape[1], HALF_ROWS, dates, iter_ref, chosen_ref, z_ref, nr, ni,
+        more, sq, vec, link_ref, comp_ref, start,
+    )
+
+
+def box_sum(field, lanes, edges):
+    last_two, last_one, first_one, first_two = lanes
+    keep_before, keep_after = edges
+    out = []
+    for x in inner_sums(field):
+        before = jnp.where(keep_before, pltpu.roll(x, 1, 0), 0.0)
+        after = jnp.where(keep_after, pltpu.roll(x, SUB - 1, 0), 0.0)
+        near = pltpu.roll(jnp.where(last_one, before, x), 1, 1) + pltpu.roll(
+            jnp.where(first_one, after, x), LANES - 1, 1
+        )
+        far = pltpu.roll(jnp.where(last_two, before, x), 2, 1) + pltpu.roll(
+            jnp.where(first_two, after, x), LANES - 2, 1
+        )
+        out.append(x + near + far)
+    return out
+
+
+def masks(tiles):
+    at = lane()
+    lanes = (at >= LANES - 2, at >= LANES - 1, at < 1, at < 2)
+    column = sublane() % tiles
+    return lanes, (column != 0, column != tiles - 1)
+
+
+def extend_kernel(par_ref, outer_ref, inner_ref, rest_ref, x_ref, y_ref, out_ref):
     top = upper()
     odd_device = par_ref[0] == 1
     for k in range(HALF_ROWS):
@@ -370,8 +506,11 @@
         out_ref[0, HALF_ROWS - 1 - k] = re
         out_ref[1, HALF_ROWS - 1 - k] = im
     for part in range(2):
-        for k in range(comp_ref.shape[1]):
-            out_ref[part, HALF_ROWS + k] = comp_ref[part, k]
+        at = HALF_ROWS
+        for ref in (outer_ref, inner_ref, rest_ref):
+            for k in range(ref.shape[1]):
+                out_ref[part, at] = ref[part, k]
+                at += 1
 
 
 def offsets_kernel(tiles, place_ref, own_ref, a_ref, b_ref, unit_ref, total_ref):
@@ -427,12 +566,16 @@
         total_ref[1, k] = before_r * after_i + before_i * after_r
 
 
-def result_kernel(rows, tiles, link_ref, datum_ref, out_ref):
+def result_kernel(rows, tiles, outer_ref, inner_ref, rest_ref, datum_ref, out_ref):
     half = rows // 2
+    links = [
+        (ref, k) for ref in (outer_ref, inner_ref, rest_ref) for k in range(ref.shape[2])
+    ]
 
     def one_date(t, carry):
         for k in range(half):
-            lr, li = link_ref[0, t, k], link_ref[1, t, k]
+            ref, at = links[k]
+            lr, li = ref[0, t, at], ref[1, t, at]
             dr, di = datum_ref[0, k], datum_ref[1, k]
             first, second = bases(k, rows, tiles)
             for part, value in enumerate((lr * dr - li * di, lr * di + li * dr)):
@@ -440,7 +583,7 @@
                 out_ref[part, t, pl.ds(second, tiles, stride=SUB), :] = value[tiles:]
         return carry
 
-    lax.fori_loop(0, link_ref.shape[1], one_date, 0)
+    lax.fori_loop(0, outer_ref.shape[1], one_date, 0)
 
 
 def swaps(count, bit=None, odd=False):
@@ -491,39 +634,88 @@
     got_x = lax.ppermute(slab_x, "space", pair_x)
 
     count = dates * (dates - 1) // 2
-    linked, comp, pack_x, pack_y = pl.pallas_call(
-        lambda *refs: phases_kernel(tiles, *refs),
+    inner = half - HALF_ROWS
+    done = min(INNER_DONE, inner - 1)
+    work = [
+        pltpu.VMEM((2 * count, SUB, LANES), jnp.float32),
+        pltpu.VMEM((3 * count + dates, SUB, LANES), jnp.float32),
+        pltpu.VMEM((2 * dates, SUB, LANES), jnp.float32),
+    ]
+
+    def window_work(vectors):
+        return [
+            pltpu.VMEM((2 * LANES, 2 * LANES), jnp.bfloat16),
+            pltpu.VMEM((dates // 2 + count, 2 * vectors * SUB, 2 * LANES), jnp.bfloat16),
+            pltpu.VMEM((dates, vectors, SUB, LANES), jnp.float32),
+        ]
+
+    def cost(vectors):
+        return pl.CostEstimate(
+            flops=vectors * 2_000_000 * 8, bytes_accessed=1 << 20, transcendentals=0
+        )
+
+    nr, ni, part, linked_a, comp_a = pl.pallas_call(
+        lambda *refs: inner_kernel(tiles, done, *refs),
         out_shape=(
-            shape(2, dates, half, SUB, LANES),
-            shape(2, half, SUB, LANES),
+            shape(count, inner, SUB, LANES),
+            shape(count, inner, SUB, LANES),
+            shape(2 * count + dates, HALF_ROWS, SUB, LANES),
+            shape(2, dates, done, SUB, LANES),
+            shape(2, done, SUB, LANES),
+        ),
+        in_specs=[smem(), smem(), vmem()],
+        out_specs=(vmem(),) * 5,
+        scratch_shapes=window_work(inner) + work,
+        compiler_params=params,
+        cost_estimate=cost(4),
+        name="inner",
+    )(iterations, reference_date, z)
+    linked_b, comp_b, pack_x, pack_y = pl.pallas_call(
+        lambda *refs: outer_kernel(tiles, *refs),
+        out_shape=(
+            shape(2, dates, HALF_ROWS, SUB, LANES),
+            shape(2, HALF_ROWS, SUB, LANES),
             shape(HALF_ROWS, SUB, LANES),
             shape(HALF_ROWS, SUB, LANES),
         ),
-        in_specs=[smem(), smem(), smem(), vmem(), vmem(), vmem()],
-        out_specs=(vmem(), vmem(), vmem(), vmem()),
-        scratch_shapes=[
-            pltpu.VMEM((2, dates, HALF_ROWS, SUB, LANES), jnp.float32),
-            pltpu.VMEM((dates, half, SUB, LANES), jnp.float32),
-            pltpu.VMEM((count, half, SUB, LANES), jnp.float32),
-            pltpu.VMEM((count, half, SUB, LANES), jnp.float32),
-            pltpu.VMEM((2 * count, SUB, LANES), jnp.float32),
-            pltpu.VMEM((3 * count + dates, SUB, LANES), jnp.float32),
-            pltpu.VMEM((2 * dates, SUB, LANES), jnp.float32),
-        ],
+        in_specs=[smem(), smem(), smem()] + [vmem()] * 4,
+        out_specs=(vmem(),) * 4,
+        scratch_shapes=[pltpu.VMEM((2, dates, HALF_ROWS, SUB, LANES), jnp.float32)]
+        + window_work(HALF_ROWS)
+        + [
+            pltpu.VMEM((count, HALF_ROWS, SUB, LANES), jnp.float32),
+            pltpu.VMEM((count, HALF_ROWS, SUB, LANES), jnp.float32),
+        ]
+        + work,
         compiler_params=params,
-        name="phases",
-    )(parity, iterations, reference_date, z, got_x, got_y)
+        cost_estimate=cost(7),
+        name="outer",
+    )(parity, iterations, reference_date, z, part, got_x, got_y)
+    start = HALF_ROWS + done
+    linked_c, comp_c = pl.pallas_call(
+        lambda *refs: rest_kernel(start, *refs),
+        out_shape=(
+            shape(2, dates, half - start, SUB, LANES),
+            shape(2, half - start, SUB, LANES),
+        ),
+        in_specs=[smem(), smem()] + [vmem()] * 4,
+        out_specs=(vmem(),) * 2,
+        scratch_shapes=work,
+        compiler_params=params,
+        cost_estimate=cost(5),
+        name="rest",
+    )(iterations, reference_date, z, nr, ni, pack_x)
 
     more_y = lax.ppermute(pack_y, "space", pair_y)
     more_x = lax.ppermute(pack_x, "space", pair_x)
     wide = pl.pallas_call(
         extend_kernel,
         out_shape=shape(2, ext, SUB, LANES),
-        in_specs=[smem(), vmem(), vmem(), vmem()],
+        in_specs=[smem()] + [vmem()] * 5,
         out_specs=vmem(),
         compiler_params=params,
         name="extend",
-    )(parity, comp, more_x, more_y)
+    )(parity, comp_b, comp_a, comp_c, more_x, more_y)
     other_a = lax.ppermute(wide, "tm", swaps(members))
     other_b = lax.ppermute(wide, "tm", swaps(members, odd=True))
     where = jnp.stack([place, place % 2]).astype(jnp.int32)
@@ -544,11 +736,11 @@
     out = pl.pallas_call(
         lambda *refs: result_kernel(rows, tiles, *refs),
         out_shape=shape(2, dates, rows * tiles, LANES),
-        in_specs=[vmem(), vmem()],
+        in_specs=[vmem()] * 4,
         out_specs=vmem(),
         compiler_params=params,
         name="result",
-    )(linked, datum)
+    )(linked_b, linked_a, linked_c, datum)
     out = out.reshape(2, dates, rows // SUB, tiles, SUB, LANES)
     return jnp.swapaxes(out, -3, -2).reshape(2, dates, rows, columns)
 

time: 64.6 us -> 56.2 us (0.87)
  the two profiles are of different devices: /device:TPU:10 before, /device:TPU:0 now
where the time goes in v2:
time: 56.2 us; the launch traced here: 55.9 us
  Pallas kernels  20.7 us (37%)
  starting transfers between devices  18.3 us (33%)
  waiting for transfers between devices  12.5 us (22%)
  local copies, waits for them, and re-layouts  2.86 us (5%)
  between operations  1.42 us (3%)
    ppermute x2, waiting for transfers between devices, local(): other = lax.ppermute(total, 'tm', swaps(members, bit=bit))  9.91 us
    ppermute x2, starting transfers between devices, local(): other = lax.ppermute(total, 'tm', swaps(members, bit=bit))  9.25 us
    pallas_call x1, Pallas kernels, local(): pl.pallas_call(lambda *refs: outer_kernel(tiles, *refs), out_shape=(shape...  7.11 us
    pallas_call x1, Pallas kernels, local(): pl.pallas_call(lambda *refs: rest_kernel(start, *refs), out_shape=(shape(...  5.36 us
    pallas_call x1, Pallas kernels, local(): pl.pallas_call(lambda *refs: inner_kernel(tiles, done, *refs), out_shape=...  5.17 us
    ppermute x1, starting transfers between devices, local(): more_x = lax.ppermute(pack_x, 'space', pair_x)  3.91 us
    unnamed x6, local copies, waits for them, and re-layouts  2.86 us
    ppermute x1, waiting for transfers between devices, local(): other_a = lax.ppermute(wide, 'tm', swaps(members))  2.57 us
  transfers between devices with their start and end apart: 8, of which 3 were waited for; matrix products, arithmetic and copies ran while one was open for 0% of the time, Pallas kernels for 19%

profile of v2, /device:TPU:0, one launch (start us, length us, event | category | flops | bytes accessed | tf_op | source)
XLA Modules:
  0.0 55.9 jit_solution(12744834725056572223)
XLA Ops:
  0.0 0.0 copy-start
  0.0 1.0 %copy-done = f32[10,24,512]{2,1,0:T(8,128)S(1)} copy-done((f32[10,24,512]{2,1,0:T(8,128)S(1)}, f32[10,24,512]{2,1,0:T(8,128)}, u32[]{:S(2)}) %copy-start) | copy-done | bytes 491544
  1.0 0.0 copy-start.1
  1.0 1.0 %copy-done.1 = f32[10,24,512]{2,1,0:T(8,128)S(1)} copy-done((f32[10,24,512]{2,1,0:T(8,128)S(1)}, f32[10,24,512]{2,1,0:T(8,128)}, u32[]{:S(2)}) %copy-start.1) | copy-done | bytes 491544
  2.1 0.0 copy-start.2
  2.1 0.8 %copy-done.2 = s32[24,512]{1,0:T(8,128)S(1)} copy-done((s32[24,512]{1,0:T(8,128)S(1)}, s32[24,512]{1,0:T(8,128)}, u32[]{:S(2)}) %copy-start.2) | copy-done | bytes 49176
  2.9 0.8 %images.1 = (f32[2,10,17,8,128]{4,3,2,1,0:T(8,128)S(1)}, f32[10,5,8,128]{3,2,1,0:T(8,128)S(1)}, f32[10,5,8,128]{3,2,1,0:T(8,128)S(1)}) custom-call(s32[1]{0:T(128)} %bitcast.refs_0_.par_ref, f32[10,96,128]{2,1,0:T(8,128)S(1)} %bitcast.23, f32[10,96,128]{2,1,0:T(8,128)S(1)} %bitcast.24, s32[96,128]{1,0:T(8,128)S(1)} %bitcast.25), custom_call_target="tpu_custom_call" | custom-call | tf_op jit(solution)/shard_map/images/pallas_call | solution.py:620
  3.7 0.6 collective-permute-start
  4.3 0.7 %collective-permute-start.1 = (f32[10,5,8,128]{3,2,1,0:T(8,128)S(1)}, f32[10,5,8,128]{3,2,1,0:T(8,128)S(1)}, u32[]{:S(2)}, u32[]{:S(2)}) collective-permute-start(f32[10,5,8,128]{3,2,1,0:T(8,128)S(1)} %get-tuple-element.24), channel_id=1, source_target_pairs={{1,2},{2,1},{5,6},{6,5},{9,10},{10,9},{13,14},{14,13},{17,18},{18,... | collective-permute-start | bytes 614408 | tf_op jit(solution)/shard_map/ppermute | solution.py:633
  6.2 5.2 %inner.1 = (f32[45,7,8,128]{3,2,1,0:T(8,128)S(1)}, f32[45,7,8,128]{3,2,1,0:T(8,128)S(1)}, f32[100,5,8,128]{3,2,1,0:T(8,128)S(1)}, f32[2,10,2,8,128]{4,3,2,1,0:T(8,128)S(1)}, f32[2,2,8,128]{3,2,1,0:T(8,128)S(1)}) custom-call(s32[1]{0:T(128)S(6)} %copy.6.refs_0_.refs_1_, s32[1]{0:T(128)S(6)} %copy.7.refs_1_.refs_2_, ...), custom_call_target="tpu_custom_call" | custom-call | flops 64000000 | bytes 1048576 | tf_op jit(solution)/shard_map/inner/pallas_call | solution.py:657
  11.4 0.0 collective-permute-done.refs_5_
  11.4 0.0 collective-permute-done.1.refs_6_
  11.4 7.1 %outer.1 = (f32[2,10,5,8,128]{4,3,2,1,0:T(8,128)S(1)}, f32[2,5,8,128]{3,2,1,0:T(8,128)S(1)}, f32[5,8,128]{2,1,0:T(8,128)S(1)}, f32[5,8,128]{2,1,0:T(8,128)S(1)}) custom-call(s32[1]{0:T(128)} %bitcast.refs_0_.par_ref, s32[1]{0:T(128)S(6)} %copy.6.refs_0_.refs_1_, s32[1]{0:T(128)S(6)} %copy.7.refs_1_.refs_2_, ...), custom_call_target="tpu_custom_call" | custom-call | flops 112000000 | bytes 1048576 | tf_op jit(solution)/shard_map/outer/pallas_call | solution.py:673
  18.5 3.9 %collective-permute-start.2 = (f32[5,8,128]{2,1,0:T(8,128)S(1)}, f32[5,8,128]{2,1,0:T(8,128)S(1)}, u32[]{:S(2)}, u32[]{:S(2)}) collective-permute-start(f32[5,8,128]{2,1,0:T(8,128)S(1)} %get-tuple-element.29.refs_5_), channel_id=1, source_target_pairs={{0,1},{2,3},{1,0},{3,2},{4,5},{6,7},{5,4},{7,6},{8,9},{10,11},{9,8... | collective-permute-start | bytes 61448 | tf_op jit(solution)/shard_map/ppermute | solution.py:710
  22.5 0.7 %collective-permute-start.3 = (f32[5,8,128]{2,1,0:T(8,128)S(1)}, f32[5,8,128]{2,1,0:T(8,128)S(1)}, u32[]{:S(2)}, u32[]{:S(2)}) collective-permute-start(f32[5,8,128]{2,1,0:T(8,128)S(1)} %get-tuple-element.34), channel_id=1, source_target_pairs={{1,2},{2,1},{5,6},{6,5},{9,10},{10,9},{13,14},{14,13},{17,18},{18,... | collective-permute-start | bytes 61448 | tf_op jit(solution)/shard_map/ppermute | solution.py:709
  23.1 5.4 %rest.1 = (f32[2,10,5,8,128]{4,3,2,1,0:T(8,128)S(1)}, f32[2,5,8,128]{3,2,1,0:T(8,128)S(1)}) custom-call(s32[1]{0:T(128)S(6)} %copy.6.refs_0_.refs_1_, s32[1]{0:T(128)S(6)} %copy.7.refs_1_.refs_2_, f32[2,10,17,8,128]{4,3,2,1,0:T(8,128)S(1)} %get-tuple-element.21.refs_2_.refs_3_, f32[45,7,8,128]{3,2,1,0:T(8,128)S(1)} %get-tuple-element.27.refs_3_, ...), custom_call_target="tpu_custom_call" | custom-call | flops 80000000 | bytes 1048576 | tf_op jit(solution)/shard_map/rest/pallas_call | solution.py:695
  28.5 0.0 collective-permute-done.2.x_ref
  28.5 0.0 collective-permute-done.3.y_ref
  28.5 2.6 %collective-permute-start.4 = (f32[2,17,8,128]{3,2,1,0:T(8,128)S(1)}, f32[2,17,8,128]{3,2,1,0:T(8,128)S(1)}, u32[]{:S(2)}, u32[]{:S(2)}) collective-permute-start(f32[2,17,8,128]{3,2,1,0:T(8,128)S(1)} %extend.1.refs_1_), channel_id=1, source_target_pairs={{0,4},{8,12},{16,20},{24,28},{4,0},{12,8},{20,16},{28,24},{1,5},{9... | collective-permute-start | bytes 417800 | tf_op jit(solution)/shard_map/ppermute | solution.py:719
  31.1 0.7 %collective-permute-start.5 = (f32[2,17,8,128]{3,2,1,0:T(8,128)S(1)}, f32[2,17,8,128]{3,2,1,0:T(8,128)S(1)}, u32[]{:S(2)}, u32[]{:S(2)}) collective-permute-start(f32[2,17,8,128]{3,2,1,0:T(8,128)S(1)} %extend.1.refs_1_), channel_id=1, source_target_pairs={{4,8},{12,16},{20,24},{8,4},{16,12},{24,20},{5,9},{13,17},{21,25},... | collective-permute-start | bytes 417800 | tf_op jit(solution)/shard_map/ppermute | solution.py:720
  31.8 0.1 pad_add_fusion.refs_0_
  31.8 2.6 %collective-permute-done.4.refs_2_ = f32[2,17,8,128]{3,2,1,0:T(8,128)S(1)} collective-permute-done((f32[2,17,8,128]{3,2,1,0:T(8,128)S(1)}, f32[2,17,8,128]{3,2,1,0:T(8,128)S(1)}, u32[]{:S(2)}, u32[]{:S(2)}) %collective-permute-start.4) | collective-permute-done | bytes 139296 | tf_op jit(solution)/shard_map/ppermute | solution.py:719
  34.4 0.0 collective-permute-done.5.refs_3_
  34.4 1.0 %offsets.1 = (f32[2,12,8,128]{3,2,1,0:T(8,128)S(1)}, f32[2,12,8,128]{3,2,1,0:T(8,128)S(1)}) custom-call(s32[2]{0:T(128)S(1)} %pad_add_fusion.refs_0_, f32[2,17,8,128]{3,2,1,0:T(8,128)S(1)} %extend.1.refs_1_, f32[2,17,8,128]{3,2,1,0:T(8,128)S(1)} %collective-permute-done.4.refs_2_, f32[2,17,8,128]{3,2,1,0:T(8,128)S(1)} %collective-permute-done.5.refs_3_), custom_call_target="tpu_custom_call" | custom-call | tf_op jit(solution)/shard_map/offsets/pallas_call | solution.py:722
  35.4 8.1 %collective-permute-start.6 = (f32[2,12,8,128]{3,2,1,0:T(8,128)S(1)}, f32[2,12,8,128]{3,2,1,0:T(8,128)S(1)}, u32[]{:S(2)}, u32[]{:S(2)}) collective-permute-start(f32[2,12,8,128]{3,2,1,0:T(8,128)S(1)} %get-tuple-element.36), channel_id=1, source_target_pairs={{0,8},{4,12},{8,0},{12,4},{16,24},{20,28},{24,16},{28,20},{1,9},{5... | collective-permute-start | bytes 294920 | tf_op jit(solution)/shard_map/ppermute | solution.py:732
  43.5 3.4 %collective-permute-done.6 = f32[2,12,8,128]{3,2,1,0:T(8,128)S(1)} collective-permute-done((f32[2,12,8,128]{3,2,1,0:T(8,128)S(1)}, f32[2,12,8,128]{3,2,1,0:T(8,128)S(1)}, u32[]{:S(2)}, u32[]{:S(2)}) %collective-permute-start.6) | collective-permute-done | bytes 98336 | tf_op jit(solution)/shard_map/ppermute | solution.py:732
  47.0 1.2 %collective-permute-start.7 = (f32[2,12,8,128]{3,2,1,0:T(8,128)S(1)}, f32[2,12,8,128]{3,2,1,0:T(8,128)S(1)}, u32[]{:S(2)}, u32[]{:S(2)}) collective-permute-start(f32[2,12,8,128]{3,2,1,0:T(8,128)S(1)} %pad_maximum_fusion), channel_id=1, source_target_pairs={{0,16},{4,20},{8,24},{12,28},{16,0},{20,4},{24,8},{28,12},{1,17},{... | collective-permute-start | bytes 294920 | tf_op jit(solution)/shard_map/ppermute | solution.py:732
  48.2 6.5 %collective-permute-done.7 = f32[2,12,8,128]{3,2,1,0:T(8,128)S(1)} collective-permute-done((f32[2,12,8,128]{3,2,1,0:T(8,128)S(1)}, f32[2,12,8,128]{3,2,1,0:T(8,128)S(1)}, u32[]{:S(2)}, u32[]{:S(2)}) %collective-permute-start.7) | collective-permute-done | bytes 98336 | tf_op jit(solution)/shard_map/ppermute | solution.py:732
  54.7 1.2 %result.1 = f32[2,10,96,128]{3,2,1,0:T(8,128)} custom-call(f32[2,10,5,8,128]{4,3,2,1,0:T(8,128)S(1)} %get-tuple-element.25.refs_0_, f32[2,10,2,8,128]{4,3,2,1,0:T(8,128)S(1)} %get-tuple-element.26.refs_1_, f32[2,10,5,8,128]{4,3,2,1,0:T(8,128)S(1)} %get-tuple-element.30.refs_2_, f32[2,12,8,128]{3,2,1,0:T(8,128)S(1)} %maximum_select_fusion.1.refs_3_), custom_call_target="tpu_custom_call" | custom-call | tf_op jit(solution)/shard_map/result/pallas_call | solution.py:736
  (6 shorter events, 0.1 us)
Async XLA Ops:
  0.0 1.0 %copy-start = (f32[10,24,512]{2,1,0:T(8,128)S(1)}, f32[10,24,512]{2,1,0:T(8,128)}, u32[]{:S(2)}) copy-start(f32[10,24,512]{2,1,0:T(8,128)} %param.5) | copy-start | bytes 1474564
  1.0 1.0 %copy-start.1 = (f32[10,24,512]{2,1,0:T(8,128)S(1)}, f32[10,24,512]{2,1,0:T(8,128)}, u32[]{:S(2)}) copy-start(f32[10,24,512]{2,1,0:T(8,128)} %param.6) | copy-start | bytes 1474564
  2.1 0.8 %copy-start.2 = (s32[24,512]{1,0:T(8,128)S(1)}, s32[24,512]{1,0:T(8,128)}, u32[]{:S(2)}) copy-start(s32[24,512]{1,0:T(8,128)} %param.7) | copy-start | bytes 147460
  3.7 7.7 %collective-permute-start = (f32[10,5,8,128]{3,2,1,0:T(8,128)S(1)}, f32[10,5,8,128]{3,2,1,0:T(8,128)S(1)}, u32[]{:S(2)}, u32[]{:S(2)}) collective-permute-start(f32[10,5,8,128]{3,2,1,0:T(8,128)S(1)} %get-tuple-element.23), channel_id=1, source_target_pairs={{0,1},{2,3},{1,0},{3,2},{4,5},{6,7},{5,4},{7,6},{8,9},{10,11},{9,8... | collective-permute-start | bytes 614408 | tf_op jit(solution)/shard_map/ppermute | solution.py:634
  4.3 7.2 %collective-permute-start.1 = (f32[10,5,8,128]{3,2,1,0:T(8,128)S(1)}, f32[10,5,8,128]{3,2,1,0:T(8,128)S(1)}, u32[]{:S(2)}, u32[]{:S(2)}) collective-permute-start(f32[10,5,8,128]{3,2,1,0:T(8,128)S(1)} %get-tuple-element.24), channel_id=1, source_target_pairs={{1,2},{2,1},{5,6},{6,5},{9,10},{10,9},{13,14},{14,13},{17,18},{18,... | collective-permute-start | bytes 614408 | tf_op jit(solution)/shard_map/ppermute | solution.py:633
  18.5 9.9 %collective-permute-start.2 = (f32[5,8,128]{2,1,0:T(8,128)S(1)}, f32[5,8,128]{2,1,0:T(8,128)S(1)}, u32[]{:S(2)}, u32[]{:S(2)}) collective-permute-start(f32[5,8,128]{2,1,0:T(8,128)S(1)} %get-tuple-element.29.refs_5_), channel_id=1, source_target_pairs={{0,1},{2,3},{1,0},{3,2},{4,5},{6,7},{5,4},{7,6},{8,9},{10,11},{9,8... | collective-permute-start | bytes 61448 | tf_op jit(solution)/shard_map/ppermute | solution.py:710
  22.5 6.0 %collective-permute-start.3 = (f32[5,8,128]{2,1,0:T(8,128)S(1)}, f32[5,8,128]{2,1,0:T(8,128)S(1)}, u32[]{:S(2)}, u32[]{:S(2)}) collective-permute-start(f32[5,8,128]{2,1,0:T(8,128)S(1)} %get-tuple-element.34), channel_id=1, source_target_pairs={{1,2},{2,1},{5,6},{6,5},{9,10},{10,9},{13,14},{14,13},{17,18},{18,... | collective-permute-start | bytes 61448 | tf_op jit(solution)/shard_map/ppermute | solution.py:709
  28.5 5.9 %collective-permute-start.4 = (f32[2,17,8,128]{3,2,1,0:T(8,128)S(1)}, f32[2,17,8,128]{3,2,1,0:T(8,128)S(1)}, u32[]{:S(2)}, u32[]{:S(2)}) collective-permute-start(f32[2,17,8,128]{3,2,1,0:T(8,128)S(1)} %extend.1.refs_1_), channel_id=1, source_target_pairs={{0,4},{8,12},{16,20},{24,28},{4,0},{12,8},{20,16},{28,24},{1,5},{9... | collective-permute-start | bytes 417800 | tf_op jit(solution)/shard_map/ppermute | solution.py:719
  31.1 3.3 %collective-permute-start.5 = (f32[2,17,8,128]{3,2,1,0:T(8,128)S(1)}, f32[2,17,8,128]{3,2,1,0:T(8,128)S(1)}, u32[]{:S(2)}, u32[]{:S(2)}) collective-permute-start(f32[2,17,8,128]{3,2,1,0:T(8,128)S(1)} %extend.1.refs_1_), channel_id=1, source_target_pairs={{4,8},{12,16},{20,24},{8,4},{16,12},{24,20},{5,9},{13,17},{21,25},... | collective-permute-start | bytes 417800 | tf_op jit(solution)/shard_map/ppermute | solution.py:720
  35.4 11.5 %collective-permute-start.6 = (f32[2,12,8,128]{3,2,1,0:T(8,128)S(1)}, f32[2,12,8,128]{3,2,1,0:T(8,128)S(1)}, u32[]{:S(2)}, u32[]{:S(2)}) collective-permute-start(f32[2,12,8,128]{3,2,1,0:T(8,128)S(1)} %get-tuple-element.36), channel_id=1, source_target_pairs={{0,8},{4,12},{8,0},{12,4},{16,24},{20,28},{24,16},{28,20},{1,9},{5... | collective-permute-start | bytes 294920 | tf_op jit(solution)/shard_map/ppermute | solution.py:732
  47.0 7.7 %collective-permute-start.7 = (f32[2,12,8,128]{3,2,1,0:T(8,128)S(1)}, f32[2,12,8,128]{3,2,1,0:T(8,128)S(1)}, u32[]{:S(2)}, u32[]{:S(2)}) collective-permute-start(f32[2,12,8,128]{3,2,1,0:T(8,128)S(1)} %pad_maximum_fusion), channel_id=1, source_target_pairs={{0,16},{4,20},{8,24},{12,28},{16,0},{20,4},{24,8},{28,12},{1,17},{... | collective-permute-start | bytes 294920 | tf_op jit(solution)/shard_map/ppermute | solution.py:732

commit v3 on v2

--- a/solution.py
+++ b/solution.py
@@ -5,9 +5,12 @@
 from jax.experimental.pallas import tpu as pltpu
 from jax.sharding import PartitionSpec as P
 
+
 WIN_ROWS = 11
 WIN_COLS = 5
-INNER_DONE = 2
+INNER_DONE = 1
+MIDDLE = 2
+PIECE = 5
 ITERS = 20
 HALF_ROWS = WIN_ROWS // 2
 
@@ -16,11 +19,15 @@
 
 LANES = 128
 SUB = 8
-VMEM_LIMIT = 40 * 1024 * 1024
+VMEM_LIMIT = 52 * 1024 * 1024
 
 
 def vmem():
     return pl.BlockSpec(memory_space=pltpu.VMEM)
+
+
+def hbm():
+    return pl.BlockSpec(memory_space=pltpu.MemorySpace.HBM)
 
 
 def smem():
@@ -74,10 +81,30 @@
     return sin_x, cos_x
 
 
-def images_kernel(rows, tiles, par_ref, amp_ref, phase_ref, valid_ref, z_ref, x_ref, y_ref):
+def images_kernel(
+    rows, tiles, par_ref, amp_hbm, phase_hbm, valid_hbm, z_ref, x_ref, y_ref,
+    amp_ref, phase_ref, valid_ref, sems,
+):
     half = rows // 2
+    dates = z_ref.shape[1]
     top = upper()
     odd = par_ref[0] == 1
+    step = PIECE if dates % PIECE == 0 else dates
+    copies = []
+    for p in range(dates // step):
+        part = pl.ds(p * step, step)
+        copies.append(
+            [
+                pltpu.make_async_copy(amp_hbm.at[part], amp_ref.at[part], sems.at[0, p]),
+                pltpu.make_async_copy(phase_hbm.at[part], phase_ref.at[part], sems.at[1, p]),
+            ]
+        )
+    weights = pltpu.make_async_copy(valid_hbm, valid_ref, sems.at[2, 0])
+    weights.start()
+    for pair in copies:
+        for copy in pair:
+            copy.start()
+    weights.wait()
     roots = []
     for k in range(half):
         valid = load_pair(valid_ref, (), k, rows, tiles, top)
@@ -99,7 +126,10 @@
                 y_ref[t, k] = jnp.where(odd, second, first)
         return carry
 
-    lax.fori_loop(0, z_ref.shape[1], one_date, 0)
+    for p, pair in enumerate(copies):
+        for copy in pair:
+            copy.wait()
+        lax.fori_loop(p * step, (p + 1) * step, one_date, 0)
 
 
 def unpack(first, second, top):
@@ -181,7 +211,7 @@
 CHUNK = 5
 
 
-def coherence(dates, vectors, fields, split_ref, band_ref, inv_ref, nr_ref, ni_ref, sides):
+def coherence(dates, vectors, fields, split_ref, band_ref, inv_ref, places, sides):
     pairs = pair_list(dates)
     band = band_ref[...]
     powers = [fields(i, i) for i in range(dates)]
@@ -203,8 +233,9 @@
             base = (e - first) * 2 * vectors
             for k in range(vectors):
                 scale = inv_ref[i, k] * inv_ref[j, k]
-                nr_ref[e, k] = sums[base + k] * scale
-                ni_ref[e, k] = sums[base + vectors + k] * scale
+                nr_ref, ni_ref, at = places[k]
+                nr_ref[e, at] = sums[base + k] * scale
+                ni_ref[e, at] = sums[base + vectors + k] * scale
 
 
 def cross(a, b):
@@ -219,15 +250,13 @@
 
 
 def iterate(
-    first, last, offset, dates, iter_ref, chosen_ref, z_ref, nr, ni, more, sq, vec,
+    first, last, offset, dates, scalars, z_ref, nr, ni, more, sq, vec,
     link_ref, comp_ref, out_offset=0,
 ):
     pairs = pair_list(dates)
     index = {pair: e for e, pair in enumerate(pairs)}
     count = len(pairs)
-    turns = jnp.minimum(iter_ref[0], ITERS)
-    odd_turns = turns % 2 == 1
-    steps = jnp.where(odd_turns, turns // 2, turns // 2 - 1)
+    iter_ref, chosen_ref = scalars
     groups = []
     at = 0
     for size in (3, 3, 4) if dates == 10 else (dates,):
@@ -293,6 +322,10 @@
             size[j] = add_to(size[j], 1, value)
         for i in range(dates):
             sq[3 * count + i] = size[i] + 0.25
+
+        turns = jnp.minimum(iter_ref[0], ITERS)
+        odd_turns = turns % 2 == 1
+        steps = jnp.where(odd_turns, turns // 2, turns // 2 - 1)
 
         def row_sums(re_of, im_of, own):
             sr, si = [own(i) for i in range(dates)], [None] * dates
@@ -378,15 +411,21 @@
 
 def inner_kernel(
     tiles, done, iter_ref, chosen_ref, z_ref,
-    nr, ni, part_ref, link_ref, comp_ref,
-    band, split, inv, more, sq, vec,
+    nr_b, ni_b, nr_c, ni_c, part_ref, link_ref, comp_ref,
+    band, split, inv, nr_a, ni_a, more, sq, vec,
 ):
     dates = z_ref.shape[1]
-    vectors = nr.shape[1]
+    places = [
+        (nr, ni, k)
+        for nr, ni in ((nr_a, ni_a), (nr_b, ni_b), (nr_c, ni_c))
+        for k in range(nr.shape[1])
+    ]
+    vectors = len(places)
     ext = vectors + 2 * HALF_ROWS
     pairs = pair_list(dates)
     count = len(pairs)
     index = {pair: e for e, pair in enumerate(pairs)}
+    scalars = iter_ref, chosen_ref
     fill_band(band)
 
     def image(t):
@@ -408,9 +447,9 @@
         keep(count + e, im)
         return inner_sums(re), inner_sums(im)
 
-    coherence(dates, vectors, fields, split, band, inv, nr, ni, side_masks(tiles))
+    coherence(dates, vectors, fields, split, band, inv, places, side_masks(tiles))
     iterate(
-        HALF_ROWS, HALF_ROWS + done, HALF_ROWS, dates, iter_ref, chosen_ref, z_ref, nr, ni,
+        HALF_ROWS, HALF_ROWS + done, HALF_ROWS, dates, scalars, z_ref, nr_a, ni_a,
         more, sq, vec, link_ref, comp_ref, HALF_ROWS,
     )
 
@@ -423,14 +462,16 @@
     dates = z_ref.shape[1]
     top = upper()
     odd_device = par_ref[0] == 1
+    edge = par_ref[1] == 1
     pairs = pair_list(dates)
     count = len(pairs)
     index = {pair: e for e, pair in enumerate(pairs)}
+    scalars = iter_ref, chosen_ref
     fill_band(band)
 
     def fill(t, carry):
         for k in range(HALF_ROWS):
-            a, b = x_ref[t, k], y_ref[t, k]
+            a, b = x_ref[t, k], jnp.where(edge, 0.0, y_ref[t, k])
             re, im = unpack(jnp.where(odd_device, a, b), jnp.where(odd_device, b, a), top)
             halo[0, t, k] = re
             halo[1, t, k] = im
@@ -452,9 +493,10 @@
         e = index[i, j]
         return add(e, re), add(count + e, im)
 
-    coherence(dates, HALF_ROWS, fields, split, band, inv, nr, ni, side_masks(tiles))
+    places = [(nr, ni, k) for k in range(HALF_ROWS)]
+    coherence(dates, HALF_ROWS, fields, split, band, inv, places, side_masks(tiles))
     iterate(
-        0, HALF_ROWS, 0, dates, iter_ref, chosen_ref, z_ref, nr, ni, more, sq, vec,
+        0, HALF_ROWS, 0, dates, scalars, z_ref, nr, ni, more, sq, vec,
         link_ref, comp_ref,
     )
     for k in range(HALF_ROWS):
@@ -464,11 +506,13 @@
 
 
 def rest_kernel(
-    start, iter_ref, chosen_ref, z_ref, nr, ni, after_ref, link_ref, comp_ref, more, sq, vec
+    start, iter_ref, chosen_ref, z_ref, nr, ni, after_ref, link_ref, comp_ref,
+    more, sq, vec,
 ):
     dates = z_ref.shape[1]
+    scalars = iter_ref, chosen_ref
     iterate(
-        start, start + comp_ref.shape[1], HALF_ROWS, dates, iter_ref, chosen_ref, z_ref, nr, ni,
+        start, start + comp_ref.shape[1], start, dates, scalars, z_ref, nr, ni,
         more, sq, vec, link_ref, comp_ref, start,
     )
 
@@ -497,32 +541,44 @@
     return lanes, (column != 0, column != tiles - 1)
 
 
-def extend_kernel(par_ref, outer_ref, inner_ref, rest_ref, x_ref, y_ref, out_ref):
+def extend_kernel(par_ref, outer_ref, inner_ref, x_ref, y_ref, out_ref):
     top = upper()
     odd_device = par_ref[0] == 1
+    edge = par_ref[1] == 1
     for k in range(HALF_ROWS):
-        a, b = x_ref[k], y_ref[k]
+        a, b = x_ref[k], jnp.where(edge, 0.0, y_ref[k])
         re, im = unpack(jnp.where(odd_device, a, b), jnp.where(odd_device, b, a), top)
         out_ref[0, HALF_ROWS - 1 - k] = re
         out_ref[1, HALF_ROWS - 1 - k] = im
     for part in range(2):
         at = HALF_ROWS
-        for ref in (outer_ref, inner_ref, rest_ref):
+        for ref in (outer_ref, inner_ref):
             for k in range(ref.shape[1]):
                 out_ref[part, at] = ref[part, k]
                 at += 1
 
 
-def offsets_kernel(tiles, place_ref, own_ref, a_ref, b_ref, unit_ref, total_ref):
+def gather_kernel(first_ref, second_ref, out_ref):
+    for part in range(2):
+        at = 0
+        for ref in (first_ref, second_ref):
+            for k in range(ref.shape[1]):
+                out_ref[part, at] = ref[part, k]
+                at += 1
+
+
+def offsets_kernel(
+    tiles, place_ref, own_w, own_n, a_w, a_n, b_w, b_n, unit_ref, total_ref
+):
     lanes, edges = masks(tiles)
     half = unit_ref.shape[1]
     odd_stack = place_ref[1] == 1
     first_stack = place_ref[0] == 0
 
-    def whole(ref):
+    def whole(*refs):
         parts = []
         for part in range(2):
-            rows_in = [ref[part, k] for k in range(ref.shape[1])]
+            rows_in = [ref[part, k] for ref in refs for k in range(ref.shape[1])]
             rows_in += [flip(rows_in[-1 - k]) for k in range(HALF_ROWS)]
             parts.append(rows_in)
         return parts
@@ -530,11 +586,11 @@
     def power(re, im):
         return box_sum([a * a + b * b for a, b in zip(re, im)], lanes, edges)
 
-    own_r, own_i = whole(own_ref)
+    own_r, own_i = whole(own_w, own_n)
     own = [p + 1.0 for p in power(own_r, own_i)]
 
-    def unit(ref):
-        re, im = whole(ref)
+    def unit(*refs):
+        re, im = whole(*refs)
         other = power(re, im)
         cross_r = box_sum(
             [a * c + b * d for a, b, c, d in zip(own_r, own_i, re, im)], lanes, edges
@@ -551,7 +607,7 @@
             out.append((off_r * back, off_i * back))
         return out
 
-    pair_a, pair_b = unit(a_ref), unit(b_ref)
+    pair_a, pair_b = unit(a_w, a_n), unit(b_w, b_n)
     for k in range(half):
         (ar, ai), (br, bi) = pair_a[k], pair_b[k]
         before_r = jnp.where(odd_stack, ar, br)
@@ -566,11 +622,10 @@
         total_ref[1, k] = before_r * after_i + before_i * after_r
 
 
-def result_kernel(rows, tiles, outer_ref, inner_ref, rest_ref, datum_ref, out_ref):
+def result_kernel(rows, tiles, outer_ref, inner_ref, middle_ref, last_ref, datum_ref, out_ref):
     half = rows // 2
-    links = [
-        (ref, k) for ref in (outer_ref, inner_ref, rest_ref) for k in range(ref.shape[2])
-    ]
+    parts = (outer_ref, inner_ref, middle_ref, last_ref)
+    links = [(ref, k) for ref in parts for k in range(ref.shape[2])]
 
     def one_date(t, carry):
         for k in range(half):
@@ -588,17 +643,17 @@
 
 def swaps(count, bit=None, odd=False):
     if bit is not None:
-        return [(i, i ^ bit) for i in range(count) if (i ^ bit) < count]
-    first = 1 if odd else 0
-    pairs = [(i, i + 1) for i in range(first, count - 1, 2)]
-    return pairs + [(j, i) for i, j in pairs]
+        return [(i, i ^ bit) for i in range(count)]
+    if odd:
+        return [(i, (i + 1 if i % 2 else i - 1) % count) for i in range(count)]
+    return [(i, i ^ 1) for i in range(count)]
 
 
 def times(a, b):
     return jnp.stack([a[0] * b[0] - a[1] * b[1], a[0] * b[1] + a[1] * b[0]])
 
 
-def local(amplitude, phase, validity, iterations, reference_date):
+def linked_phases(amplitude, phase, validity, iterations, reference_date):
     dates, rows, columns = amplitude.shape
     half = rows // 2
     tiles = columns // LANES
@@ -606,7 +661,9 @@
     members = lax.axis_size("tm")
     blocks = lax.axis_size("space")
     place = lax.axis_index("tm")
-    parity = (lax.axis_index("space") % 2).reshape(1)
+    block = lax.axis_index("space")
+    edge = (block == 0) | (block == blocks - 1)
+    parity = jnp.stack([block % 2, edge.astype(jnp.int32)])
     params = pltpu.CompilerParams(vmem_limit_bytes=VMEM_LIMIT)
 
     def shape(*dims):
@@ -616,6 +673,9 @@
         lead = x.shape[:-2]
         x = x.reshape(lead + (rows // SUB, SUB, tiles, LANES))
         return jnp.swapaxes(x, -3, -2).reshape(lead + (rows * tiles, LANES))
+
+    def far_memory(x):
+        return pltpu.with_memory_space_constraint(x, pltpu.MemorySpace.HBM)
 
     z, slab_x, slab_y = pl.pallas_call(
         lambda *refs: images_kernel(rows, tiles, *refs),
@@ -624,11 +684,17 @@
             shape(dates, HALF_ROWS, SUB, LANES),
             shape(dates, HALF_ROWS, SUB, LANES),
         ),
-        in_specs=[smem(), vmem(), vmem(), vmem()],
+        in_specs=[smem(), hbm(), hbm(), hbm()],
         out_specs=(vmem(), vmem(), vmem()),
+        scratch_shapes=[
+            pltpu.VMEM((dates, rows * tiles, LANES), jnp.float32),
+            pltpu.VMEM((dates, rows * tiles, LANES), jnp.float32),
+            pltpu.VMEM((rows * tiles, LANES), jnp.int32),
+            pltpu.SemaphoreType.DMA((3, dates)),
+        ],
         compiler_params=params,
         name="images",
-    )(parity, tiled(amplitude), tiled(phase), tiled(validity))
+    )(parity, *(far_memory(tiled(x)) for x in (amplitude, phase, validity)))
     pair_x, pair_y = swaps(blocks), swaps(blocks, odd=True)
     got_y = lax.ppermute(slab_y, "space", pair_y)
     got_x = lax.ppermute(slab_x, "space", pair_x)
@@ -654,18 +720,24 @@
             flops=vectors * 2_000_000 * 8, bytes_accessed=1 << 20, transcendentals=0
         )
 
-    nr, ni, part, linked_a, comp_a = pl.pallas_call(
+    middle = min(MIDDLE, inner - done - 1)
+    last = inner - done - middle
+    nr_b, ni_b, nr_c, ni_c, part, linked_a, comp_a = pl.pallas_call(
         lambda *refs: inner_kernel(tiles, done, *refs),
         out_shape=(
-            shape(count, inner, SUB, LANES),
-            shape(count, inner, SUB, LANES),
+            shape(count, middle, SUB, LANES),
+            shape(count, middle, SUB, LANES),
+            shape(count, last, SUB, LANES),
+            shape(count, last, SUB, LANES),
             shape(2 * count + dates, HALF_ROWS, SUB, LANES),
             shape(2, dates, done, SUB, LANES),
             shape(2, done, SUB, LANES),
         ),
         in_specs=[smem(), smem(), vmem()],
-        out_specs=(vmem(),) * 5,
-        scratch_shapes=window_work(inner) + work,
+        out_specs=(vmem(),) * 7,
+        scratch_shapes=window_work(inner)
+        + [pltpu.VMEM((count, done, SUB, LANES), jnp.float32)] * 2
+        + work,
         compiler_params=params,
         cost_estimate=cost(4),
         name="inner",
@@ -678,7 +750,7 @@
             shape(HALF_ROWS, SUB, LANES),
             shape(HALF_ROWS, SUB, LANES),
         ),
-        in_specs=[smem(), smem(), smem()] + [vmem()] * 4,
+        in_specs=[smem()] * 3 + [vmem()] * 4,
         out_specs=(vmem(),) * 4,
         scratch_shapes=[pltpu.VMEM((2, dates, HALF_ROWS, SUB, LANES), jnp.float32)]
         + window_work(HALF_ROWS)
@@ -691,63 +763,81 @@
         cost_estimate=cost(7),
         name="outer",
     )(parity, iterations, reference_date, z, part, got_x, got_y)
-    start = HALF_ROWS + done
-    linked_c, comp_c = pl.pallas_call(
-        lambda *refs: rest_kernel(start, *refs),
-        out_shape=(
-            shape(2, dates, half - start, SUB, LANES),
-            shape(2, half - start, SUB, LANES),
-        ),
-        in_specs=[smem(), smem()] + [vmem()] * 4,
-        out_specs=(vmem(),) * 2,
-        scratch_shapes=work,
-        compiler_params=params,
-        cost_estimate=cost(5),
-        name="rest",
-    )(iterations, reference_date, z, nr, ni, pack_x)
-
     more_y = lax.ppermute(pack_y, "space", pair_y)
     more_x = lax.ppermute(pack_x, "space", pair_x)
+
+    def rest(start, nr, ni, after):
+        vectors = nr.shape[1]
+
+        return pl.pallas_call(
+            lambda *refs: rest_kernel(start, *refs),
+            out_shape=(
+                shape(2, dates, vectors, SUB, LANES),
+                shape(2, vectors, SUB, LANES),
+            ),
+            in_specs=[smem()] * 2 + [vmem()] * 4,
+            out_specs=(vmem(),) * 2,
+            scratch_shapes=work,
+            compiler_params=params,
+            cost_estimate=cost(vectors),
+            name="rest",
+        )(iterations, reference_date, z, nr, ni, after)
+
+    start = HALF_ROWS + done
+    linked_c, comp_c = rest(start, nr_b, ni_b, pack_x)
+    start += middle
     wide = pl.pallas_call(
         extend_kernel,
-        out_shape=shape(2, ext, SUB, LANES),
-        in_specs=[smem()] + [vmem()] * 5,
+        out_shape=shape(2, 2 * HALF_ROWS + done, SUB, LANES),
+        in_specs=[smem()] + [vmem()] * 4,
         out_specs=vmem(),
         compiler_params=params,
         name="extend",
-    )(parity, comp_b, comp_a, comp_c, more_x, more_y)
-    other_a = lax.ppermute(wide, "tm", swaps(members))
-    other_b = lax.ppermute(wide, "tm", swaps(members, odd=True))
+    )(parity, comp_b, comp_a, more_x, more_y)
+    near, far = swaps(members), swaps(members, odd=True)
+    wide_b = lax.ppermute(wide, "tm", far)
+    wide_a = lax.ppermute(wide, "tm", near)
+    linked_d, comp_d = rest(start, nr_c, ni_c, wide)
+    narrow = pl.pallas_call(
+        gather_kernel,
+        out_shape=shape(2, half - HALF_ROWS - done, SUB, LANES),
+        in_specs=[vmem()] * 2,
+        out_specs=vmem(),
+        compiler_params=params,
+        name="gather",
+    )(comp_c, comp_d)
+    narrow_b = lax.ppermute(narrow, "tm", far)
+    narrow_a = lax.ppermute(narrow, "tm", near)
     where = jnp.stack([place, place % 2]).astype(jnp.int32)
     datum, total = pl.pallas_call(
         lambda *refs: offsets_kernel(tiles, *refs),
         out_shape=(shape(2, half, SUB, LANES), shape(2, half, SUB, LANES)),
-        in_specs=[smem(), vmem(), vmem(), vmem()],
+        in_specs=[smem()] + [vmem()] * 6,
         out_specs=(vmem(), vmem()),
         compiler_params=params,
         name="offsets",
-    )(where, wide, other_a, other_b)
+    )(where, wide, narrow, wide_a, narrow_a, wide_b, narrow_b)
     bit = 2
     while bit < members:
-        other = lax.ppermute(total, "tm", swaps(members, bit=bit))
+        other = lax.ppermute(total, "tm", swaps(members, bit=2 * bit - 2))
         datum = jnp.where((place & bit) != 0, times(datum, other), datum)
         total = times(total, other)
         bit *= 2
     out = pl.pallas_call(
         lambda *refs: result_kernel(rows, tiles, *refs),
         out_shape=shape(2, dates, rows * tiles, LANES),
-        in_specs=[vmem()] * 4,
+        in_specs=[vmem()] * 5,
         out_specs=vmem(),
         compiler_params=params,
         name="result",
-    )(linked_b, linked_a, linked_c, datum)
+    )(linked_b, linked_a, linked_c, linked_d, datum)
     out = out.reshape(2, dates, rows // SUB, tiles, SUB, LANES)
     return jnp.swapaxes(out, -3, -2).reshape(2, dates, rows, columns)
 
 
 def solution(mesh):
     return jax.shard_map(
-        local,
+        linked_phases,
         mesh=mesh,
         in_specs=(
             P("tm", "space", None),

time: 56.2 us -> 61 us (1.085)
  Pallas kernels: 20.7 us -> 32.6 us
  starting transfers between devices: 18.3 us -> 11.8 us
  local copies, waits for them, and re-layouts: 2.86 us -> 1.1 us
  waiting for transfers between devices: 12.5 us -> 13.6 us
    pallas_call x7 -> x9, Pallas kernels: 20.7 us -> 32.6 us  [the longest x2 10.3 us: rest(): pl.pallas_call(lambda *refs: rest_kernel(start, *refs), out_shape=(shape(...]
    ppermute x8 -> x10, starting transfers between devices: 18.3 us -> 11.8 us  [the longest x1 3.12 us: linked_phases(): wide_b = lax.ppermute(wide, 'tm', far)]
    unnamed x6 -> x4, local copies, waits for them, and re-layouts: 2.86 us -> 1.1 us
    ppermute x8 -> x10, waiting for transfers between devices: 12.5 us -> 13.6 us  [the longest x2 9.32 us: linked_phases(): other = lax.ppermute(total, 'tm', swaps(members, bit=2 * bit - 2))]
  transfers between devices with their start and end apart: 8 -> 10, of which waited for: 3 -> 4; matrix products, arithmetic and copies ran while one was open for 0% -> 0% of each run, Pallas kernels for 19% -> 18%
where the time goes in v3:
time: 61 us; the launch traced here: 60.8 us
  Pallas kernels  32.6 us (53%)
  waiting for transfers between devices  13.6 us (22%)
  starting transfers between devices  11.8 us (19%)
  between operations  1.47 us (2%)
  local copies, waits for them, and re-layouts  1.1 us (2%)
    pallas_call x2, Pallas kernels, rest(): pl.pallas_call(lambda *refs: rest_kernel(start, *refs), out_shape=(shape(...  10.3 us
    pallas_call x1, Pallas kernels, linked_phases(): pl.pallas_call(lambda *refs: outer_kernel(tiles, *refs), out_shape=(shape...  9.91 us
    ppermute x2, waiting for transfers between devices, linked_phases(): other = lax.ppermute(total, 'tm', swaps(members, bit=2 * bit - 2))  9.32 us
    pallas_call x1, Pallas kernels, linked_phases(): pl.pallas_call(lambda *refs: inner_kernel(tiles, done, *refs), out_shape=...  6.85 us
    ppermute x1, starting transfers between devices, linked_phases(): wide_b = lax.ppermute(wide, 'tm', far)  3.12 us
    pallas_call x1, Pallas kernels, linked_phases(): pl.pallas_call(lambda *refs: images_kernel(rows, tiles, *refs), out_shape...  2.72 us
    ppermute x1, starting transfers between devices, linked_phases(): got_y = lax.ppermute(slab_y, 'space', pair_y)  2.59 us
    ppermute x1, waiting for transfers between devices, linked_phases(): narrow_b = lax.ppermute(narrow, 'tm', far)  2.46 us
  transfers between devices with their start and end apart: 10, of which 4 were waited for; matrix products, arithmetic and copies ran while one was open for 0% of the time, Pallas kernels for 18%

profile of v3, /device:TPU:0, one launch (start us, length us, event | category | flops | bytes accessed | tf_op | source)
XLA Modules:
  0.0 60.8 jit_solution(5515841301789652570)
XLA Ops:
  0.0 0.1 pad_add_fusion.refs_0_.par_ref
  0.1 2.7 %images.1 = (f32[2,10,17,8,128]{4,3,2,1,0:T(8,128)S(1)}, f32[10,5,8,128]{3,2,1,0:T(8,128)S(1)}, f32[10,5,8,128]{3,2,1,0:T(8,128)S(1)}) custom-call(s32[2]{0:T(128)S(1)} %pad_add_fusion.refs_0_.par_ref, f32[10,96,128]{2,1,0:T(8,128)} %bitcast.24, f32[10,96,128]{2,1,0:T(8,128)} %bitcast.25, s32[96,128]{1,0:T(8,128)} %bitcast.26), custom_call_target="tpu_custom_call" | custom-call | tf_op jit(solution)/shard_map/images/pallas_call | solution.py:680
  2.8 0.0 copy-start
  2.8 1.1 %copy-done = f32[2,10,17,8,128]{4,3,2,1,0:T(8,128)} copy-done((f32[2,10,17,8,128]{4,3,2,1,0:T(8,128)}, f32[2,10,17,8,128]{4,3,2,1,0:T(8,128)S(1)}, u32[]{:S(2)}) %copy-start) | copy-done | bytes 1392664
  3.9 0.5 collective-permute-start
  4.4 2.6 %collective-permute-start.1 = (f32[10,5,8,128]{3,2,1,0:T(8,128)S(1)}, f32[10,5,8,128]{3,2,1,0:T(8,128)S(1)}, u32[]{:S(2)}, u32[]{:S(2)}) collective-permute-start(f32[10,5,8,128]{3,2,1,0:T(8,128)S(1)} %get-tuple-element.28), channel_id=1, source_target_pairs={{0,3},{1,2},{2,1},{3,0},{4,7},{5,6},{6,5},{7,4},{8,11},{9,10},{10,... | collective-permute-start | bytes 614408 | tf_op jit(solution)/shard_map/ppermute | solution.py:699
  8.3 6.9 %inner.1 = (f32[45,2,8,128]{3,2,1,0:T(8,128)S(1)}, f32[45,2,8,128]{3,2,1,0:T(8,128)S(1)}, f32[45,4,8,128]{3,2,1,0:T(8,128)S(1)}, f32[45,4,8,128]{3,2,1,0:T(8,128...) custom-call(s32[1]{0:T(128)S(6)} %copy.6.refs_0_.refs_1_, ...), custom_call_target="tpu_custom_call" | custom-call | flops 64000000 | bytes 1048576 | tf_op jit(solution)/shard_map/inner/pallas_call | solution.py:725
  15.1 0.0 collective-permute-done.refs_5_
  15.1 0.0 collective-permute-done.1.refs_6_
  15.1 9.9 %outer.1 = (f32[2,10,5,8,128]{4,3,2,1,0:T(8,128)S(1)}, f32[2,5,8,128]{3,2,1,0:T(8,128)S(1)}, f32[5,8,128]{2,1,0:T(8,128)S(1)}, f32[5,8,128]{2,1,0:T(8,128)S(1)}) custom-call(s32[2]{0:T(128)S(1)} %pad_add_fusion.refs_0_.par_ref, s32[1]{0:T(128)S(6)} %copy.6.refs_0_.refs_1_, s32[1]{0:T(128)S(6)} %copy.7.refs_1_.refs_2_, f32[2,10,17,8,128]{4,3,2,1,0:T(8,128)} %copy-done, ...), custom_call_target="tpu_custom_call" | custom-call | flops 112000000 | bytes 1048576 | tf_op jit(solution)/shard_map/outer/pallas_call | solution.py:745
  25.1 0.0 copy-start.1
  25.1 0.1 collective-permute-start.2
  25.2 0.1 collective-permute-start.3
  25.2 3.9 %rest.2 = (f32[2,10,2,8,128]{4,3,2,1,0:T(8,128)S(1)}, f32[2,2,8,128]{3,2,1,0:T(8,128)S(1)}) custom-call(s32[1]{0:T(128)S(6)} %copy.6.refs_0_.refs_1_, s32[1]{0:T(128)S(6)} %copy.7.refs_1_.refs_2_, f32[2,10,17,8,128]{4,3,2,1,0:T(8,128)} %copy-done, f32[45,2,8,128]{3,2,1,0:T(8,128)S(1)} %get-tuple-element.31.refs_3_, ...), custom_call_target="tpu_custom_call" | custom-call | flops 32000000 | bytes 1048576 | tf_op jit(solution)/shard_map/rest/pallas_call | solution.py:772
  29.2 0.0 collective-permute-done.2.x_ref
  29.2 0.0 collective-permute-done.3.y_ref
  29.2 0.6 extend.1.refs_5_.refs_1_
  29.7 0.0 copy-done.1
  29.7 6.4 %rest.3 = (f32[2,10,4,8,128]{4,3,2,1,0:T(8,128)S(1)}, f32[2,4,8,128]{3,2,1,0:T(8,128)S(1)}) custom-call(s32[1]{0:T(128)S(6)} %copy.6.refs_0_.refs_1_, s32[1]{0:T(128)S(6)} %copy.7.refs_1_.refs_2_, f32[2,10,17,8,128]{4,3,2,1,0:T(8,128)} %copy-done, f32[45,4,8,128]{3,2,1,0:T(8,128)S(1)} %get-tuple-element.35.refs_3_, f32[45,4,8,128]{3,2,1,0:T(8,128)S(1)} %copy-done.1, ...), custom_call_target="tpu_custom_call" | custom-call | flops 64000000 | bytes 1048576 | tf_op jit(solution)/shard_map/rest/pallas_call | solution.py:772
  36.2 2.1 %collective-permute-start.5 = (f32[2,6,8,128]{3,2,1,0:T(8,128)S(1)}, f32[2,6,8,128]{3,2,1,0:T(8,128)S(1)}, u32[]{:S(2)}, u32[]{:S(2)}) collective-permute-start(f32[2,6,8,128]{3,2,1,0:T(8,128)S(1)} %gather.1.refs_2_), channel_id=1, source_target_pairs={{0,4},{4,0},{8,12},{12,8},{16,20},{20,16},{24,28},{28,24},{1,5},{5... | collective-permute-start | bytes 147464 | tf_op jit(solution)/shard_map/ppermute | solution.py:810
  38.3 1.6 %collective-permute-start.7 = (f32[2,6,8,128]{3,2,1,0:T(8,128)S(1)}, f32[2,6,8,128]{3,2,1,0:T(8,128)S(1)}, u32[]{:S(2)}, u32[]{:S(2)}) collective-permute-start(f32[2,6,8,128]{3,2,1,0:T(8,128)S(1)} %gather.1.refs_2_), channel_id=1, source_target_pairs={{0,28},{4,8},{8,4},{12,16},{16,12},{20,24},{24,20},{28,0},{1,29},{... | collective-permute-start | bytes 147464 | tf_op jit(solution)/shard_map/ppermute | solution.py:809
  39.9 0.0 collective-permute-start.4
  39.9 3.1 %collective-permute-start.6 = (f32[2,11,8,128]{3,2,1,0:T(8,128)S(1)}, f32[2,11,8,128]{3,2,1,0:T(8,128)S(1)}, u32[]{:S(2)}, u32[]{:S(2)}) collective-permute-start(f32[2,11,8,128]{3,2,1,0:T(8,128)S(1)} %extend.1.refs_5_.refs_1_), channel_id=1, source_target_pairs={{0,28},{4,8},{8,4},{12,16},{16,12},{20,24},{24,20},{28,0},{1,29},{... | collective-permute-start | bytes 270344 | tf_op jit(solution)/shard_map/ppermute | solution.py:798
  43.0 0.1 pad_add_fusion.1.refs_0_
  43.1 0.0 collective-permute-done.5.refs_4_
  43.1 2.5 %collective-permute-done.7.refs_6_ = f32[2,6,8,128]{3,2,1,0:T(8,128)S(1)} collective-permute-done((f32[2,6,8,128]{3,2,1,0:T(8,128)S(1)}, f32[2,6,8,128]{3,2,1,0:T(8,128)S(1)}, u32[]{:S(2)}, u32[]{:S(2)}) %collective-permute-start.7) | collective-permute-done | bytes 49184 | tf_op jit(solution)/shard_map/ppermute | solution.py:809
  45.5 1.8 %collective-permute-done.4.refs_3_ = f32[2,11,8,128]{3,2,1,0:T(8,128)S(1)} collective-permute-done((f32[2,11,8,128]{3,2,1,0:T(8,128)S(1)}, f32[2,11,8,128]{3,2,1,0:T(8,128)S(1)}, u32[]{:S(2)}, u32[]{:S(2)}) %collective-permute-start.4) | collective-permute-done | bytes 90144 | tf_op jit(solution)/shard_map/ppermute | solution.py:799
  47.3 0.0 collective-permute-done.6.refs_5_
  47.3 1.0 %offsets.1 = (f32[2,12,8,128]{3,2,1,0:T(8,128)S(1)}, f32[2,12,8,128]{3,2,1,0:T(8,128)S(1)}) custom-call(s32[2]{0:T(128)S(1)} %pad_add_fusion.1.refs_0_, f32[2,11,8,128]{3,2,1,0:T(8,128)S(1)} %extend.1.refs_5_.refs_1_, f32[2,6,8,128]{3,2,1,0:T(8,128)S(1)} %gather.1.refs_2_, f32[2,11,8,128]{3,2,1,0:T(8,128)S(1)} %collective-permute-done.4.refs_3_, ...), custom_call_target="tpu_custom_call" | custom-call | tf_op jit(solution)/shard_map/offsets/pallas_call | solution.py:812
  48.3 0.1 collective-permute-start.8
  48.4 4.6 %collective-permute-done.8 = f32[2,12,8,128]{3,2,1,0:T(8,128)S(1)} collective-permute-done((f32[2,12,8,128]{3,2,1,0:T(8,128)S(1)}, f32[2,12,8,128]{3,2,1,0:T(8,128)S(1)}, u32[]{:S(2)}, u32[]{:S(2)}) %collective-permute-start.8) | collective-permute-done | bytes 98336 | tf_op jit(solution)/shard_map/ppermute | solution.py:822
  53.1 1.7 %collective-permute-start.9 = (f32[2,12,8,128]{3,2,1,0:T(8,128)S(1)}, f32[2,12,8,128]{3,2,1,0:T(8,128)S(1)}, u32[]{:S(2)}, u32[]{:S(2)}) collective-permute-start(f32[2,12,8,128]{3,2,1,0:T(8,128)S(1)} %pad_maximum_fusion), channel_id=1, source_target_pairs={{0,24},{4,28},{8,16},{12,20},{16,8},{20,12},{24,0},{28,4},{1,25},{... | collective-permute-start | bytes 294920 | tf_op jit(solution)/shard_map/ppermute | solution.py:822
  54.8 4.7 %collective-permute-done.9 = f32[2,12,8,128]{3,2,1,0:T(8,128)S(1)} collective-permute-done((f32[2,12,8,128]{3,2,1,0:T(8,128)S(1)}, f32[2,12,8,128]{3,2,1,0:T(8,128)S(1)}, u32[]{:S(2)}, u32[]{:S(2)}) %collective-permute-start.9) | collective-permute-done | bytes 98336 | tf_op jit(solution)/shard_map/ppermute | solution.py:822
  59.6 1.2 %result.1 = f32[2,10,96,128]{3,2,1,0:T(8,128)} custom-call(f32[2,10,5,8,128]{4,3,2,1,0:T(8,128)S(1)} %get-tuple-element.29.refs_0_, f32[2,10,1,8,128]{4,3,2,1,0:T(8,128)S(1)} %get-tuple-element.30.refs_1_, f32[2,10,2,8,128]{4,3,2,1,0:T(8,128)S(1)} %get-tuple-element.34.refs_2_, f32[2,10,4,8,128]{4,3,2,1,0:T(8,128)S(1)} %get-tuple-element.40.refs_3_, ...), custom_call_target="tpu_custom_call" | custom-call | tf_op jit(solution)/shard_map/result/pallas_call | solution.py:826
  (6 shorter events, 0.1 us)
Async XLA Ops:
  2.8 1.1 %copy-start = (f32[2,10,17,8,128]{4,3,2,1,0:T(8,128)}, f32[2,10,17,8,128]{4,3,2,1,0:T(8,128)S(1)}, u32[]{:S(2)}) copy-start(f32[2,10,17,8,128]{4,3,2,1,0:T(8,128)S(1)} %get-tuple-element.25.refs_2_.refs_3_) | copy-start | bytes 4177924
  3.9 11.2 %collective-permute-start = (f32[10,5,8,128]{3,2,1,0:T(8,128)S(1)}, f32[10,5,8,128]{3,2,1,0:T(8,128)S(1)}, u32[]{:S(2)}, u32[]{:S(2)}) collective-permute-start(f32[10,5,8,128]{3,2,1,0:T(8,128)S(1)} %get-tuple-element.27), channel_id=1, source_target_pairs={{0,1},{1,0},{2,3},{3,2},{4,5},{5,4},{6,7},{7,6},{8,9},{9,8},{10,11... | collective-permute-start | bytes 614408 | tf_op jit(solution)/shard_map/ppermute | solution.py:700
  4.4 10.7 %collective-permute-start.1 = (f32[10,5,8,128]{3,2,1,0:T(8,128)S(1)}, f32[10,5,8,128]{3,2,1,0:T(8,128)S(1)}, u32[]{:S(2)}, u32[]{:S(2)}) collective-permute-start(f32[10,5,8,128]{3,2,1,0:T(8,128)S(1)} %get-tuple-element.28), channel_id=1, source_target_pairs={{0,3},{1,2},{2,1},{3,0},{4,7},{5,6},{6,5},{7,4},{8,11},{9,10},{10,... | collective-permute-start | bytes 614408 | tf_op jit(solution)/shard_map/ppermute | solution.py:699
  25.1 4.7 %copy-start.1 = (f32[45,4,8,128]{3,2,1,0:T(8,128)S(1)}, f32[45,4,8,128]{3,2,1,0:T(8,128)}, u32[]{:S(2)}) copy-start(f32[45,4,8,128]{3,2,1,0:T(8,128)} %get-tuple-element.36.refs_4_) | copy-start | bytes 2211844
  25.1 4.1 %collective-permute-start.2 = (f32[5,8,128]{2,1,0:T(8,128)S(1)}, f32[5,8,128]{2,1,0:T(8,128)S(1)}, u32[]{:S(2)}, u32[]{:S(2)}) collective-permute-start(f32[5,8,128]{2,1,0:T(8,128)S(1)} %get-tuple-element.33.refs_5_), channel_id=1, source_target_pairs={{0,1},{1,0},{2,3},{3,2},{4,5},{5,4},{6,7},{7,6},{8,9},{9,8},{10,11... | collective-permute-start | bytes 61448 | tf_op jit(solution)/shard_map/ppermute | solution.py:767
  25.2 4.0 %collective-permute-start.3 = (f32[5,8,128]{2,1,0:T(8,128)S(1)}, f32[5,8,128]{2,1,0:T(8,128)S(1)}, u32[]{:S(2)}, u32[]{:S(2)}) collective-permute-start(f32[5,8,128]{2,1,0:T(8,128)S(1)} %get-tuple-element.39), channel_id=1, source_target_pairs={{0,3},{1,2},{2,1},{3,0},{4,7},{5,6},{6,5},{7,4},{8,11},{9,10},{10,... | collective-permute-start | bytes 61448 | tf_op jit(solution)/shard_map/ppermute | solution.py:766
  36.2 6.9 %collective-permute-start.5 = (f32[2,6,8,128]{3,2,1,0:T(8,128)S(1)}, f32[2,6,8,128]{3,2,1,0:T(8,128)S(1)}, u32[]{:S(2)}, u32[]{:S(2)}) collective-permute-start(f32[2,6,8,128]{3,2,1,0:T(8,128)S(1)} %gather.1.refs_2_), channel_id=1, source_target_pairs={{0,4},{4,0},{8,12},{12,8},{16,20},{20,16},{24,28},{28,24},{1,5},{5... | collective-permute-start | bytes 147464 | tf_op jit(solution)/shard_map/ppermute | solution.py:810
  38.3 7.3 %collective-permute-start.7 = (f32[2,6,8,128]{3,2,1,0:T(8,128)S(1)}, f32[2,6,8,128]{3,2,1,0:T(8,128)S(1)}, u32[]{:S(2)}, u32[]{:S(2)}) collective-permute-start(f32[2,6,8,128]{3,2,1,0:T(8,128)S(1)} %gather.1.refs_2_), channel_id=1, source_target_pairs={{0,28},{4,8},{8,4},{12,16},{16,12},{20,24},{24,20},{28,0},{1,29},{... | collective-permute-start | bytes 147464 | tf_op jit(solution)/shard_map/ppermute | solution.py:809
  39.9 7.4 %collective-permute-start.4 = (f32[2,11,8,128]{3,2,1,0:T(8,128)S(1)}, f32[2,11,8,128]{3,2,1,0:T(8,128)S(1)}, u32[]{:S(2)}, u32[]{:S(2)}) collective-permute-start(f32[2,11,8,128]{3,2,1,0:T(8,128)S(1)} %extend.1.refs_5_.refs_1_), channel_id=1, source_target_pairs={{0,4},{4,0},{8,12},{12,8},{16,20},{20,16},{24,28},{28,24},{1,5},{5... | collective-permute-start | bytes 270344 | tf_op jit(solution)/shard_map/ppermute | solution.py:799
  39.9 7.4 %collective-permute-start.6 = (f32[2,11,8,128]{3,2,1,0:T(8,128)S(1)}, f32[2,11,8,128]{3,2,1,0:T(8,128)S(1)}, u32[]{:S(2)}, u32[]{:S(2)}) collective-permute-start(f32[2,11,8,128]{3,2,1,0:T(8,128)S(1)} %extend.1.refs_5_.refs_1_), channel_id=1, source_target_pairs={{0,28},{4,8},{8,4},{12,16},{16,12},{20,24},{24,20},{28,0},{1,29},{... | collective-permute-start | bytes 270344 | tf_op jit(solution)/shard_map/ppermute | solution.py:798
  48.3 4.7 %collective-permute-start.8 = (f32[2,12,8,128]{3,2,1,0:T(8,128)S(1)}, f32[2,12,8,128]{3,2,1,0:T(8,128)S(1)}, u32[]{:S(2)}, u32[]{:S(2)}) collective-permute-start(f32[2,12,8,128]{3,2,1,0:T(8,128)S(1)} %get-tuple-element.44), channel_id=1, source_target_pairs={{0,8},{4,12},{8,0},{12,4},{16,24},{20,28},{24,16},{28,20},{1,9},{5... | collective-permute-start | bytes 294920 | tf_op jit(solution)/shard_map/ppermute | solution.py:822
  53.1 6.5 %collective-permute-start.9 = (f32[2,12,8,128]{3,2,1,0:T(8,128)S(1)}, f32[2,12,8,128]{3,2,1,0:T(8,128)S(1)}, u32[]{:S(2)}, u32[]{:S(2)}) collective-permute-start(f32[2,12,8,128]{3,2,1,0:T(8,128)S(1)} %pad_maximum_fusion), channel_id=1, source_target_pairs={{0,24},{4,28},{8,16},{12,20},{16,8},{20,12},{24,0},{28,4},{1,25},{... | collective-permute-start | bytes 294920 | tf_op jit(solution)/shard_map/ppermute | solution.py:822

commit v4 on v3

--- a/solution.py
+++ b/solution.py
@@ -5,11 +5,9 @@
 from jax.experimental.pallas import tpu as pltpu
 from jax.sharding import PartitionSpec as P
 
-
 WIN_ROWS = 11
 WIN_COLS = 5
-INNER_DONE = 1
-MIDDLE = 2
+INNER_DONE = 2
 PIECE = 5
 ITERS = 20
 HALF_ROWS = WIN_ROWS // 2
@@ -19,7 +17,7 @@
 
 LANES = 128
 SUB = 8
-VMEM_LIMIT = 52 * 1024 * 1024
+VMEM_LIMIT = 40 * 1024 * 1024
 
 
 def vmem():
@@ -411,13 +409,13 @@
 
 def inner_kernel(
     tiles, done, iter_ref, chosen_ref, z_ref,
-    nr_b, ni_b, nr_c, ni_c, part_ref, link_ref, comp_ref,
+    nr_b, ni_b, part_ref, link_ref, comp_ref,
     band, split, inv, nr_a, ni_a, more, sq, vec,
 ):
     dates = z_ref.shape[1]
     places = [
         (nr, ni, k)
-        for nr, ni in ((nr_a, ni_a), (nr_b, ni_b), (nr_c, ni_c))
+        for nr, ni in ((nr_a, ni_a), (nr_b, ni_b))
         for k in range(nr.shape[1])
     ]
     vectors = len(places)
@@ -541,7 +539,7 @@
     return lanes, (column != 0, column != tiles - 1)
 
 
-def extend_kernel(par_ref, outer_ref, inner_ref, x_ref, y_ref, out_ref):
+def extend_kernel(par_ref, outer_ref, inner_ref, rest_ref, x_ref, y_ref, out_ref):
     top = upper()
     odd_device = par_ref[0] == 1
     edge = par_ref[1] == 1
@@ -552,23 +550,14 @@
         out_ref[1, HALF_ROWS - 1 - k] = im
     for part in range(2):
         at = HALF_ROWS
-        for ref in (outer_ref, inner_ref):
+        for ref in (outer_ref, inner_ref, rest_ref):
             for k in range(ref.shape[1]):
                 out_ref[part, at] = ref[part, k]
                 at += 1
 
 
-def gather_kernel(first_ref, second_ref, out_ref):
-    for part in range(2):
-        at = 0
-        for ref in (first_ref, second_ref):
-            for k in range(ref.shape[1]):
-                out_ref[part, at] = ref[part, k]
-                at += 1
-
-
 def offsets_kernel(
-    tiles, place_ref, own_w, own_n, a_w, a_n, b_w, b_n, unit_ref, total_ref
+    tiles, place_ref, own_ref, a_ref, b_ref, unit_ref, total_ref
 ):
     lanes, edges = masks(tiles)
     half = unit_ref.shape[1]
@@ -586,7 +575,7 @@
     def power(re, im):
         return box_sum([a * a + b * b for a, b in zip(re, im)], lanes, edges)
 
-    own_r, own_i = whole(own_w, own_n)
+    own_r, own_i = whole(own_ref)
     own = [p + 1.0 for p in power(own_r, own_i)]
 
     def unit(*refs):
@@ -607,7 +596,7 @@
             out.append((off_r * back, off_i * back))
         return out
 
-    pair_a, pair_b = unit(a_w, a_n), unit(b_w, b_n)
+    pair_a, pair_b = unit(a_ref), unit(b_ref)
     for k in range(half):
         (ar, ai), (br, bi) = pair_a[k], pair_b[k]
         before_r = jnp.where(odd_stack, ar, br)
@@ -622,9 +611,9 @@
         total_ref[1, k] = before_r * after_i + before_i * after_r
 
 
-def result_kernel(rows, tiles, outer_ref, inner_ref, middle_ref, last_ref, datum_ref, out_ref):
+def result_kernel(rows, tiles, outer_ref, inner_ref, rest_ref, datum_ref, out_ref):
     half = rows // 2
-    parts = (outer_ref, inner_ref, middle_ref, last_ref)
+    parts = (outer_ref, inner_ref, rest_ref)
     links = [(ref, k) for ref in parts for k in range(ref.shape[2])]
 
     def one_date(t, carry):
@@ -649,11 +638,16 @@
     return [(i, i ^ 1) for i in range(count)]
 
 
+def inner_swaps(count):
+    pairs = [(i, i + 1) for i in range(1, count - 1, 2)]
+    return pairs + [(j, i) for i, j in pairs]
+
+
 def times(a, b):
     return jnp.stack([a[0] * b[0] - a[1] * b[1], a[0] * b[1] + a[1] * b[0]])
 
 
-def linked_phases(amplitude, phase, validity, iterations, reference_date):
+def local(amplitude, phase, validity, iterations, reference_date):
     dates, rows, columns = amplitude.shape
     half = rows // 2
     tiles = columns // LANES
@@ -720,21 +714,17 @@
             flops=vectors * 2_000_000 * 8, bytes_accessed=1 << 20, transcendentals=0
         )
 
-    middle = min(MIDDLE, inner - done - 1)
-    last = inner - done - middle
-    nr_b, ni_b, nr_c, ni_c, part, linked_a, comp_a = pl.pallas_call(
+    nr, ni, part, linked_a, comp_a = pl.pallas_call(
         lambda *refs: inner_kernel(tiles, done, *refs),
         out_shape=(
-            shape(count, middle, SUB, LANES),
-            shape(count, middle, SUB, LANES),
-            shape(count, last, SUB, LANES),
-            shape(count, last, SUB, LANES),
+            shape(count, inner - done, SUB, LANES),
+            shape(count, inner - done, SUB, LANES),
             shape(2 * count + dates, HALF_ROWS, SUB, LANES),
             shape(2, dates, done, SUB, LANES),
             shape(2, done, SUB, LANES),
         ),
         in_specs=[smem(), smem(), vmem()],
-        out_specs=(vmem(),) * 7,
+        out_specs=(vmem(),) * 5,
         scratch_shapes=window_work(inner)
         + [pltpu.VMEM((count, done, SUB, LANES), jnp.float32)] * 2
         + work,
@@ -766,57 +756,39 @@
     more_y = lax.ppermute(pack_y, "space", pair_y)
     more_x = lax.ppermute(pack_x, "space", pair_x)
 
-    def rest(start, nr, ni, after):
-        vectors = nr.shape[1]
-
-        return pl.pallas_call(
-            lambda *refs: rest_kernel(start, *refs),
-            out_shape=(
-                shape(2, dates, vectors, SUB, LANES),
-                shape(2, vectors, SUB, LANES),
-            ),
-            in_specs=[smem()] * 2 + [vmem()] * 4,
-            out_specs=(vmem(),) * 2,
-            scratch_shapes=work,
-            compiler_params=params,
-            cost_estimate=cost(vectors),
-            name="rest",
-        )(iterations, reference_date, z, nr, ni, after)
-
     start = HALF_ROWS + done
-    linked_c, comp_c = rest(start, nr_b, ni_b, pack_x)
-    start += middle
+    linked_c, comp_c = pl.pallas_call(
+        lambda *refs: rest_kernel(start, *refs),
+        out_shape=(
+            shape(2, dates, half - start, SUB, LANES),
+            shape(2, half - start, SUB, LANES),
+        ),
+        in_specs=[smem()] * 2 + [vmem()] * 4,
+        out_specs=(vmem(),) * 2,
+        scratch_shapes=work,
+        compiler_params=params,
+        cost_estimate=cost(5),
+        name="rest",
+    )(iterations, reference_date, z, nr, ni, pack_x)
     wide = pl.pallas_call(
         extend_kernel,
-        out_shape=shape(2, 2 * HALF_ROWS + done, SUB, LANES),
-        in_specs=[smem()] + [vmem()] * 4,
+        out_shape=shape(2, ext, SUB, LANES),
+        in_specs=[smem()] + [vmem()] * 5,
         out_specs=vmem(),
         compiler_params=params,
         name="extend",
-    )(parity, comp_b, comp_a, more_x, more_y)
-    near, far = swaps(members), swaps(members, odd=True)
-    wide_b = lax.ppermute(wide, "tm", far)
-    wide_a = lax.ppermute(wide, "tm", near)
-    linked_d, comp_d = rest(start, nr_c, ni_c, wide)
-    narrow = pl.pallas_call(
-        gather_kernel,
-        out_shape=shape(2, half - HALF_ROWS - done, SUB, LANES),
-        in_specs=[vmem()] * 2,
-        out_specs=vmem(),
-        compiler_params=params,
-        name="gather",
-    )(comp_c, comp_d)
-    narrow_b = lax.ppermute(narrow, "tm", far)
-    narrow_a = lax.ppermute(narrow, "tm", near)
+    )(parity, comp_b, comp_a, comp_c, more_x, more_y)
+    other_a = lax.ppermute(wide, "tm", swaps(members))
+    other_b = lax.ppermute(wide, "tm", inner_swaps(members))
     where = jnp.stack([place, place % 2]).astype(jnp.int32)
     datum, total = pl.pallas_call(
         lambda *refs: offsets_kernel(tiles, *refs),
         out_shape=(shape(2, half, SUB, LANES), shape(2, half, SUB, LANES)),
-        in_specs=[smem()] + [vmem()] * 6,
+        in_specs=[smem()] + [vmem()] * 3,
         out_specs=(vmem(), vmem()),
         compiler_params=params,
         name="offsets",
-    )(where, wide, narrow, wide_a, narrow_a, wide_b, narrow_b)
+    )(where, wide, other_a, other_b)
     bit = 2
     while bit < members:
         other = lax.ppermute(total, "tm", swaps(members, bit=2 * bit - 2))
@@ -826,18 +798,18 @@
     out = pl.pallas_call(
         lambda *refs: result_kernel(rows, tiles, *refs),
         out_shape=shape(2, dates, rows * tiles, LANES),
-        in_specs=[vmem()] * 5,
+        in_specs=[vmem()] * 4,
         out_specs=vmem(),
         compiler_params=params,
         name="result",
-    )(linked_b, linked_a, linked_c, linked_d, datum)
+    )(linked_b, linked_a, linked_c, datum)
     out = out.reshape(2, dates, rows // SUB, tiles, SUB, LANES)
     return jnp.swapaxes(out, -3, -2).reshape(2, dates, rows, columns)
 
 
 def solution(mesh):
     return jax.shard_map(
-        linked_phases,
+        local,
         mesh=mesh,
         in_specs=(
             P("tm", "space", None),

time: 61 us -> 51.6 us (0.85)
  Pallas kernels: 32.6 us -> 20.9 us
  starting transfers between devices: 11.8 us -> 20.8 us
  waiting for transfers between devices: 13.6 us -> 8.62 us
  local copies, waits for them, and re-layouts: 1.1 us -> 0 us
    pallas_call x9 -> x7, Pallas kernels: 32.6 us -> 20.9 us  [the longest x1 6.48 us: local(): pl.pallas_call(lambda *refs: outer_kernel(tiles, *refs), out_shape=(shape...]
    ppermute x10 -> x8, starting transfers between devices: 11.8 us -> 20.8 us  [the longest x2 12.7 us: local(): other = lax.ppermute(total, 'tm', swaps(members, bit=2 * bit - 2))]
    ppermute x10 -> x8, waiting for transfers between devices: 13.6 us -> 8.62 us  [the longest x2 5.28 us: local(): other = lax.ppermute(total, 'tm', swaps(members, bit=2 * bit - 2))]
    unnamed x4 -> x0, local copies, waits for them, and re-layouts: 1.1 us -> none
  transfers between devices with their start and end apart: 10 -> 8, of which waited for: 4 -> 3; matrix products, arithmetic and copies ran while one was open for 0% -> 0% of each run, Pallas kernels for 18% -> 17%
where the time goes in v4:
time: 51.6 us; the launch traced here: 52 us
  Pallas kernels  20.9 us (41%)
  starting transfers between devices  20.8 us (40%)
  waiting for transfers between devices  8.62 us (17%)
  between operations  1.42 us (3%)
    ppermute x2, starting transfers between devices, local(): other = lax.ppermute(total, 'tm', swaps(members, bit=2 * bit - 2))  12.7 us
    pallas_call x1, Pallas kernels, local(): pl.pallas_call(lambda *refs: outer_kernel(tiles, *refs), out_shape=(shape...  6.48 us
    ppermute x2, waiting for transfers between devices, local(): other = lax.ppermute(total, 'tm', swaps(members, bit=2 * bit - 2))  5.28 us
    pallas_call x1, Pallas kernels, local(): pl.pallas_call(lambda *refs: inner_kernel(tiles, done, *refs), out_shape=...  4.72 us
    pallas_call x1, Pallas kernels, local(): pl.pallas_call(lambda *refs: rest_kernel(start, *refs), out_shape=(shape(...  4.19 us
    ppermute x1, starting transfers between devices, local(): other_a = lax.ppermute(wide, 'tm', swaps(members))  3.41 us
    ppermute x1, waiting for transfers between devices, local(): other_a = lax.ppermute(wide, 'tm', swaps(members))  3.33 us
    pallas_call x1, Pallas kernels, local(): pl.pallas_call(lambda *refs: images_kernel(rows, tiles, *refs), out_shape...  2.72 us
  transfers between devices with their start and end apart: 8, of which 3 were waited for; matrix products, arithmetic and copies ran while one was open for 0% of the time, Pallas kernels for 17%

profile of v4, /device:TPU:0, one launch (start us, length us, event | category | flops | bytes accessed | tf_op | source)
XLA Modules:
  0.0 52.0 jit_solution(4685236507354206342)
XLA Ops:
  0.0 0.1 pad_add_fusion.refs_0_.par_ref
  0.1 2.7 %images.1 = (f32[2,10,17,8,128]{4,3,2,1,0:T(8,128)S(1)}, f32[10,5,8,128]{3,2,1,0:T(8,128)S(1)}, f32[10,5,8,128]{3,2,1,0:T(8,128)S(1)}) custom-call(s32[2]{0:T(128)S(1)} %pad_add_fusion.refs_0_.par_ref, f32[10,96,128]{2,1,0:T(8,128)} %bitcast.24, f32[10,96,128]{2,1,0:T(8,128)} %bitcast.25, s32[96,128]{1,0:T(8,128)} %bitcast.26), custom_call_target="tpu_custom_call" | custom-call | tf_op jit(solution)/shard_map/images/pallas_call | solution.py:674
  2.8 0.6 %collective-permute-start = (f32[10,5,8,128]{3,2,1,0:T(8,128)S(1)}, f32[10,5,8,128]{3,2,1,0:T(8,128)S(1)}, u32[]{:S(2)}, u32[]{:S(2)}) collective-permute-start(f32[10,5,8,128]{3,2,1,0:T(8,128)S(1)} %get-tuple-element.23), channel_id=1, source_target_pairs={{0,1},{1,0},{2,3},{3,2},{4,5},{5,4},{6,7},{7,6},{8,9},{9,8},{10,11... | collective-permute-start | bytes 614408 | tf_op jit(solution)/shard_map/ppermute | solution.py:694
  3.4 2.6 %collective-permute-start.1 = (f32[10,5,8,128]{3,2,1,0:T(8,128)S(1)}, f32[10,5,8,128]{3,2,1,0:T(8,128)S(1)}, u32[]{:S(2)}, u32[]{:S(2)}) collective-permute-start(f32[10,5,8,128]{3,2,1,0:T(8,128)S(1)} %get-tuple-element.24), channel_id=1, source_target_pairs={{0,3},{1,2},{2,1},{3,0},{4,7},{5,6},{6,5},{7,4},{8,11},{9,10},{10,... | collective-permute-start | bytes 614408 | tf_op jit(solution)/shard_map/ppermute | solution.py:693
  7.3 4.7 %inner.1 = (f32[45,5,8,128]{3,2,1,0:T(8,128)S(1)}, f32[45,5,8,128]{3,2,1,0:T(8,128)S(1)}, f32[100,5,8,128]{3,2,1,0:T(8,128)S(1)}, f32[2,10,2,8,128]{4,3,2,1,0:T(8,128)S(1)}, f32[2,2,8,128]{3,2,1,0:T(8,128)S(1)}) custom-call(s32[1]{0:T(128)S(6)} %copy.6.refs_0_.refs_1_, s32[1]{0:T(128)S(6)} %copy.7.refs_1_.refs_2_, ...), custom_call_target="tpu_custom_call" | custom-call | flops 64000000 | bytes 1048576 | tf_op jit(solution)/shard_map/inner/pallas_call | solution.py:717
  12.0 0.0 collective-permute-done.refs_5_
  12.0 0.0 collective-permute-done.1.refs_6_
  12.0 6.5 %outer.1 = (f32[2,10,5,8,128]{4,3,2,1,0:T(8,128)S(1)}, f32[2,5,8,128]{3,2,1,0:T(8,128)S(1)}, f32[5,8,128]{2,1,0:T(8,128)S(1)}, f32[5,8,128]{2,1,0:T(8,128)S(1)}) custom-call(s32[2]{0:T(128)S(1)} %pad_add_fusion.refs_0_.par_ref, s32[1]{0:T(128)S(6)} %copy.6.refs_0_.refs_1_, s32[1]{0:T(128)S(6)} %copy.7.refs_1_.refs_2_, ...), custom_call_target="tpu_custom_call" | custom-call | flops 112000000 | bytes 1048576 | tf_op jit(solution)/shard_map/outer/pallas_call | solution.py:735
  18.5 0.1 collective-permute-start.2
  18.6 0.7 %collective-permute-start.3 = (f32[5,8,128]{2,1,0:T(8,128)S(1)}, f32[5,8,128]{2,1,0:T(8,128)S(1)}, u32[]{:S(2)}, u32[]{:S(2)}) collective-permute-start(f32[5,8,128]{2,1,0:T(8,128)S(1)} %get-tuple-element.34), channel_id=1, source_target_pairs={{0,3},{1,2},{2,1},{3,0},{4,7},{5,6},{6,5},{7,4},{8,11},{9,10},{10,... | collective-permute-start | bytes 61448 | tf_op jit(solution)/shard_map/ppermute | solution.py:756
  19.3 4.2 %rest.1 = (f32[2,10,5,8,128]{4,3,2,1,0:T(8,128)S(1)}, f32[2,5,8,128]{3,2,1,0:T(8,128)S(1)}) custom-call(s32[1]{0:T(128)S(6)} %copy.6.refs_0_.refs_1_, s32[1]{0:T(128)S(6)} %copy.7.refs_1_.refs_2_, f32[2,10,17,8,128]{4,3,2,1,0:T(8,128)S(1)} %get-tuple-element.21.refs_2_.refs_3_, f32[45,5,8,128]{3,2,1,0:T(8,128)S(1)} %get-tuple-element.27.refs_3_, ...), custom_call_target="tpu_custom_call" | custom-call | flops 80000000 | bytes 1048576 | tf_op jit(solution)/shard_map/rest/pallas_call | solution.py:760
  23.5 0.0 collective-permute-done.2.x_ref
  23.5 0.0 collective-permute-done.3.y_ref
  23.6 0.6 %extend.1.refs_1_ = f32[2,17,8,128]{3,2,1,0:T(8,128)S(1)} custom-call(s32[2]{0:T(128)S(1)} %pad_add_fusion.refs_0_.par_ref, f32[2,5,8,128]{3,2,1,0:T(8,128)S(1)} %get-tuple-element.31.outer_ref, f32[2,2,8,128]{3,2,1,0:T(8,128)S(1)} %get-tuple-element.32.inner_ref, f32[2,5,8,128]{3,2,1,0:T(8,128)S(1)} %get-tuple-element.33.rest_ref, ...), custom_call_target="tpu_custom_call" | custom-call | tf_op jit(solution)/shard_map/extend/pallas_call | solution.py:773
  24.1 3.4 %collective-permute-start.4 = (f32[2,17,8,128]{3,2,1,0:T(8,128)S(1)}, f32[2,17,8,128]{3,2,1,0:T(8,128)S(1)}, u32[]{:S(2)}, u32[]{:S(2)}) collective-permute-start(f32[2,17,8,128]{3,2,1,0:T(8,128)S(1)} %extend.1.refs_1_), channel_id=1, source_target_pairs={{0,4},{4,0},{8,12},{12,8},{16,20},{20,16},{24,28},{28,24},{1,5},{5... | collective-permute-start | bytes 417800 | tf_op jit(solution)/shard_map/ppermute | solution.py:781
  27.5 0.7 %collective-permute-start.5 = (f32[2,17,8,128]{3,2,1,0:T(8,128)S(1)}, f32[2,17,8,128]{3,2,1,0:T(8,128)S(1)}, u32[]{:S(2)}, u32[]{:S(2)}) collective-permute-start(f32[2,17,8,128]{3,2,1,0:T(8,128)S(1)} %extend.1.refs_1_), channel_id=1, source_target_pairs={{4,8},{12,16},{20,24},{8,4},{16,12},{24,20},{5,9},{13,17},{21,25},... | collective-permute-start | bytes 417800 | tf_op jit(solution)/shard_map/ppermute | solution.py:782
  28.2 0.1 pad_add_fusion.1.refs_0_
  28.3 3.3 %collective-permute-done.4.refs_2_ = f32[2,17,8,128]{3,2,1,0:T(8,128)S(1)} collective-permute-done((f32[2,17,8,128]{3,2,1,0:T(8,128)S(1)}, f32[2,17,8,128]{3,2,1,0:T(8,128)S(1)}, u32[]{:S(2)}, u32[]{:S(2)}) %collective-permute-start.4) | collective-permute-done | bytes 139296 | tf_op jit(solution)/shard_map/ppermute | solution.py:781
  31.6 0.0 collective-permute-done.5.refs_3_
  31.6 1.0 %offsets.1 = (f32[2,12,8,128]{3,2,1,0:T(8,128)S(1)}, f32[2,12,8,128]{3,2,1,0:T(8,128)S(1)}) custom-call(s32[2]{0:T(128)S(1)} %pad_add_fusion.1.refs_0_, f32[2,17,8,128]{3,2,1,0:T(8,128)S(1)} %extend.1.refs_1_, f32[2,17,8,128]{3,2,1,0:T(8,128)S(1)} %collective-permute-done.4.refs_2_, f32[2,17,8,128]{3,2,1,0:T(8,128)S(1)} %collective-permute-done.5.refs_3_), custom_call_target="tpu_custom_call" | custom-call | tf_op jit(solution)/shard_map/offsets/pallas_call | solution.py:784
  32.6 8.6 %collective-permute-start.6 = (f32[2,12,8,128]{3,2,1,0:T(8,128)S(1)}, f32[2,12,8,128]{3,2,1,0:T(8,128)S(1)}, u32[]{:S(2)}, u32[]{:S(2)}) collective-permute-start(f32[2,12,8,128]{3,2,1,0:T(8,128)S(1)} %get-tuple-element.36), channel_id=1, source_target_pairs={{0,8},{4,12},{8,0},{12,4},{16,24},{20,28},{24,16},{28,20},{1,9},{5... | collective-permute-start | bytes 294920 | tf_op jit(solution)/shard_map/ppermute | solution.py:794
  41.3 2.6 %collective-permute-done.6 = f32[2,12,8,128]{3,2,1,0:T(8,128)S(1)} collective-permute-done((f32[2,12,8,128]{3,2,1,0:T(8,128)S(1)}, f32[2,12,8,128]{3,2,1,0:T(8,128)S(1)}, u32[]{:S(2)}, u32[]{:S(2)}) %collective-permute-start.6) | collective-permute-done | bytes 98336 | tf_op jit(solution)/shard_map/ppermute | solution.py:794
  43.9 4.1 %collective-permute-start.7 = (f32[2,12,8,128]{3,2,1,0:T(8,128)S(1)}, f32[2,12,8,128]{3,2,1,0:T(8,128)S(1)}, u32[]{:S(2)}, u32[]{:S(2)}) collective-permute-start(f32[2,12,8,128]{3,2,1,0:T(8,128)S(1)} %pad_maximum_fusion), channel_id=1, source_target_pairs={{0,24},{4,28},{8,16},{12,20},{16,8},{20,12},{24,0},{28,4},{1,25},{... | collective-permute-start | bytes 294920 | tf_op jit(solution)/shard_map/ppermute | solution.py:794
  48.1 2.7 %collective-permute-done.7 = f32[2,12,8,128]{3,2,1,0:T(8,128)S(1)} collective-permute-done((f32[2,12,8,128]{3,2,1,0:T(8,128)S(1)}, f32[2,12,8,128]{3,2,1,0:T(8,128)S(1)}, u32[]{:S(2)}, u32[]{:S(2)}) %collective-permute-start.7) | collective-permute-done | bytes 98336 | tf_op jit(solution)/shard_map/ppermute | solution.py:794
  50.8 1.2 %result.1 = f32[2,10,96,128]{3,2,1,0:T(8,128)} custom-call(f32[2,10,5,8,128]{4,3,2,1,0:T(8,128)S(1)} %get-tuple-element.25.refs_0_, f32[2,10,2,8,128]{4,3,2,1,0:T(8,128)S(1)} %get-tuple-element.26.refs_1_, f32[2,10,5,8,128]{4,3,2,1,0:T(8,128)S(1)} %get-tuple-element.30.refs_2_, f32[2,12,8,128]{3,2,1,0:T(8,128)S(1)} %maximum_select_fusion.1.refs_3_), custom_call_target="tpu_custom_call" | custom-call | tf_op jit(solution)/shard_map/result/pallas_call | solution.py:798
  (5 shorter events, 0.1 us)
Async XLA Ops:
  2.8 9.2 %collective-permute-start = (f32[10,5,8,128]{3,2,1,0:T(8,128)S(1)}, f32[10,5,8,128]{3,2,1,0:T(8,128)S(1)}, u32[]{:S(2)}, u32[]{:S(2)}) collective-permute-start(f32[10,5,8,128]{3,2,1,0:T(8,128)S(1)} %get-tuple-element.23), channel_id=1, source_target_pairs={{0,1},{1,0},{2,3},{3,2},{4,5},{5,4},{6,7},{7,6},{8,9},{9,8},{10,11... | collective-permute-start | bytes 614408 | tf_op jit(solution)/shard_map/ppermute | solution.py:694
  3.4 8.6 %collective-permute-start.1 = (f32[10,5,8,128]{3,2,1,0:T(8,128)S(1)}, f32[10,5,8,128]{3,2,1,0:T(8,128)S(1)}, u32[]{:S(2)}, u32[]{:S(2)}) collective-permute-start(f32[10,5,8,128]{3,2,1,0:T(8,128)S(1)} %get-tuple-element.24), channel_id=1, source_target_pairs={{0,3},{1,2},{2,1},{3,0},{4,7},{5,6},{6,5},{7,4},{8,11},{9,10},{10,... | collective-permute-start | bytes 614408 | tf_op jit(solution)/shard_map/ppermute | solution.py:693
  18.5 5.1 %collective-permute-start.2 = (f32[5,8,128]{2,1,0:T(8,128)S(1)}, f32[5,8,128]{2,1,0:T(8,128)S(1)}, u32[]{:S(2)}, u32[]{:S(2)}) collective-permute-start(f32[5,8,128]{2,1,0:T(8,128)S(1)} %get-tuple-element.29.refs_5_), channel_id=1, source_target_pairs={{0,1},{1,0},{2,3},{3,2},{4,5},{5,4},{6,7},{7,6},{8,9},{9,8},{10,11... | collective-permute-start | bytes 61448 | tf_op jit(solution)/shard_map/ppermute | solution.py:757
  18.6 4.9 %collective-permute-start.3 = (f32[5,8,128]{2,1,0:T(8,128)S(1)}, f32[5,8,128]{2,1,0:T(8,128)S(1)}, u32[]{:S(2)}, u32[]{:S(2)}) collective-permute-start(f32[5,8,128]{2,1,0:T(8,128)S(1)} %get-tuple-element.34), channel_id=1, source_target_pairs={{0,3},{1,2},{2,1},{3,0},{4,7},{5,6},{6,5},{7,4},{8,11},{9,10},{10,... | collective-permute-start | bytes 61448 | tf_op jit(solution)/shard_map/ppermute | solution.py:756
  24.1 7.5 %collective-permute-start.4 = (f32[2,17,8,128]{3,2,1,0:T(8,128)S(1)}, f32[2,17,8,128]{3,2,1,0:T(8,128)S(1)}, u32[]{:S(2)}, u32[]{:S(2)}) collective-permute-start(f32[2,17,8,128]{3,2,1,0:T(8,128)S(1)} %extend.1.refs_1_), channel_id=1, source_target_pairs={{0,4},{4,0},{8,12},{12,8},{16,20},{20,16},{24,28},{28,24},{1,5},{5... | collective-permute-start | bytes 417800 | tf_op jit(solution)/shard_map/ppermute | solution.py:781
  27.5 4.1 %collective-permute-start.5 = (f32[2,17,8,128]{3,2,1,0:T(8,128)S(1)}, f32[2,17,8,128]{3,2,1,0:T(8,128)S(1)}, u32[]{:S(2)}, u32[]{:S(2)}) collective-permute-start(f32[2,17,8,128]{3,2,1,0:T(8,128)S(1)} %extend.1.refs_1_), channel_id=1, source_target_pairs={{4,8},{12,16},{20,24},{8,4},{16,12},{24,20},{5,9},{13,17},{21,25},... | collective-permute-start | bytes 417800 | tf_op jit(solution)/shard_map/ppermute | solution.py:782
  32.6 11.2 %collective-permute-start.6 = (f32[2,12,8,128]{3,2,1,0:T(8,128)S(1)}, f32[2,12,8,128]{3,2,1,0:T(8,128)S(1)}, u32[]{:S(2)}, u32[]{:S(2)}) collective-permute-start(f32[2,12,8,128]{3,2,1,0:T(8,128)S(1)} %get-tuple-element.36), channel_id=1, source_target_pairs={{0,8},{4,12},{8,0},{12,4},{16,24},{20,28},{24,16},{28,20},{1,9},{5... | collective-permute-start | bytes 294920 | tf_op jit(solution)/shard_map/ppermute | solution.py:794
  43.9 6.8 %collective-permute-start.7 = (f32[2,12,8,128]{3,2,1,0:T(8,128)S(1)}, f32[2,12,8,128]{3,2,1,0:T(8,128)S(1)}, u32[]{:S(2)}, u32[]{:S(2)}) collective-permute-start(f32[2,12,8,128]{3,2,1,0:T(8,128)S(1)} %pad_maximum_fusion), channel_id=1, source_target_pairs={{0,24},{4,28},{8,16},{12,20},{16,8},{20,12},{24,0},{28,4},{1,25},{... | collective-permute-start | bytes 294920 | tf_op jit(solution)/shard_map/ppermute | solution.py:794

commit v5 on v4

--- a/solution.py
+++ b/solution.py
@@ -8,7 +8,7 @@
 WIN_ROWS = 11
 WIN_COLS = 5
 INNER_DONE = 2
-PIECE = 5
+PIECE = 2
 ITERS = 20
 HALF_ROWS = WIN_ROWS // 2
 
@@ -38,6 +38,11 @@
 
 def lane():
     return lax.broadcasted_iota(jnp.int32, (SUB, LANES), 1)
+
+
+def row_place():
+    at = lax.axis_index("space")
+    return at % 2 == 1, (at == 0) | (at == lax.axis_size("space") - 1)
 
 
 def flip(x):
@@ -80,13 +85,13 @@
 
 
 def images_kernel(
-    rows, tiles, par_ref, amp_hbm, phase_hbm, valid_hbm, z_ref, x_ref, y_ref,
+    rows, tiles, amp_hbm, phase_hbm, valid_hbm, z_ref, x_ref, y_ref,
     amp_ref, phase_ref, valid_ref, sems,
 ):
     half = rows // 2
     dates = z_ref.shape[1]
     top = upper()
-    odd = par_ref[0] == 1
+    odd, _ = row_place()
     step = PIECE if dates % PIECE == 0 else dates
     copies = []
     for p in range(dates // step):
@@ -248,13 +253,12 @@
 
 
 def iterate(
-    first, last, offset, dates, scalars, z_ref, nr, ni, more, sq, vec,
+    first, last, offset, dates, iter_ref, z_ref, nr, ni, more, sq, vec,
     link_ref, comp_ref, out_offset=0,
 ):
     pairs = pair_list(dates)
     index = {pair: e for e, pair in enumerate(pairs)}
     count = len(pairs)
-    iter_ref, chosen_ref = scalars
     groups = []
     at = 0
     for size in (3, 3, 4) if dates == 10 else (dates,):
@@ -387,9 +391,6 @@
         scale = lax.rsqrt(length)
         vr = [a * scale for a in vectors[:dates]]
         vi = [a * scale for a in vectors[dates:]]
-        for i in range(dates):
-            vec[i] = vr[i]
-            vec[dates + i] = vi[i]
         cr = ci = None
         for i in range(dates):
             zr, zi = z_ref[0, i, whole_k], z_ref[1, i, whole_k]
@@ -397,18 +398,16 @@
             ci = add_to(ci, 1, vr[i] * zi - vi[i] * zr)
         comp_ref[0, place] = cr
         comp_ref[1, place] = ci
-        ref_r = vec[chosen_ref[0]] * float(dates)
-        ref_i = vec[dates + chosen_ref[0]] * float(dates)
         for i in range(dates):
-            link_ref[0, i, place] = vr[i] * ref_r + vi[i] * ref_i
-            link_ref[1, i, place] = vi[i] * ref_r - vr[i] * ref_i
+            link_ref[0, i, place] = vr[i]
+            link_ref[1, i, place] = vi[i]
         return carry
 
     lax.fori_loop(first, last, one_vector, 0)
 
 
 def inner_kernel(
-    tiles, done, iter_ref, chosen_ref, z_ref,
+    tiles, done, iter_ref, z_ref,
     nr_b, ni_b, part_ref, link_ref, comp_ref,
     band, split, inv, nr_a, ni_a, more, sq, vec,
 ):
@@ -423,7 +422,6 @@
     pairs = pair_list(dates)
     count = len(pairs)
     index = {pair: e for e, pair in enumerate(pairs)}
-    scalars = iter_ref, chosen_ref
     fill_band(band)
 
     def image(t):
@@ -447,24 +445,22 @@
 
     coherence(dates, vectors, fields, split, band, inv, places, side_masks(tiles))
     iterate(
-        HALF_ROWS, HALF_ROWS + done, HALF_ROWS, dates, scalars, z_ref, nr_a, ni_a,
+        HALF_ROWS, HALF_ROWS + done, HALF_ROWS, dates, iter_ref, z_ref, nr_a, ni_a,
         more, sq, vec, link_ref, comp_ref, HALF_ROWS,
     )
 
 
 def outer_kernel(
-    tiles, par_ref, iter_ref, chosen_ref, z_ref, part_ref, x_ref, y_ref,
+    tiles, iter_ref, z_ref, part_ref, x_ref, y_ref,
     link_ref, comp_ref, pack_x_ref, pack_y_ref,
     halo, band, split, inv, nr, ni, more, sq, vec,
 ):
     dates = z_ref.shape[1]
     top = upper()
-    odd_device = par_ref[0] == 1
-    edge = par_ref[1] == 1
+    odd_device, edge = row_place()
     pairs = pair_list(dates)
     count = len(pairs)
     index = {pair: e for e, pair in enumerate(pairs)}
-    scalars = iter_ref, chosen_ref
     fill_band(band)
 
     def fill(t, carry):
@@ -494,7 +490,7 @@
     places = [(nr, ni, k) for k in range(HALF_ROWS)]
     coherence(dates, HALF_ROWS, fields, split, band, inv, places, side_masks(tiles))
     iterate(
-        0, HALF_ROWS, 0, dates, scalars, z_ref, nr, ni, more, sq, vec,
+        0, HALF_ROWS, 0, dates, iter_ref, z_ref, nr, ni, more, sq, vec,
         link_ref, comp_ref,
     )
     for k in range(HALF_ROWS):
@@ -504,13 +500,12 @@
 
 
 def rest_kernel(
-    start, iter_ref, chosen_ref, z_ref, nr, ni, after_ref, link_ref, comp_ref,
+    start, iter_ref, z_ref, nr, ni, after_ref, link_ref, comp_ref,
     more, sq, vec,
 ):
     dates = z_ref.shape[1]
-    scalars = iter_ref, chosen_ref
     iterate(
-        start, start + comp_ref.shape[1], start, dates, scalars, z_ref, nr, ni,
+        start, start + comp_ref.shape[1], start, dates, iter_ref, z_ref, nr, ni,
         more, sq, vec, link_ref, comp_ref, start,
     )
 
@@ -539,10 +534,9 @@
     return lanes, (column != 0, column != tiles - 1)
 
 
-def extend_kernel(par_ref, outer_ref, inner_ref, rest_ref, x_ref, y_ref, out_ref):
+def extend_kernel(outer_ref, inner_ref, rest_ref, x_ref, y_ref, out_ref):
     top = upper()
-    odd_device = par_ref[0] == 1
-    edge = par_ref[1] == 1
+    odd_device, edge = row_place()
     for k in range(HALF_ROWS):
         a, b = x_ref[k], jnp.where(edge, 0.0, y_ref[k])
         re, im = unpack(jnp.where(odd_device, a, b), jnp.where(odd_device, b, a), top)
@@ -557,12 +551,13 @@
 
 
 def offsets_kernel(
-    tiles, place_ref, own_ref, a_ref, b_ref, unit_ref, total_ref
+    tiles, own_ref, a_ref, b_ref, unit_ref, total_ref
 ):
     lanes, edges = masks(tiles)
     half = unit_ref.shape[1]
-    odd_stack = place_ref[1] == 1
-    first_stack = place_ref[0] == 0
+    place = lax.axis_index("tm")
+    odd_stack = place % 2 == 1
+    first_stack = place == 0
 
     def whole(*refs):
         parts = []
@@ -611,23 +606,46 @@
         total_ref[1, k] = before_r * after_i + before_i * after_r
 
 
-def result_kernel(rows, tiles, outer_ref, inner_ref, rest_ref, datum_ref, out_ref):
+def result_kernel(
+    rows, tiles, chosen_ref, outer_ref, inner_ref, rest_ref, datum_ref, out_hbm,
+    out_ref, turn, sems,
+):
     half = rows // 2
     parts = (outer_ref, inner_ref, rest_ref)
     links = [(ref, k) for ref in parts for k in range(ref.shape[2])]
+    dates = outer_ref.shape[1]
+
+    chosen = chosen_ref[0]
+    for k, (ref, at) in enumerate(links):
+        vr = ref[0, chosen, at] * float(dates)
+        vi = ref[1, chosen, at] * float(dates)
+        dr, di = datum_ref[0, k], datum_ref[1, k]
+        turn[0, k] = dr * vr + di * vi
+        turn[1, k] = di * vr - dr * vi
+
+    def copies(t):
+        return [
+            pltpu.make_async_copy(out_ref.at[part, t], out_hbm.at[part, t], sems.at[part, t])
+            for part in range(2)
+        ]
 
     def one_date(t, carry):
         for k in range(half):
             ref, at = links[k]
             lr, li = ref[0, t, at], ref[1, t, at]
-            dr, di = datum_ref[0, k], datum_ref[1, k]
+            dr, di = turn[0, k], turn[1, k]
             first, second = bases(k, rows, tiles)
             for part, value in enumerate((lr * dr - li * di, lr * di + li * dr)):
                 out_ref[part, t, pl.ds(first, tiles, stride=SUB), :] = value[:tiles]
                 out_ref[part, t, pl.ds(second, tiles, stride=SUB), :] = value[tiles:]
+        for copy in copies(t):
+            copy.start()
         return carry
 
-    lax.fori_loop(0, outer_ref.shape[1], one_date, 0)
+    lax.fori_loop(0, dates, one_date, 0)
+    for t in range(dates):
+        for copy in copies(t):
+            copy.wait()
 
 
 def swaps(count, bit=None, odd=False):
@@ -655,9 +673,6 @@
     members = lax.axis_size("tm")
     blocks = lax.axis_size("space")
     place = lax.axis_index("tm")
-    block = lax.axis_index("space")
-    edge = (block == 0) | (block == blocks - 1)
-    parity = jnp.stack([block % 2, edge.astype(jnp.int32)])
     params = pltpu.CompilerParams(vmem_limit_bytes=VMEM_LIMIT)
 
     def shape(*dims):
@@ -678,7 +693,7 @@
             shape(dates, HALF_ROWS, SUB, LANES),
             shape(dates, HALF_ROWS, SUB, LANES),
         ),
-        in_specs=[smem(), hbm(), hbm(), hbm()],
+        in_specs=[hbm(), hbm(), hbm()],
         out_specs=(vmem(), vmem(), vmem()),
         scratch_shapes=[
             pltpu.VMEM((dates, rows * tiles, LANES), jnp.float32),
@@ -688,7 +703,7 @@
         ],
         compiler_params=params,
         name="images",
-    )(parity, *(far_memory(tiled(x)) for x in (amplitude, phase, validity)))
+    )(*(far_memory(tiled(x)) for x in (amplitude, phase, validity)))
     pair_x, pair_y = swaps(blocks), swaps(blocks, odd=True)
     got_y = lax.ppermute(slab_y, "space", pair_y)
     got_x = lax.ppermute(slab_x, "space", pair_x)
@@ -723,7 +738,7 @@
             shape(2, dates, done, SUB, LANES),
             shape(2, done, SUB, LANES),
         ),
-        in_specs=[smem(), smem(), vmem()],
+        in_specs=[smem(), vmem()],
         out_specs=(vmem(),) * 5,
         scratch_shapes=window_work(inner)
         + [pltpu.VMEM((count, done, SUB, LANES), jnp.float32)] * 2
@@ -731,7 +746,7 @@
         compiler_params=params,
         cost_estimate=cost(4),
         name="inner",
-    )(iterations, reference_date, z)
+    )(iterations, z)
     linked_b, comp_b, pack_x, pack_y = pl.pallas_call(
         lambda *refs: outer_kernel(tiles, *refs),
         out_shape=(
@@ -740,7 +755,7 @@
             shape(HALF_ROWS, SUB, LANES),
             shape(HALF_ROWS, SUB, LANES),
         ),
-        in_specs=[smem()] * 3 + [vmem()] * 4,
+        in_specs=[smem()] + [vmem()] * 4,
         out_specs=(vmem(),) * 4,
         scratch_shapes=[pltpu.VMEM((2, dates, HALF_ROWS, SUB, LANES), jnp.float32)]
         + window_work(HALF_ROWS)
@@ -752,7 +767,7 @@
         compiler_params=params,
         cost_estimate=cost(7),
         name="outer",
-    )(parity, iterations, reference_date, z, part, got_x, got_y)
+    )(iterations, z, part, got_x, got_y)
     more_y = lax.ppermute(pack_y, "space", pair_y)
     more_x = lax.ppermute(pack_x, "space", pair_x)
 
@@ -763,32 +778,31 @@
             shape(2, dates, half - start, SUB, LANES),
             shape(2, half - start, SUB, LANES),
         ),
-        in_specs=[smem()] * 2 + [vmem()] * 4,
+        in_specs=[smem()] + [vmem()] * 4,
         out_specs=(vmem(),) * 2,
         scratch_shapes=work,
         compiler_params=params,
         cost_estimate=cost(5),
         name="rest",
-    )(iterations, reference_date, z, nr, ni, pack_x)
+    )(iterations, z, nr, ni, pack_x)
     wide = pl.pallas_call(
         extend_kernel,
         out_shape=shape(2, ext, SUB, LANES),
-        in_specs=[smem()] + [vmem()] * 5,
+        in_specs=[vmem()] * 5,
         out_specs=vmem(),
         compiler_params=params,
         name="extend",
-    )(parity, comp_b, comp_a, comp_c, more_x, more_y)
+    )(comp_b, comp_a, comp_c, more_x, more_y)
     other_a = lax.ppermute(wide, "tm", swaps(members))
     other_b = lax.ppermute(wide, "tm", inner_swaps(members))
-    where = jnp.stack([place, place % 2]).astype(jnp.int32)
     datum, total = pl.pallas_call(
         lambda *refs: offsets_kernel(tiles, *refs),
         out_shape=(shape(2, half, SUB, LANES), shape(2, half, SUB, LANES)),
-        in_specs=[smem()] + [vmem()] * 3,
+        in_specs=[vmem()] * 3,
         out_specs=(vmem(), vmem()),
         compiler_params=params,
         name="offsets",
-    )(where, wide, other_a, other_b)
+    )(wide, other_a, other_b)
     bit = 2
     while bit < members:
         other = lax.ppermute(total, "tm", swaps(members, bit=2 * bit - 2))
@@ -798,11 +812,16 @@
     out = pl.pallas_call(
         lambda *refs: result_kernel(rows, tiles, *refs),
         out_shape=shape(2, dates, rows * tiles, LANES),
-        in_specs=[vmem()] * 4,
-        out_specs=vmem(),
+        in_specs=[smem()] + [vmem()] * 4,
+        out_specs=hbm(),
+        scratch_shapes=[
+            pltpu.VMEM((2, dates, rows * tiles, LANES), jnp.float32),
+            pltpu.VMEM((2, half, SUB, LANES), jnp.float32),
+            pltpu.SemaphoreType.DMA((2, dates)),
+        ],
         compiler_params=params,
         name="result",
-    )(linked_b, linked_a, linked_c, datum)
+    )(reference_date, linked_b, linked_a, linked_c, datum)
     out = out.reshape(2, dates, rows // SUB, tiles, SUB, LANES)
     return jnp.swapaxes(out, -3, -2).reshape(2, dates, rows, columns)
 

time: 51.6 us -> 47.5 us (0.921)
  starting transfers between devices: 20.8 us -> 14.8 us
  Pallas kernels: 20.9 us -> 22.2 us
    ppermute x2, starting transfers between devices: 12.7 us -> 9.28 us  [local(): other = lax.ppermute(total, 'tm', swaps(members, bit=2 * bit - 2))]
    ppermute x1, starting transfers between devices: 3.41 us -> 0.88 us  [local(): other_a = lax.ppermute(wide, 'tm', swaps(members))]
    pallas_call x1, Pallas kernels: 4.19 us -> 5.67 us  [local(): pl.pallas_call(lambda *refs: rest_kernel(start, *refs), out_shape=(shape(...]
    ppermute x1, waiting for transfers between devices: 3.33 us -> 4.52 us  [local(): other_a = lax.ppermute(wide, 'tm', swaps(members))]
    pallas_call x1, Pallas kernels: 6.48 us -> 7.5 us  [local(): pl.pallas_call(lambda *refs: outer_kernel(tiles, *refs), out_shape=(shape...]
    ppermute x2, waiting for transfers between devices: 5.28 us -> 4.53 us  [local(): other = lax.ppermute(total, 'tm', swaps(members, bit=2 * bit - 2))]
    pallas_call x1, Pallas kernels: 2.72 us -> 2.07 us  [local(): pl.pallas_call(lambda *refs: images_kernel(rows, tiles, *refs), out_shape...]
    pallas_call x1, Pallas kernels: 4.72 us -> 5.35 us  [local(): pl.pallas_call(lambda *refs: inner_kernel(tiles, done, *refs), out_shape=...]
  transfers between devices with their start and end apart: 8 -> 8, of which waited for: 3 -> 3; matrix products, arithmetic and copies ran while one was open for 0% -> 0% of each run, Pallas kernels for 17% -> 23%
where the time goes in v5:
time: 47.5 us; the launch traced here: 47.6 us
  Pallas kernels  22.2 us (47%)
  starting transfers between devices  14.8 us (31%)
  waiting for transfers between devices  9.06 us (19%)
  between operations  1.42 us (3%)
    ppermute x2, starting transfers between devices, local(): other = lax.ppermute(total, 'tm', swaps(members, bit=2 * bit - 2))  9.28 us
    pallas_call x1, Pallas kernels, local(): pl.pallas_call(lambda *refs: outer_kernel(tiles, *refs), out_shape=(shape...  7.5 us
    pallas_call x1, Pallas kernels, local(): pl.pallas_call(lambda *refs: rest_kernel(start, *refs), out_shape=(shape(...  5.67 us
    pallas_call x1, Pallas kernels, local(): pl.pallas_call(lambda *refs: inner_kernel(tiles, done, *refs), out_shape=...  5.35 us
    ppermute x2, waiting for transfers between devices, local(): other = lax.ppermute(total, 'tm', swaps(members, bit=2 * bit - 2))  4.53 us
    ppermute x1, waiting for transfers between devices, local(): other_a = lax.ppermute(wide, 'tm', swaps(members))  4.52 us
    ppermute x1, starting transfers between devices, local(): got_y = lax.ppermute(slab_y, 'space', pair_y)  2.59 us
    pallas_call x1, Pallas kernels, local(): pl.pallas_call(lambda *refs: images_kernel(rows, tiles, *refs), out_shape...  2.07 us
  transfers between devices with their start and end apart: 8, of which 3 were waited for; matrix products, arithmetic and copies ran while one was open for 0% of the time, Pallas kernels for 23%

profile of v5, /device:TPU:0, one launch (start us, length us, event | category | flops | bytes accessed | tf_op | source)
XLA Modules:
  0.0 47.6 jit_solution(3182184573050518530)
XLA Ops:
  0.0 2.1 %images.1 = (f32[2,10,17,8,128]{4,3,2,1,0:T(8,128)S(1)}, f32[10,5,8,128]{3,2,1,0:T(8,128)S(1)}, f32[10,5,8,128]{3,2,1,0:T(8,128)S(1)}) custom-call(f32[10,96,128]{2,1,0:T(8,128)} %bitcast.20, f32[10,96,128]{2,1,0:T(8,128)} %bitcast.21, s32[96,128]{1,0:T(8,128)} %bitcast.22), custom_call_target="tpu_custom_call" | custom-call | tf_op jit(solution)/shard_map/images/pallas_call | solution.py:689
  2.1 0.6 %collective-permute-start = (f32[10,5,8,128]{3,2,1,0:T(8,128)S(1)}, f32[10,5,8,128]{3,2,1,0:T(8,128)S(1)}, u32[]{:S(2)}, u32[]{:S(2)}) collective-permute-start(f32[10,5,8,128]{3,2,1,0:T(8,128)S(1)} %get-tuple-element.23), channel_id=1, source_target_pairs={{0,1},{1,0},{2,3},{3,2},{4,5},{5,4},{6,7},{7,6},{8,9},{9,8},{10,11... | collective-permute-start | bytes 614408 | tf_op jit(solution)/shard_map/ppermute | solution.py:709
  2.6 2.6 %collective-permute-start.1 = (f32[10,5,8,128]{3,2,1,0:T(8,128)S(1)}, f32[10,5,8,128]{3,2,1,0:T(8,128)S(1)}, u32[]{:S(2)}, u32[]{:S(2)}) collective-permute-start(f32[10,5,8,128]{3,2,1,0:T(8,128)S(1)} %get-tuple-element.24), channel_id=1, source_target_pairs={{0,3},{1,2},{2,1},{3,0},{4,7},{5,6},{6,5},{7,4},{8,11},{9,10},{10,... | collective-permute-start | bytes 614408 | tf_op jit(solution)/shard_map/ppermute | solution.py:708
  5.9 5.4 %inner.1 = (f32[45,5,8,128]{3,2,1,0:T(8,128)S(1)}, f32[45,5,8,128]{3,2,1,0:T(8,128)S(1)}, f32[100,5,8,128]{3,2,1,0:T(8,128)S(1)}, f32[2,10,2,8,128]{4,3,2,1,0:T(8,128)S(1)}, f32[2,2,8,128]{3,2,1,0:T(8,128)S(1)}) custom-call(s32[1]{0:T(128)S(6)} %copy.6.refs_0_, f32[2,10,17,8,128]{4,3,2,1,0:T(8,128)S(1)} %get-tuple-element.21.refs_1_), custom_call_target="tpu_custom_call" | custom-call | flops 64000000 | bytes 1048576 | tf_op jit(solution)/shard_map/inner/pallas_call | solution.py:732
  11.2 0.0 collective-permute-done.refs_3_
  11.2 0.0 collective-permute-done.1.refs_4_
  11.3 7.5 %outer.1 = (f32[2,10,5,8,128]{4,3,2,1,0:T(8,128)S(1)}, f32[2,5,8,128]{3,2,1,0:T(8,128)S(1)}, f32[5,8,128]{2,1,0:T(8,128)S(1)}, f32[5,8,128]{2,1,0:T(8,128)S(1)}) custom-call(s32[1]{0:T(128)S(6)} %copy.6.refs_0_, f32[2,10,17,8,128]{4,3,2,1,0:T(8,128)S(1)} %get-tuple-element.21.refs_1_, f32[100,5,8,128]{3,2,1,0:T(8,128)S(1)} %get-tuple-element.22.refs_2_, ...), custom_call_target="tpu_custom_call" | custom-call | flops 112000000 | bytes 1048576 | tf_op jit(solution)/shard_map/outer/pallas_call | solution.py:750
  18.8 0.1 collective-permute-start.2
  18.9 0.7 %collective-permute-start.3 = (f32[5,8,128]{2,1,0:T(8,128)S(1)}, f32[5,8,128]{2,1,0:T(8,128)S(1)}, u32[]{:S(2)}, u32[]{:S(2)}) collective-permute-start(f32[5,8,128]{2,1,0:T(8,128)S(1)} %get-tuple-element.34), channel_id=1, source_target_pairs={{0,3},{1,2},{2,1},{3,0},{4,7},{5,6},{6,5},{7,4},{8,11},{9,10},{10,... | collective-permute-start | bytes 61448 | tf_op jit(solution)/shard_map/ppermute | solution.py:771
  19.6 5.7 %rest.1 = (f32[2,10,5,8,128]{4,3,2,1,0:T(8,128)S(1)}, f32[2,5,8,128]{3,2,1,0:T(8,128)S(1)}) custom-call(s32[1]{0:T(128)S(6)} %copy.6.refs_0_, f32[2,10,17,8,128]{4,3,2,1,0:T(8,128)S(1)} %get-tuple-element.21.refs_1_, f32[45,5,8,128]{3,2,1,0:T(8,128)S(1)} %get-tuple-element.27.refs_2_, f32[45,5,8,128]{3,2,1,0:T(8,128)S(1)} %get-tuple-element.28.refs_3_, ...), custom_call_target="tpu_custom_call" | custom-call | flops 80000000 | bytes 1048576 | tf_op jit(solution)/shard_map/rest/pallas_call | solution.py:775
  25.3 0.0 collective-permute-done.2.x_ref
  25.3 0.0 collective-permute-done.3.y_ref
  25.4 0.9 %collective-permute-start.4 = (f32[2,17,8,128]{3,2,1,0:T(8,128)S(1)}, f32[2,17,8,128]{3,2,1,0:T(8,128)S(1)}, u32[]{:S(2)}, u32[]{:S(2)}) collective-permute-start(f32[2,17,8,128]{3,2,1,0:T(8,128)S(1)} %extend.1.refs_0_), channel_id=1, source_target_pairs={{0,4},{4,0},{8,12},{12,8},{16,20},{20,16},{24,28},{28,24},{1,5},{5... | collective-permute-start | bytes 417800 | tf_op jit(solution)/shard_map/ppermute | solution.py:796
  26.2 0.7 %collective-permute-start.5 = (f32[2,17,8,128]{3,2,1,0:T(8,128)S(1)}, f32[2,17,8,128]{3,2,1,0:T(8,128)S(1)}, u32[]{:S(2)}, u32[]{:S(2)}) collective-permute-start(f32[2,17,8,128]{3,2,1,0:T(8,128)S(1)} %extend.1.refs_0_), channel_id=1, source_target_pairs={{4,8},{12,16},{20,24},{8,4},{16,12},{24,20},{5,9},{13,17},{21,25},... | collective-permute-start | bytes 417800 | tf_op jit(solution)/shard_map/ppermute | solution.py:797
  26.9 4.5 %collective-permute-done.4.refs_1_ = f32[2,17,8,128]{3,2,1,0:T(8,128)S(1)} collective-permute-done((f32[2,17,8,128]{3,2,1,0:T(8,128)S(1)}, f32[2,17,8,128]{3,2,1,0:T(8,128)S(1)}, u32[]{:S(2)}, u32[]{:S(2)}) %collective-permute-start.4) | collective-permute-done | bytes 139296 | tf_op jit(solution)/shard_map/ppermute | solution.py:796
  31.4 0.0 collective-permute-done.5.refs_2_
  31.4 0.5 %offsets.1 = (f32[2,12,8,128]{3,2,1,0:T(8,128)S(1)}, f32[2,12,8,128]{3,2,1,0:T(8,128)S(1)}) custom-call(f32[2,17,8,128]{3,2,1,0:T(8,128)S(1)} %extend.1.refs_0_, f32[2,17,8,128]{3,2,1,0:T(8,128)S(1)} %collective-permute-done.4.refs_1_, f32[2,17,8,128]{3,2,1,0:T(8,128)S(1)} %collective-permute-done.5.refs_2_), custom_call_target="tpu_custom_call" | custom-call | tf_op jit(solution)/shard_map/offsets/pallas_call | solution.py:798
  31.9 4.1 %collective-permute-start.6 = (f32[2,12,8,128]{3,2,1,0:T(8,128)S(1)}, f32[2,12,8,128]{3,2,1,0:T(8,128)S(1)}, u32[]{:S(2)}, u32[]{:S(2)}) collective-permute-start(f32[2,12,8,128]{3,2,1,0:T(8,128)S(1)} %get-tuple-element.36), channel_id=1, source_target_pairs={{0,8},{4,12},{8,0},{12,4},{16,24},{20,28},{24,16},{28,20},{1,9},{5... | collective-permute-start | bytes 294920 | tf_op jit(solution)/shard_map/ppermute | solution.py:808
  36.7 1.9 %collective-permute-done.6 = f32[2,12,8,128]{3,2,1,0:T(8,128)S(1)} collective-permute-done((f32[2,12,8,128]{3,2,1,0:T(8,128)S(1)}, f32[2,12,8,128]{3,2,1,0:T(8,128)S(1)}, u32[]{:S(2)}, u32[]{:S(2)}) %collective-permute-start.6) | collective-permute-done | bytes 98336 | tf_op jit(solution)/shard_map/ppermute | solution.py:808
  38.7 5.1 %collective-permute-start.7 = (f32[2,12,8,128]{3,2,1,0:T(8,128)S(1)}, f32[2,12,8,128]{3,2,1,0:T(8,128)S(1)}, u32[]{:S(2)}, u32[]{:S(2)}) collective-permute-start(f32[2,12,8,128]{3,2,1,0:T(8,128)S(1)} %pad_maximum_fusion), channel_id=1, source_target_pairs={{0,24},{4,28},{8,16},{12,20},{16,8},{20,12},{24,0},{28,4},{1,25},{... | collective-permute-start | bytes 294920 | tf_op jit(solution)/shard_map/ppermute | solution.py:808
  43.9 2.6 %collective-permute-done.7 = f32[2,12,8,128]{3,2,1,0:T(8,128)S(1)} collective-permute-done((f32[2,12,8,128]{3,2,1,0:T(8,128)S(1)}, f32[2,12,8,128]{3,2,1,0:T(8,128)S(1)}, u32[]{:S(2)}, u32[]{:S(2)}) %collective-permute-start.7) | collective-permute-done | bytes 98336 | tf_op jit(solution)/shard_map/ppermute | solution.py:808
  46.5 1.1 %result.1 = f32[2,10,96,128]{3,2,1,0:T(8,128)} custom-call(s32[1]{0:T(128)S(6)} %copy.7.refs_0_, f32[2,10,5,8,128]{4,3,2,1,0:T(8,128)S(1)} %get-tuple-element.25.refs_1_, f32[2,10,2,8,128]{4,3,2,1,0:T(8,128)S(1)} %get-tuple-element.26.refs_2_, f32[2,10,5,8,128]{4,3,2,1,0:T(8,128)S(1)} %get-tuple-element.30.refs_3_, ...), custom_call_target="tpu_custom_call" | custom-call | tf_op jit(solution)/shard_map/result/pallas_call | solution.py:812
  (6 shorter events, 0.1 us)
Async XLA Ops:
  2.1 9.2 %collective-permute-start = (f32[10,5,8,128]{3,2,1,0:T(8,128)S(1)}, f32[10,5,8,128]{3,2,1,0:T(8,128)S(1)}, u32[]{:S(2)}, u32[]{:S(2)}) collective-permute-start(f32[10,5,8,128]{3,2,1,0:T(8,128)S(1)} %get-tuple-element.23), channel_id=1, source_target_pairs={{0,1},{1,0},{2,3},{3,2},{4,5},{5,4},{6,7},{7,6},{8,9},{9,8},{10,11... | collective-permute-start | bytes 614408 | tf_op jit(solution)/shard_map/ppermute | solution.py:709
  2.6 8.6 %collective-permute-start.1 = (f32[10,5,8,128]{3,2,1,0:T(8,128)S(1)}, f32[10,5,8,128]{3,2,1,0:T(8,128)S(1)}, u32[]{:S(2)}, u32[]{:S(2)}) collective-permute-start(f32[10,5,8,128]{3,2,1,0:T(8,128)S(1)} %get-tuple-element.24), channel_id=1, source_target_pairs={{0,3},{1,2},{2,1},{3,0},{4,7},{5,6},{6,5},{7,4},{8,11},{9,10},{10,... | collective-permute-start | bytes 614408 | tf_op jit(solution)/shard_map/ppermute | solution.py:708
  18.8 6.6 %collective-permute-start.2 = (f32[5,8,128]{2,1,0:T(8,128)S(1)}, f32[5,8,128]{2,1,0:T(8,128)S(1)}, u32[]{:S(2)}, u32[]{:S(2)}) collective-permute-start(f32[5,8,128]{2,1,0:T(8,128)S(1)} %get-tuple-element.29.refs_4_), channel_id=1, source_target_pairs={{0,1},{1,0},{2,3},{3,2},{4,5},{5,4},{6,7},{7,6},{8,9},{9,8},{10,11... | collective-permute-start | bytes 61448 | tf_op jit(solution)/shard_map/ppermute | solution.py:772
  18.9 6.4 %collective-permute-start.3 = (f32[5,8,128]{2,1,0:T(8,128)S(1)}, f32[5,8,128]{2,1,0:T(8,128)S(1)}, u32[]{:S(2)}, u32[]{:S(2)}) collective-permute-start(f32[5,8,128]{2,1,0:T(8,128)S(1)} %get-tuple-element.34), channel_id=1, source_target_pairs={{0,3},{1,2},{2,1},{3,0},{4,7},{5,6},{6,5},{7,4},{8,11},{9,10},{10,... | collective-permute-start | bytes 61448 | tf_op jit(solution)/shard_map/ppermute | solution.py:771
  25.4 6.1 %collective-permute-start.4 = (f32[2,17,8,128]{3,2,1,0:T(8,128)S(1)}, f32[2,17,8,128]{3,2,1,0:T(8,128)S(1)}, u32[]{:S(2)}, u32[]{:S(2)}) collective-permute-start(f32[2,17,8,128]{3,2,1,0:T(8,128)S(1)} %extend.1.refs_0_), channel_id=1, source_target_pairs={{0,4},{4,0},{8,12},{12,8},{16,20},{20,16},{24,28},{28,24},{1,5},{5... | collective-permute-start | bytes 417800 | tf_op jit(solution)/shard_map/ppermute | solution.py:796
  26.2 5.2 %collective-permute-start.5 = (f32[2,17,8,128]{3,2,1,0:T(8,128)S(1)}, f32[2,17,8,128]{3,2,1,0:T(8,128)S(1)}, u32[]{:S(2)}, u32[]{:S(2)}) collective-permute-start(f32[2,17,8,128]{3,2,1,0:T(8,128)S(1)} %extend.1.refs_0_), channel_id=1, source_target_pairs={{4,8},{12,16},{20,24},{8,4},{16,12},{24,20},{5,9},{13,17},{21,25},... | collective-permute-start | bytes 417800 | tf_op jit(solution)/shard_map/ppermute | solution.py:797
  31.9 6.7 %collective-permute-start.6 = (f32[2,12,8,128]{3,2,1,0:T(8,128)S(1)}, f32[2,12,8,128]{3,2,1,0:T(8,128)S(1)}, u32[]{:S(2)}, u32[]{:S(2)}) collective-permute-start(f32[2,12,8,128]{3,2,1,0:T(8,128)S(1)} %get-tuple-element.36), channel_id=1, source_target_pairs={{0,8},{4,12},{8,0},{12,4},{16,24},{20,28},{24,16},{28,20},{1,9},{5... | collective-permute-start | bytes 294920 | tf_op jit(solution)/shard_map/ppermute | solution.py:808
  38.7 7.7 %collective-permute-start.7 = (f32[2,12,8,128]{3,2,1,0:T(8,128)S(1)}, f32[2,12,8,128]{3,2,1,0:T(8,128)S(1)}, u32[]{:S(2)}, u32[]{:S(2)}) collective-permute-start(f32[2,12,8,128]{3,2,1,0:T(8,128)S(1)} %pad_maximum_fusion), channel_id=1, source_target_pairs={{0,24},{4,28},{8,16},{12,20},{16,8},{20,12},{24,0},{28,4},{1,25},{... | collective-permute-start | bytes 294920 | tf_op jit(solution)/shard_map/ppermute | solution.py:808

commit v6 on v5

--- a/solution.py
+++ b/solution.py
@@ -5,9 +5,10 @@
 from jax.experimental.pallas import tpu as pltpu
 from jax.sharding import PartitionSpec as P
 
+
 WIN_ROWS = 11
 WIN_COLS = 5
-INNER_DONE = 2
+INNER_DONE = 3
 PIECE = 2
 ITERS = 20
 HALF_ROWS = WIN_ROWS // 2
@@ -665,7 +666,7 @@
     return jnp.stack([a[0] * b[0] - a[1] * b[1], a[0] * b[1] + a[1] * b[0]])
 
 
-def local(amplitude, phase, validity, iterations, reference_date):
+def linked_phases(amplitude, phase, validity, iterations, reference_date):
     dates, rows, columns = amplitude.shape
     half = rows // 2
     tiles = columns // LANES
@@ -828,7 +829,7 @@
 
 def solution(mesh):
     return jax.shard_map(
-        local,
+        linked_phases,
         mesh=mesh,
         in_specs=(
             P("tm", "space", None),

time: 47.5 us -> 47.1 us (level)
  Pallas kernels: 22.2 us -> 23.5 us
  waiting for transfers between devices: 9.06 us -> 7.81 us
  starting transfers between devices: 14.8 us -> 14.1 us
    pallas_call x7, Pallas kernels: 22.2 us -> 23.5 us  [the longest x1 7.95 us: linked_phases(): pl.pallas_call(lambda *refs: outer_kernel(tiles, *refs), out_shape=(shape...]
    ppermute x8, waiting for transfers between devices: 9.06 us -> 7.81 us  [the longest x2 4.54 us: linked_phases(): other = lax.ppermute(total, 'tm', swaps(members, bit=2 * bit - 2))]
    ppermute x8, starting transfers between devices: 14.8 us -> 14.1 us  [the longest x2 8.03 us: linked_phases(): other = lax.ppermute(total, 'tm', swaps(members, bit=2 * bit - 2))]
  transfers between devices with their start and end apart: 8 -> 8, of which waited for: 3 -> 3; matrix products, arithmetic and copies ran while one was open for 0% -> 0% of each run, Pallas kernels for 23% -> 25%
where the time goes in v6:
time: 47.1 us; the launch traced here: 46.9 us
  Pallas kernels  23.5 us (50%)
  starting transfers between devices  14.1 us (30%)
  waiting for transfers between devices  7.81 us (17%)
  between operations  1.42 us (3%)
    ppermute x2, starting transfers between devices, linked_phases(): other = lax.ppermute(total, 'tm', swaps(members, bit=2 * bit - 2))  8.03 us
    pallas_call x1, Pallas kernels, linked_phases(): pl.pallas_call(lambda *refs: outer_kernel(tiles, *refs), out_shape=(shape...  7.95 us
    pallas_call x1, Pallas kernels, linked_phases(): pl.pallas_call(lambda *refs: inner_kernel(tiles, done, *refs), out_shape=...  6.77 us
    pallas_call x1, Pallas kernels, linked_phases(): pl.pallas_call(lambda *refs: rest_kernel(start, *refs), out_shape=(shape(...  5.06 us
    ppermute x2, waiting for transfers between devices, linked_phases(): other = lax.ppermute(total, 'tm', swaps(members, bit=2 * bit - 2))  4.54 us
    ppermute x1, waiting for transfers between devices, linked_phases(): other_a = lax.ppermute(wide, 'tm', swaps(members))  3.26 us
    ppermute x1, starting transfers between devices, linked_phases(): got_y = lax.ppermute(slab_y, 'space', pair_y)  2.59 us
    ppermute x1, starting transfers between devices, linked_phases(): other_a = lax.ppermute(wide, 'tm', swaps(members))  2.13 us
  transfers between devices with their start and end apart: 8, of which 3 were waited for; matrix products, arithmetic and copies ran while one was open for 0% of the time, Pallas kernels for 25%

profile of v6, /device:TPU:0, one launch (start us, length us, event | category | flops | bytes accessed | tf_op | source)
XLA Modules:
  0.0 46.9 jit_solution(3582287750125497923)
XLA Ops:
  0.0 2.1 %images.1 = (f32[2,10,17,8,128]{4,3,2,1,0:T(8,128)S(1)}, f32[10,5,8,128]{3,2,1,0:T(8,128)S(1)}, f32[10,5,8,128]{3,2,1,0:T(8,128)S(1)}) custom-call(f32[10,96,128]{2,1,0:T(8,128)} %bitcast.20, f32[10,96,128]{2,1,0:T(8,128)} %bitcast.21, s32[96,128]{1,0:T(8,128)} %bitcast.22), custom_call_target="tpu_custom_call" | custom-call | tf_op jit(solution)/shard_map/images/pallas_call | solution.py:690
  2.1 0.6 %collective-permute-start = (f32[10,5,8,128]{3,2,1,0:T(8,128)S(1)}, f32[10,5,8,128]{3,2,1,0:T(8,128)S(1)}, u32[]{:S(2)}, u32[]{:S(2)}) collective-permute-start(f32[10,5,8,128]{3,2,1,0:T(8,128)S(1)} %get-tuple-element.23), channel_id=1, source_target_pairs={{0,1},{1,0},{2,3},{3,2},{4,5},{5,4},{6,7},{7,6},{8,9},{9,8},{10,11... | collective-permute-start | bytes 614408 | tf_op jit(solution)/shard_map/ppermute | solution.py:710
  2.6 2.6 %collective-permute-start.1 = (f32[10,5,8,128]{3,2,1,0:T(8,128)S(1)}, f32[10,5,8,128]{3,2,1,0:T(8,128)S(1)}, u32[]{:S(2)}, u32[]{:S(2)}) collective-permute-start(f32[10,5,8,128]{3,2,1,0:T(8,128)S(1)} %get-tuple-element.24), channel_id=1, source_target_pairs={{0,3},{1,2},{2,1},{3,0},{4,7},{5,6},{6,5},{7,4},{8,11},{9,10},{10,... | collective-permute-start | bytes 614408 | tf_op jit(solution)/shard_map/ppermute | solution.py:709
  5.9 6.8 %inner.1 = (f32[45,4,8,128]{3,2,1,0:T(8,128)S(1)}, f32[45,4,8,128]{3,2,1,0:T(8,128)S(1)}, f32[100,5,8,128]{3,2,1,0:T(8,128)S(1)}, f32[2,10,3,8,128]{4,3,2,1,0:T(8,128)S(1)}, f32[2,3,8,128]{3,2,1,0:T(8,128)S(1)}) custom-call(s32[1]{0:T(128)S(6)} %copy.6.refs_0_, f32[2,10,17,8,128]{4,3,2,1,0:T(8,128)S(1)} %get-tuple-element.21.refs_1_), custom_call_target="tpu_custom_call" | custom-call | flops 64000000 | bytes 1048576 | tf_op jit(solution)/shard_map/inner/pallas_call | solution.py:733
  12.7 0.0 collective-permute-done.refs_3_
  12.7 0.0 collective-permute-done.1.refs_4_
  12.7 8.0 %outer.1 = (f32[2,10,5,8,128]{4,3,2,1,0:T(8,128)S(1)}, f32[2,5,8,128]{3,2,1,0:T(8,128)S(1)}, f32[5,8,128]{2,1,0:T(8,128)S(1)}, f32[5,8,128]{2,1,0:T(8,128)S(1)}) custom-call(s32[1]{0:T(128)S(6)} %copy.6.refs_0_, f32[2,10,17,8,128]{4,3,2,1,0:T(8,128)S(1)} %get-tuple-element.21.refs_1_, f32[100,5,8,128]{3,2,1,0:T(8,128)S(1)} %get-tuple-element.22.refs_2_, ...), custom_call_target="tpu_custom_call" | custom-call | flops 112000000 | bytes 1048576 | tf_op jit(solution)/shard_map/outer/pallas_call | solution.py:751
  20.6 0.1 collective-permute-start.2
  20.8 0.0 collective-permute-start.3
  20.8 5.1 %rest.1 = (f32[2,10,4,8,128]{4,3,2,1,0:T(8,128)S(1)}, f32[2,4,8,128]{3,2,1,0:T(8,128)S(1)}) custom-call(s32[1]{0:T(128)S(6)} %copy.6.refs_0_, f32[2,10,17,8,128]{4,3,2,1,0:T(8,128)S(1)} %get-tuple-element.21.refs_1_, f32[45,4,8,128]{3,2,1,0:T(8,128)S(1)} %get-tuple-element.27.refs_2_, f32[45,4,8,128]{3,2,1,0:T(8,128)S(1)} %get-tuple-element.28.refs_3_, ...), custom_call_target="tpu_custom_call" | custom-call | flops 80000000 | bytes 1048576 | tf_op jit(solution)/shard_map/rest/pallas_call | solution.py:776
  25.9 0.0 collective-permute-done.2.x_ref
  25.9 0.0 collective-permute-done.3.y_ref
  25.9 2.1 %collective-permute-start.4 = (f32[2,17,8,128]{3,2,1,0:T(8,128)S(1)}, f32[2,17,8,128]{3,2,1,0:T(8,128)S(1)}, u32[]{:S(2)}, u32[]{:S(2)}) collective-permute-start(f32[2,17,8,128]{3,2,1,0:T(8,128)S(1)} %extend.1.refs_0_), channel_id=1, source_target_pairs={{0,4},{4,0},{8,12},{12,8},{16,20},{20,16},{24,28},{28,24},{1,5},{5... | collective-permute-start | bytes 417800 | tf_op jit(solution)/shard_map/ppermute | solution.py:797
  28.0 0.7 %collective-permute-start.5 = (f32[2,17,8,128]{3,2,1,0:T(8,128)S(1)}, f32[2,17,8,128]{3,2,1,0:T(8,128)S(1)}, u32[]{:S(2)}, u32[]{:S(2)}) collective-permute-start(f32[2,17,8,128]{3,2,1,0:T(8,128)S(1)} %extend.1.refs_0_), channel_id=1, source_target_pairs={{4,8},{12,16},{20,24},{8,4},{16,12},{24,20},{5,9},{13,17},{21,25},... | collective-permute-start | bytes 417800 | tf_op jit(solution)/shard_map/ppermute | solution.py:798
  28.7 3.3 %collective-permute-done.4.refs_1_ = f32[2,17,8,128]{3,2,1,0:T(8,128)S(1)} collective-permute-done((f32[2,17,8,128]{3,2,1,0:T(8,128)S(1)}, f32[2,17,8,128]{3,2,1,0:T(8,128)S(1)}, u32[]{:S(2)}, u32[]{:S(2)}) %collective-permute-start.4) | collective-permute-done | bytes 139296 | tf_op jit(solution)/shard_map/ppermute | solution.py:797
  32.0 0.0 collective-permute-done.5.refs_2_
  32.0 0.5 %offsets.1 = (f32[2,12,8,128]{3,2,1,0:T(8,128)S(1)}, f32[2,12,8,128]{3,2,1,0:T(8,128)S(1)}) custom-call(f32[2,17,8,128]{3,2,1,0:T(8,128)S(1)} %extend.1.refs_0_, f32[2,17,8,128]{3,2,1,0:T(8,128)S(1)} %collective-permute-done.4.refs_1_, f32[2,17,8,128]{3,2,1,0:T(8,128)S(1)} %collective-permute-done.5.refs_2_), custom_call_target="tpu_custom_call" | custom-call | tf_op jit(solution)/shard_map/offsets/pallas_call | solution.py:799
  32.5 3.4 %collective-permute-start.6 = (f32[2,12,8,128]{3,2,1,0:T(8,128)S(1)}, f32[2,12,8,128]{3,2,1,0:T(8,128)S(1)}, u32[]{:S(2)}, u32[]{:S(2)}) collective-permute-start(f32[2,12,8,128]{3,2,1,0:T(8,128)S(1)} %get-tuple-element.36), channel_id=1, source_target_pairs={{0,8},{4,12},{8,0},{12,4},{16,24},{20,28},{24,16},{28,20},{1,9},{5... | collective-permute-start | bytes 294920 | tf_op jit(solution)/shard_map/ppermute | solution.py:809
  36.5 1.9 %collective-permute-done.6 = f32[2,12,8,128]{3,2,1,0:T(8,128)S(1)} collective-permute-done((f32[2,12,8,128]{3,2,1,0:T(8,128)S(1)}, f32[2,12,8,128]{3,2,1,0:T(8,128)S(1)}, u32[]{:S(2)}, u32[]{:S(2)}) %collective-permute-start.6) | collective-permute-done | bytes 98336 | tf_op jit(solution)/shard_map/ppermute | solution.py:809
  38.5 4.6 %collective-permute-start.7 = (f32[2,12,8,128]{3,2,1,0:T(8,128)S(1)}, f32[2,12,8,128]{3,2,1,0:T(8,128)S(1)}, u32[]{:S(2)}, u32[]{:S(2)}) collective-permute-start(f32[2,12,8,128]{3,2,1,0:T(8,128)S(1)} %pad_maximum_fusion), channel_id=1, source_target_pairs={{0,24},{4,28},{8,16},{12,20},{16,8},{20,12},{24,0},{28,4},{1,25},{... | collective-permute-start | bytes 294920 | tf_op jit(solution)/shard_map/ppermute | solution.py:809
  43.2 2.6 %collective-permute-done.7 = f32[2,12,8,128]{3,2,1,0:T(8,128)S(1)} collective-permute-done((f32[2,12,8,128]{3,2,1,0:T(8,128)S(1)}, f32[2,12,8,128]{3,2,1,0:T(8,128)S(1)}, u32[]{:S(2)}, u32[]{:S(2)}) %collective-permute-start.7) | collective-permute-done | bytes 98336 | tf_op jit(solution)/shard_map/ppermute | solution.py:809
  45.8 1.1 %result.1 = f32[2,10,96,128]{3,2,1,0:T(8,128)} custom-call(s32[1]{0:T(128)S(6)} %copy.7.refs_0_, f32[2,10,5,8,128]{4,3,2,1,0:T(8,128)S(1)} %get-tuple-element.25.refs_1_, f32[2,10,3,8,128]{4,3,2,1,0:T(8,128)S(1)} %get-tuple-element.26.refs_2_, f32[2,10,4,8,128]{4,3,2,1,0:T(8,128)S(1)} %get-tuple-element.30.refs_3_, ...), custom_call_target="tpu_custom_call" | custom-call | tf_op jit(solution)/shard_map/result/pallas_call | solution.py:813
  (6 shorter events, 0.1 us)
Async XLA Ops:
  2.1 10.6 %collective-permute-start = (f32[10,5,8,128]{3,2,1,0:T(8,128)S(1)}, f32[10,5,8,128]{3,2,1,0:T(8,128)S(1)}, u32[]{:S(2)}, u32[]{:S(2)}) collective-permute-start(f32[10,5,8,128]{3,2,1,0:T(8,128)S(1)} %get-tuple-element.23), channel_id=1, source_target_pairs={{0,1},{1,0},{2,3},{3,2},{4,5},{5,4},{6,7},{7,6},{8,9},{9,8},{10,11... | collective-permute-start | bytes 614408 | tf_op jit(solution)/shard_map/ppermute | solution.py:710
  2.6 10.0 %collective-permute-start.1 = (f32[10,5,8,128]{3,2,1,0:T(8,128)S(1)}, f32[10,5,8,128]{3,2,1,0:T(8,128)S(1)}, u32[]{:S(2)}, u32[]{:S(2)}) collective-permute-start(f32[10,5,8,128]{3,2,1,0:T(8,128)S(1)} %get-tuple-element.24), channel_id=1, source_target_pairs={{0,3},{1,2},{2,1},{3,0},{4,7},{5,6},{6,5},{7,4},{8,11},{9,10},{10,... | collective-permute-start | bytes 614408 | tf_op jit(solution)/shard_map/ppermute | solution.py:709
  20.6 5.2 %collective-permute-start.2 = (f32[5,8,128]{2,1,0:T(8,128)S(1)}, f32[5,8,128]{2,1,0:T(8,128)S(1)}, u32[]{:S(2)}, u32[]{:S(2)}) collective-permute-start(f32[5,8,128]{2,1,0:T(8,128)S(1)} %get-tuple-element.29.refs_4_), channel_id=1, source_target_pairs={{0,1},{1,0},{2,3},{3,2},{4,5},{5,4},{6,7},{7,6},{8,9},{9,8},{10,11... | collective-permute-start | bytes 61448 | tf_op jit(solution)/shard_map/ppermute | solution.py:773
  20.8 5.1 %collective-permute-start.3 = (f32[5,8,128]{2,1,0:T(8,128)S(1)}, f32[5,8,128]{2,1,0:T(8,128)S(1)}, u32[]{:S(2)}, u32[]{:S(2)}) collective-permute-start(f32[5,8,128]{2,1,0:T(8,128)S(1)} %get-tuple-element.34), channel_id=1, source_target_pairs={{0,3},{1,2},{2,1},{3,0},{4,7},{5,6},{6,5},{7,4},{8,11},{9,10},{10,... | collective-permute-start | bytes 61448 | tf_op jit(solution)/shard_map/ppermute | solution.py:772
  25.9 6.1 %collective-permute-start.4 = (f32[2,17,8,128]{3,2,1,0:T(8,128)S(1)}, f32[2,17,8,128]{3,2,1,0:T(8,128)S(1)}, u32[]{:S(2)}, u32[]{:S(2)}) collective-permute-start(f32[2,17,8,128]{3,2,1,0:T(8,128)S(1)} %extend.1.refs_0_), channel_id=1, source_target_pairs={{0,4},{4,0},{8,12},{12,8},{16,20},{20,16},{24,28},{28,24},{1,5},{5... | collective-permute-start | bytes 417800 | tf_op jit(solution)/shard_map/ppermute | solution.py:797
  28.0 3.9 %collective-permute-start.5 = (f32[2,17,8,128]{3,2,1,0:T(8,128)S(1)}, f32[2,17,8,128]{3,2,1,0:T(8,128)S(1)}, u32[]{:S(2)}, u32[]{:S(2)}) collective-permute-start(f32[2,17,8,128]{3,2,1,0:T(8,128)S(1)} %extend.1.refs_0_), channel_id=1, source_target_pairs={{4,8},{12,16},{20,24},{8,4},{16,12},{24,20},{5,9},{13,17},{21,25},... | collective-permute-start | bytes 417800 | tf_op jit(solution)/shard_map/ppermute | solution.py:798
  32.5 6.0 %collective-permute-start.6 = (f32[2,12,8,128]{3,2,1,0:T(8,128)S(1)}, f32[2,12,8,128]{3,2,1,0:T(8,128)S(1)}, u32[]{:S(2)}, u32[]{:S(2)}) collective-permute-start(f32[2,12,8,128]{3,2,1,0:T(8,128)S(1)} %get-tuple-element.36), channel_id=1, source_target_pairs={{0,8},{4,12},{8,0},{12,4},{16,24},{20,28},{24,16},{28,20},{1,9},{5... | collective-permute-start | bytes 294920 | tf_op jit(solution)/shard_map/ppermute | solution.py:809
  38.5 7.2 %collective-permute-start.7 = (f32[2,12,8,128]{3,2,1,0:T(8,128)S(1)}, f32[2,12,8,128]{3,2,1,0:T(8,128)S(1)}, u32[]{:S(2)}, u32[]{:S(2)}) collective-permute-start(f32[2,12,8,128]{3,2,1,0:T(8,128)S(1)} %pad_maximum_fusion), channel_id=1, source_target_pairs={{0,24},{4,28},{8,16},{12,20},{16,8},{20,12},{24,0},{28,4},{1,25},{... | collective-permute-start | bytes 294920 | tf_op jit(solution)/shard_map/ppermute | solution.py:809
